TPU v7x, 512 devices: a whole 4x8x8 slice. The times are simulated.
512 devices in a mesh: fsdp: 64 (over y, z), dp: 8 (over x, core).
Axes of the slice: x: 4, y: 8, z: 8, core: 2. Of those that a mesh axis runs over, the one named last changes fastest.
Arguments:
- grad_parts: bfloat16 [8, 64, 512, 512], P('dp', None, 'fsdp'), may hold values from -2.5 to 2.5
- weights: float32 [64, 512, 512], P(None, 'fsdp', 'dp'), may hold values from -6 to 6
- left_stat: float32 [192, 512, 512], P('fsdp', 'dp'), may hold values from -6 to 6
- right_stat: float32 [192, 512, 512], P('fsdp', 'dp'), may hold values from -6 to 6
- left_codes: bfloat16 [192, 512, 512], P('fsdp'), may hold values from -1 to 1
- right_codes: bfloat16 [192, 512, 512], P('fsdp', 'dp'), may hold values from -1 to 1
- left_scales: float32 [192, 512], P('fsdp'), may hold values from 0.3 to 3
- right_scales: float32 [192, 512], P('fsdp', 'dp'), may hold values from 0.1 to 27
- owners: int32 [64], replicated, may hold values from 0 to 63, as said below
Outputs:
- new_weights: float32 [64, 512, 512], P(None, 'fsdp', 'dp')
- new_left_stat: float32 [192, 512, 512], P('fsdp', 'dp')
- new_right_stat: float32 [192, 512, 512], P('fsdp', 'dp')
Inputs may be any that keep to these rules, and one draw needn't show every extreme that they name: `owners`: each owner is named by at most 3 blocks, and some owner by exactly 3 blocks.
All inputs are finite; a program needn't handle non-finite values.
Results may differ from a plain program's by a relative error of at most 0.0095.
Values may be sent and summed in bfloat16 or wider, within the bound.
No kernel may reach another device: no remote copies, remote signals or barrier semaphores. Data moves between devices by JAX's collectives and lax.ppermute only.
A program may use at most 64 MiB of HBM per device.

v0:
```python
import jax
import jax.numpy as jnp
from jax import lax
from jax.sharding import PartitionSpec as P

stat_decay = 0.95
step_size = 0.5
epsilon = 1e-06


def split_up(x, dim, length):
    before, after = (x.shape[:dim], x.shape[dim + 1 :])
    return jnp.moveaxis(x.reshape(*before, length, -1, *after), dim, 0)


def summed_on_arrival(x, axis, dim):
    length = lax.axis_size(axis)
    blocks = lax.all_to_all(split_up(x, dim, length), axis, 0, 0, tiled=True)
    return jnp.sum(blocks.astype(jnp.float32), axis=0)


def joined_along(blocks, dim):
    dims = list(blocks.shape[1:])
    dims[dim] *= blocks.shape[0]
    return jnp.moveaxis(blocks, 0, dim).reshape(dims)


def from_everyone(x, axis):
    copies = jnp.broadcast_to(x, (lax.axis_size(axis), *x.shape))
    return lax.all_to_all(copies, axis, split_axis=0, concat_axis=0, tiled=True)


def collect(x, axis, dim):
    return joined_along(from_everyone(x, axis), dim)


def of_everyone(x, axis):
    return from_everyone(x, axis).sum(axis=0)


def slot_table(owners, capacity):
    count = owners.shape[0]
    index = jnp.arange(count, dtype=jnp.int32)
    earlier = (owners[:, None] == owners[None, :]) & (index[None, :] < index[:, None])
    rank = jnp.sum(earlier.astype(jnp.int32), axis=1)
    return owners * capacity + rank


def route_rows(summed, picker, owner_count, capacity):
    blocks = summed.shape[0]
    flat = summed.reshape(blocks, -1)
    placed = jnp.einsum("bj,bx->jx", picker, flat, preferred_element_type=jnp.float32).astype(
        jnp.bfloat16
    )
    return placed.reshape(owner_count, capacity, summed.shape[1], summed.shape[2])


def local(
    grad_parts,
    weights,
    left_stat,
    right_stat,
    left_codes,
    right_codes,
    left_scales,
    right_scales,
    owners,
):
    owner_count = lax.axis_size("fsdp")
    replica = lax.axis_index("dp")
    capacity = left_stat.shape[0]
    piece_width = left_stat.shape[1]
    block_width = left_codes.shape[1]
    slot_of = slot_table(owners, capacity)
    slot_ids = jnp.arange(owner_count * capacity, dtype=jnp.int32)
    picker = (slot_of[:, None] == slot_ids[None, :]).astype(jnp.bfloat16)
    partial_value = grad_parts[0].astype(jnp.float32)
    summed = summed_on_arrival(partial_value.astype(jnp.bfloat16), "dp", 2).astype(jnp.bfloat16)
    routed = route_rows(summed, picker, owner_count, capacity)
    arrived = lax.all_to_all(routed, "fsdp", split_axis=0, concat_axis=2, tiled=True)
    column_part = arrived.reshape(capacity, block_width, piece_width)
    whole_grad = collect(column_part, "dp", 2)
    first_row = replica * piece_width
    rows_mine = lax.dynamic_slice_in_dim(whole_grad, first_row, piece_width, 1)
    cols_mine = lax.dynamic_slice_in_dim(whole_grad, first_row, piece_width, 2)
    gram_left = jnp.einsum(
        "srk,sck->src", rows_mine, whole_grad, preferred_element_type=jnp.float32
    )
    gram_right = jnp.einsum(
        "skr,skc->src", cols_mine, whole_grad, preferred_element_type=jnp.float32
    )
    left_new = stat_decay * left_stat + (1.0 - stat_decay) * gram_left
    right_new = stat_decay * right_stat + (1.0 - stat_decay) * gram_right
    left_factor = (left_codes.astype(jnp.float32) * left_scales[:, :, None]).astype(jnp.bfloat16)
    right_factor = (right_codes.astype(jnp.float32) * right_scales[:, :, None]).astype(jnp.bfloat16)
    mixed = jnp.einsum(
        "sik,sck->sic", whole_grad, right_factor, preferred_element_type=jnp.float32
    ).astype(jnp.bfloat16)
    precond = jnp.einsum("sik,skc->sic", left_factor, mixed, preferred_element_type=jnp.float32)
    part_squares = jnp.sum(precond * precond, axis=(1, 2))
    total_squares = of_everyone(part_squares, "dp")
    grad_squares = jnp.sum(jnp.square(whole_grad.astype(jnp.float32)), axis=(1, 2))
    graft_ratio = jnp.sqrt(grad_squares) * lax.rsqrt(total_squares + epsilon)
    update = step_size * graft_ratio[:, None, None] * precond
    returned = lax.all_to_all(update, "fsdp", split_axis=1, concat_axis=0, tiled=True)
    my_update = jnp.take(returned, slot_of, axis=0)
    new_weights = weights - my_update
    return (new_weights, left_new, right_new)


def solution(mesh):
    return jax.shard_map(
        local,
        mesh=mesh,
        in_specs=(
            P("dp", None, "fsdp", None),
            P(None, "fsdp", "dp"),
            P("fsdp", "dp", None),
            P("fsdp", "dp", None),
            P("fsdp", None, None),
            P("fsdp", "dp", None),
            P("fsdp", None),
            P("fsdp", "dp"),
            P(),
        ),
        out_specs=(P(None, "fsdp", "dp"), P("fsdp", "dp", None), P("fsdp", "dp", None)),
        check_vma=False,
    )
```

profile of v0, /device:TPU:16, one launch (start us, length us, event | category | flops | bytes accessed | tf_op | source)
XLA Modules:
  0.0 115.3 jit_solution(17075889950682220723)
XLA Ops:
  0.6 1.6 %reshape.47 = bf16[64,8,8,64]{3,2,1,0:T(8,128)(2,1)S(1)} reshape(bf16[1,64,8,512]{3,2,1,0:T(8,128)(2,1)} %param.9) | data formatting | bytes 1048576 | tf_op jit(solution)/shard_map/reshape | solution.py:13
  2.3 0.1 copy.64
  2.4 0.0 copy-start.3
  2.4 1.5 %reshape.61 = bf16[8,2,16384]{2,1,0:T(2,128)(2,1)} reshape(bf16[8,64,8,64]{3,2,1,0:T(8,128)(2,1)S(1)} %copy.64) | data formatting | bytes 1048576
  4.0 4.3 %all-to-all-start = ((bf16[8,2,16384]{2,1,0:T(2,128)(2,1)}), bf16[8,2,16384]{2,1,0:T(2,128)(2,1)S(1)}, u32[]{:S(2)}, u32[]{:S(2)}) async-start(bf16[8,2,16384]{2,1,0:T(2,128)(2,1)} %reshape.61), calls=%async_computation | async-start | bytes 1048576 | tf_op jit(solution)/shard_map/all_to_all | solution.py:18
  8.3 0.0 copy-done.3
  8.3 0.2 convert_reduce_fusion
  8.5 10.1 %all-to-all-done = bf16[8,2,16384]{2,1,0:T(2,128)(2,1)S(1)} async-done(((bf16[8,2,16384]{2,1,0:T(2,128)(2,1)}), bf16[8,2,16384]{2,1,0:T(2,128)(2,1)S(1)}, u32[]{:S(2)}, u32[]{:S(2)}) %all-to-all-start) | async-done | bytes 524320 | tf_op jit(solution)/shard_map/all_to_all | solution.py:18
  18.6 0.6 reshape.62
  19.2 0.2 reduce_sum.49
  19.5 0.1 reshape.48
  19.6 0.3 convolution_convert_fusion
  19.9 0.2 reshape.49
  20.2 0.2 reshape.63
  20.4 28.5 %all_to_all.49 = bf16[64,2,768]{2,1,0:T(2,128)(2,1)S(1)} all-to-all(bf16[64,2,768]{2,1,0:T(2,128)(2,1)S(1)} %reshape.63), channel_id=1, replica_groups=mesh['fsdp'=64,'dp'=8] {'fsdp'}, dimensions={0} | all-to-all | bytes 393216 | tf_op jit(solution)/shard_map/all_to_all | solution.py:80
  48.9 0.3 reshape.64
  49.2 0.1 copy_bitcast_fusion.1
  49.3 0.2 copy.66
  49.5 0.2 broadcast_in_dim.28
  49.6 24.0 %all_to_all.50 = bf16[8,3,512,64]{2,3,1,0:T(8,128)(2,1)S(1)} all-to-all(bf16[8,3,512,64]{2,3,1,0:T(8,128)(2,1)S(1)} %broadcast_in_dim.28), channel_id=1, replica_groups=mesh['fsdp'=64,'dp'=8] {'dp'}, dimensions={0} | all-to-all | bytes 3145728 | tf_op jit(solution)/shard_map/all_to_all | solution.py:30
  73.7 0.0 copy-start.4
  73.7 0.1 copy.67
  73.8 0.5 copy-done.4
  74.3 2.5 %multiply_reduce_fusion.1 = (f32[3]{0:T(128)S(1)}, f32[3,512,64]{1,2,0:T(8,128)S(1)}) fusion(bf16[3,512,512]{1,2,0:T(8,128)(2,1)S(1)} %bitcast.26, bf16[3,64,512]{2,1,0:T(8,128)(2,1)} %param.14, f32[3,64]{1,0:T(4,128)S(1)} %copy-done.4, bf16[3,512,512]{2,1,0:T(8,128)(2,1)} %param.13, f32[3,512]{1,0:T(4,128)} %param.15), kind=kOutput, calls=%fused_computation.14 | convolution fusion | flops 204275712 | bytes 3742476 | tf_op jit(solution)/shard_map/sik,skc->sic/dot_general | solution.py:99
  76.8 0.6 broadcast_in_dim.29
  77.4 3.3 %all-to-all-start.3 = ((f32[8,1,3]{2,1,0:T(1,128)}), f32[8,1,3]{2,1,0:T(1,128)S(1)}, u32[]{:S(2)}, u32[]{:S(2)}) async-start(f32[8,1,3]{2,1,0:T(1,128)} %broadcast_in_dim.29), calls=%async_computation.3 | async-start | bytes 8192 | tf_op jit(solution)/shard_map/all_to_all | solution.py:30
  80.7 0.5 multiply_reduce_fusion
  81.2 4.6 %all-to-all-done.3 = f32[8,1,3]{2,1,0:T(1,128)S(1)} async-done(((f32[8,1,3]{2,1,0:T(1,128)}), f32[8,1,3]{2,1,0:T(1,128)S(1)}, u32[]{:S(2)}, u32[]{:S(2)}) %all-to-all-start.3) | async-done | bytes 128 | tf_op jit(solution)/shard_map/all_to_all | solution.py:30
  85.9 0.1 broadcast_multiply_fusion
  86.0 0.0 copy-start
  86.0 0.4 copy.70
  86.4 1.5 %reshape.65 = f32[64,1,1536]{2,1,0:T(1,128)} reshape(f32[512,3,64]{2,1,0:T(4,128)S(1)} %bitcast.30) | data formatting | bytes 786432
  87.9 0.0 copy-start.1
  87.9 5.9 %all-to-all-start.4 = ((f32[64,1,1536]{2,1,0:T(1,128)}), f32[64,1,1536]{2,1,0:T(1,128)S(1)}, u32[]{:S(2)}, u32[]{:S(2)}) async-start(f32[64,1,1536]{2,1,0:T(1,128)} %reshape.65), calls=%async_computation.4 | async-start | bytes 786432 | tf_op jit(solution)/shard_map/all_to_all | solution.py:105
  93.8 0.0 copy-done
  93.8 1.3 %fusion.2 = f32[3,64,512]{2,1,0:T(8,128)} fusion(bf16[3,512,512]{1,2,0:T(8,128)(2,1)S(1)} %bitcast.27, s32[]{:T(128)S(6)} %select_n.15, f32[3,64,512]{2,1,0:T(8,128)S(1)} %copy-done), kind=kOutput, calls=%fused_computation.6 | convolution fusion | flops 100958208 | bytes 2752516 | tf_op jit(solution)/shard_map/srk,sck->src/dot_general | solution.py:86
  95.1 0.0 copy-done.1
  95.1 1.3 %fusion.3 = f32[3,64,512]{2,1,0:T(8,128)} fusion(bf16[3,512,512]{1,2,0:T(8,128)(2,1)S(1)} %bitcast.28, f32[3,64,512]{2,1,0:T(8,128)S(1)} %copy-done.1, s32[]{:T(128)S(6)} %select_n.15), kind=kOutput, calls=%fused_computation.8 | convolution fusion | flops 100958208 | bytes 2555908 | tf_op jit(solution)/shard_map/skr,skc->src/dot_general | solution.py:89
  96.5 14.3 %all-to-all-done.4 = f32[64,1,1536]{2,1,0:T(1,128)S(1)} async-done(((f32[64,1,1536]{2,1,0:T(1,128)}), f32[64,1,1536]{2,1,0:T(1,128)S(1)}, u32[]{:S(2)}, u32[]{:S(2)}) %all-to-all-start.4) | async-done | bytes 393248 | tf_op jit(solution)/shard_map/all_to_all | solution.py:105
  110.8 0.5 broadcast.46
  111.3 1.6 %reduce.3 = f32[64,1536]{1,0:T(8,128)S(1)} reduce(f32[64,1,1536]{2,1,0:T(1,128)S(1)} %all-to-all-done.4, f32[]{:T(128)} %broadcast.46), dimensions={1}, to_apply=%all_to_all.40.reduce_sub_computation | reduce | bytes 786436 | tf_op jit(solution)/shard_map/all_to_all | solution.py:105
  112.9 0.6 reshape.66
  113.5 0.0 copy-start.2
  113.5 0.1 copy.84
  113.6 0.1 copy.72
  113.6 0.6 gather_fusion
  114.3 0.2 copy-done.2
  114.5 0.8 select_subtract_fusion
  (5 shorter events, 0.1 us)
Async XLA Ops:
  2.4 5.8 %copy-start.3 = (s32[64]{0:T(128)S(1)}, s32[64]{0:T(128)}, u32[]{:S(2)}) copy-start(s32[64]{0:T(128)} %param.17) | copy-start | bytes 772
  4.0 14.6 %all-to-all-start = ((bf16[8,2,16384]{2,1,0:T(2,128)(2,1)}), bf16[8,2,16384]{2,1,0:T(2,128)(2,1)S(1)}, u32[]{:S(2)}, u32[]{:S(2)}) async-start(bf16[8,2,16384]{2,1,0:T(2,128)(2,1)} %reshape.61), calls=%async_computation | async-start | bytes 1048576 | tf_op jit(solution)/shard_map/all_to_all | solution.py:18
  73.7 0.7 copy-start.4
  77.4 8.5 %all-to-all-start.3 = ((f32[8,1,3]{2,1,0:T(1,128)}), f32[8,1,3]{2,1,0:T(1,128)S(1)}, u32[]{:S(2)}, u32[]{:S(2)}) async-start(f32[8,1,3]{2,1,0:T(1,128)} %broadcast_in_dim.29), calls=%async_computation.3 | async-start | bytes 8192 | tf_op jit(solution)/shard_map/all_to_all | solution.py:30
  86.0 7.8 %copy-start = (f32[3,64,512]{2,1,0:T(8,128)S(1)}, f32[3,64,512]{2,1,0:T(8,128)}, u32[]{:S(2)}) copy-start(f32[3,64,512]{2,1,0:T(8,128)} %param.11) | copy-start | bytes 1179652
  87.9 7.2 %copy-start.1 = (f32[3,64,512]{2,1,0:T(8,128)S(1)}, f32[3,64,512]{2,1,0:T(8,128)}, u32[]{:S(2)}) copy-start(f32[3,64,512]{2,1,0:T(8,128)} %param.12) | copy-start | bytes 1179652
  87.9 22.8 %all-to-all-start.4 = ((f32[64,1,1536]{2,1,0:T(1,128)}), f32[64,1,1536]{2,1,0:T(1,128)S(1)}, u32[]{:S(2)}, u32[]{:S(2)}) async-start(f32[64,1,1536]{2,1,0:T(1,128)} %reshape.65), calls=%async_computation.4 | async-start | bytes 786432 | tf_op jit(solution)/shard_map/all_to_all | solution.py:105
  113.5 1.0 copy-start.2
where the time goes:
time: 116 us; the launch traced here: 115 us
  blocking collectives  52.5 us (45%)
  waiting for transfers between devices  29 us (25%)
  starting transfers between devices  13.5 us (12%)
  local copies, waits for them, and re-layouts  10.5 us (9%)
  matrix products  5.42 us (5%)
  other arithmetic  3.49 us (3%)
    all_to_all x1, blocking collectives, local(): lax.all_to_all(routed, 'fsdp', split_axis=0, concat_axis=2, tiled=True)  28.5 us
    all_to_all x1, blocking collectives, from_everyone(): return lax.all_to_all(copies, axis, split_axis=0, concat_axis=0, tiled=True)  24 us
    all_to_all x1, waiting for transfers between devices, local(): lax.all_to_all(update, 'fsdp', split_axis=1, concat_axis=0, tiled=True)  14.3 us
    all_to_all x1, waiting for transfers between devices, summed_on_arrival(): blocks = lax.all_to_all(split_up(x, dim, length), axis, 0, 0, tiled=True)  10.1 us
    all_to_all x1, starting transfers between devices, local(): lax.all_to_all(update, 'fsdp', split_axis=1, concat_axis=0, tiled=True)  5.85 us
    unnamed x16, local copies, waits for them, and re-layouts  5.57 us
    all_to_all x1, waiting for transfers between devices, from_everyone(): return lax.all_to_all(copies, axis, split_axis=0, concat_axis=0, tiled=True)  4.64 us
    all_to_all x1, starting transfers between devices, summed_on_arrival(): blocks = lax.all_to_all(split_up(x, dim, length), axis, 0, 0, tiled=True)  4.3 us
  transfers between devices with their start and end apart: 3, of which 3 were waited for; matrix products, arithmetic and copies ran while one was open for 3% of the time, Pallas kernels for 0%

commit v1 on v0

v1 whole, which is shorter than its diff:
```python
import jax
import jax.numpy as jnp
from jax import lax
from jax.experimental import pallas as pl
from jax.experimental.pallas import tpu as pltpu
from jax.sharding import Mesh
from jax.sharding import PartitionSpec as P

stat_decay = 0.95
step_size = 0.5
epsilon = 1e-06

bf16 = jnp.bfloat16
f32 = jnp.float32
LANES = 128
VMEM_GRANT = 16 * 1024 * 1024


def iota(shape, dim):
    return lax.broadcasted_iota(jnp.int32, shape, dim)


def dot(a, b, ca=1, cb=0):
    return lax.dot_general(a, b, (((ca,), (cb,)), ((), ())), preferred_element_type=f32)


def onehot(mask):
    return jnp.where(mask, 1.0, 0.0).astype(bf16)


def natural_row(order, first_half):
    half = (order // 256 + first_half) % 2
    return 8 * (order % 64) + 4 * half + (order // 64) % 4


def vmem(n):
    return [pl.BlockSpec(memory_space=pltpu.VMEM)] * n


SMEM = pl.BlockSpec(memory_space=pltpu.SMEM)
ANY = pl.BlockSpec(memory_space=pl.ANY)


def call(kernel, ins, outs, args):
    single = not isinstance(outs, (list, tuple))
    shapes = [outs] if single else list(outs)
    got = pl.pallas_call(
        kernel,
        out_shape=shapes,
        in_specs=ins,
        out_specs=vmem(len(shapes)),
        compiler_params=pltpu.CompilerParams(vmem_limit_bytes=VMEM_GRANT),
    )(*args)
    return got[0] if single else got


def sds(shape, dtype):
    return jax.ShapeDtypeStruct(shape, dtype)


def split_kernel(x_ref, out_ref):
    rows = x_ref.shape[0]
    target = natural_row(iota((rows, rows), 0), 0)
    perm = onehot(target == iota((rows, rows), 1))
    moved = dot(perm, x_ref[...]).astype(bf16)
    for x in range(4):
        for c in range(2):
            out_ref[2 * x + c] = moved[256 * c : 256 * c + 256, LANES * x : LANES * x + LANES]


def route_kernel(parts_ref, slot_ref, out_ref):
    total = parts_ref[0].astype(f32)
    for s in range(1, 8):
        total = total + parts_ref[s].astype(f32)
    total = total.astype(bf16)
    wide = jnp.concatenate([total[64 * r : 64 * r + 64] for r in range(4)], axis=1)
    slot = slot_ref[...]
    for k in range(3):
        pick = onehot(slot == 3 * iota((64, 64), 0) + k)
        out_ref[:, 512 * k : 512 * k + 512] = dot(pick, wide).astype(bf16)


def left_kernel(core_ref, lf_ref, after_ref, out_ref):
    back = onehot(natural_row(iota((512, 512), 0), 0) == iota((512, 512), 1))
    cols = onehot(natural_row(iota((512, 512), 1), core_ref[0]) == iota((512, 512), 0))
    for k in range(3):
        rows = dot(back, lf_ref[k]).astype(bf16)
        out_ref[k] = dot(rows, cols).astype(bf16)


def main_kernel(own_ref, other_ref, rf_ref, left_ref, g_ref, p_ref, sq_ref, gs_ref):
    lane = iota((8, LANES), 1)
    squares = jnp.zeros((8, LANES), f32)
    grad_squares = jnp.zeros((8, LANES), f32)
    for k in range(3):
        for s, src in enumerate((own_ref, other_ref)):
            for r in range(4):
                at = LANES * (4 * k + r)
                for x in range(4):
                    row = 256 * s + 64 * r
                    g_ref[k, row : row + 64, LANES * x : LANES * x + LANES] = src[
                        x, :, at : at + LANES
                    ]
        g = g_ref[k]
        rf = rf_ref[k]
        wide = jnp.concatenate([rf, jnp.zeros((128, 512), bf16), rf], axis=0)
        mixed = dot(g, wide, 1, 1).astype(bf16)
        pre = dot(left_ref[k, :256], mixed[:, :128]) + dot(left_ref[k, 256:], mixed[:, 128:])
        for t in range(4):
            at = 512 * k + LANES * t
            p_ref[:, at : at + LANES] = pre[64 * t : 64 * t + 64]
        squares = jnp.where(lane == k, jnp.sum(pre * pre), squares)
        gf = g.astype(f32)
        grad_squares = jnp.where(lane == k, jnp.sum(gf * gf), grad_squares)
    sq_ref[...] = squares
    gs_ref[...] = grad_squares


def scale_kernel(sq_ref, gs_ref, p_ref, out_ref):
    total = jnp.sum(sq_ref[...], axis=0, keepdims=True)
    ratio = step_size * jnp.sqrt(gs_ref[0:1, :]) * lax.rsqrt(total + epsilon)
    for k in range(3):
        span = slice(512 * k, 512 * k + 512)
        out_ref[:, span] = (p_ref[:, span] * ratio[:, k : k + 1]).astype(bf16)


def right_kernel(replica_ref, g_ref, stat_ref, out_ref):
    pick = onehot(iota((64, 512), 1) == 64 * replica_ref[0] + iota((64, 512), 0))
    for k in range(3):
        g = g_ref[k]
        cols = dot(pick, g, 1, 1).astype(bf16)
        out_ref[k] = stat_decay * stat_ref[k] + (1.0 - stat_decay) * dot(cols, g)


def gram_left_kernel(replica_ref, core_ref, g_ref, stat_ref, after_ref, out_ref):
    core = core_ref[0]
    order = natural_row(iota((512, 512), 1), core)
    back = onehot(order == iota((512, 512), 0))
    mine = onehot(
        natural_row(iota((64, 512), 1), core) == 64 * replica_ref[0] + iota((64, 512), 0)
    )
    for k in range(3):
        g = g_ref[k]
        rows = dot(mine, g).astype(bf16)
        whole = dot(back, g).astype(bf16)
        out_ref[k] = stat_decay * stat_ref[k] + (1.0 - stat_decay) * dot(rows, whole, 1, 1)


def final_kernel(ret_ref, slot_ref, w_ref, out_ref):
    slot = slot_ref[...]
    update = jnp.zeros((64, 512), f32)
    for k in range(3):
        pick = onehot(slot == 3 * iota((64, 64), 1) + k)
        update = update + dot(pick, ret_ref[:, 512 * k : 512 * k + 512])
    for t in range(4):
        for half in range(2):
            row = 4 * half + t
            at = LANES * t + 64 * half
            out_ref[:, row, :] = w_ref[:, row, :] - update[:, at : at + 64]


def slot_table(owners, capacity):
    count = owners.shape[0]
    index = jnp.arange(count, dtype=jnp.int32)
    earlier = (owners[:, None] == owners[None, :]) & (index[None, :] < index[:, None])
    rank = jnp.sum(earlier.astype(jnp.int32), axis=1)
    return owners * capacity + rank


def exchange(x, axis):
    return lax.all_to_all(x, axis, split_axis=0, concat_axis=0, tiled=True)


def local(
    grad_parts,
    weights,
    left_stat,
    right_stat,
    left_codes,
    right_codes,
    left_scales,
    right_scales,
    owners,
):
    core = lax.axis_index("core").astype(jnp.int32)
    replica = (2 * lax.axis_index("x") + core).astype(jnp.int32)[None]
    core = core[None]
    slot_of = slot_table(owners, 3)

    split = call(split_kernel, vmem(1), sds((8, 256, 128), bf16), (grad_parts.reshape(512, 512),))
    parts = exchange(split, ("x", "core"))
    routed = call(
        route_kernel, vmem(2), sds((64, 1536), bf16), (parts, slot_of.reshape(1, 64))
    )
    arrived = exchange(routed.reshape(64, 2, 768), "fsdp")

    left_factor = (left_codes.astype(f32) * left_scales[:, :, None]).astype(bf16)
    right_factor = (right_codes.astype(f32) * right_scales[:, :, None]).astype(bf16)
    left = call(
        left_kernel, [SMEM, *vmem(1), ANY], sds((3, 512, 512), bf16), (core, left_factor, routed)
    )

    own = exchange(jnp.broadcast_to(arrived, (4, 64, 2, 768)).reshape(256, 2, 768), "x")
    other = lax.ppermute(own, "core", [(0, 1), (1, 0)])
    grad, pre, squares, grad_squares = call(
        main_kernel,
        vmem(4),
        [
            sds((3, 512, 512), bf16),
            sds((64, 1536), f32),
            sds((8, 128), f32),
            sds((8, 128), f32),
        ],
        (own.reshape(4, 64, 1536), other.reshape(4, 64, 1536), right_factor, left),
    )
    all_squares = exchange(squares.reshape(8, 1, 128), ("x", "core")).reshape(8, 128)
    right_new = call(
        right_kernel, [SMEM, *vmem(2)], sds((3, 64, 512), f32), (replica, grad, right_stat)
    )
    scaled = call(
        scale_kernel, vmem(3), sds((64, 1536), bf16), (all_squares, grad_squares, pre)
    )
    returned = exchange(scaled.reshape(64, 2, 768), "fsdp").reshape(64, 1536)
    left_new = call(
        gram_left_kernel,
        [SMEM, SMEM, *vmem(2), ANY],
        sds((3, 64, 512), f32),
        (replica, core, grad, left_stat, scaled),
    )
    new_weights = call(
        final_kernel,
        vmem(3),
        sds((64, 8, 64), f32),
        (returned, slot_of.reshape(64, 1), weights),
    )
    return (new_weights, left_new, right_new)


def solution(mesh):
    grid = Mesh(mesh.devices.reshape(64, 4, 2), ("fsdp", "x", "core"))
    dp = ("x", "core")
    return jax.shard_map(
        local,
        mesh=grid,
        in_specs=(
            P(dp, None, "fsdp", None),
            P(None, "fsdp", dp),
            P("fsdp", dp, None),
            P("fsdp", dp, None),
            P("fsdp", None, None),
            P("fsdp", dp, None),
            P("fsdp", None),
            P("fsdp", dp),
            P(),
        ),
        out_specs=(P(None, "fsdp", dp), P("fsdp", dp, None), P("fsdp", dp, None)),
        check_vma=False,
    )
```

time: 116 us -> 103 us (0.89)
  the two profiles are of different devices: /device:TPU:16 before, /device:TPU:2 now
where the time goes in v1:
time: 103 us; the launch traced here: 102 us
  blocking collectives  46.2 us (45%)
  waiting for transfers between devices  17.9 us (17%)
  starting transfers between devices  16.5 us (16%)
  Pallas kernels  11.1 us (11%)
  local copies, waits for them, and re-layouts  9.21 us (9%)
    all_to_all x3, blocking collectives, exchange(): return lax.all_to_all(x, axis, split_axis=0, concat_axis=0, tiled=True)  46.2 us
    all_to_all x2, waiting for transfers between devices, exchange(): return lax.all_to_all(x, axis, split_axis=0, concat_axis=0, tiled=True)  17.9 us
    all_to_all x2, starting transfers between devices, exchange(): return lax.all_to_all(x, axis, split_axis=0, concat_axis=0, tiled=True)  14.6 us
    pallas_call x8, Pallas kernels, call(): pl.pallas_call(kernel, out_shape=shapes, in_specs=ins, out_specs=vmem(len...  11.1 us
    unnamed x23, local copies, waits for them, and re-layouts  3.37 us
    reshape x1, local copies, waits for them, and re-layouts, local(): other.reshape(4, 64, 1536)  3.14 us
  transfers between devices with their start and end apart: 3, of which 2 were waited for; matrix products, arithmetic and copies ran while one was open for 2% of the time, Pallas kernels for 6%

profile of v1, /device:TPU:2, one launch (start us, length us, event | category | flops | bytes accessed | tf_op | source)
XLA Modules:
  0.0 102.4 jit_solution(16877651874941072009)
XLA Ops:
  0.6 0.0 copy-start.10
  0.6 0.0 copy-start.2
  0.6 1.0 %copy-done.2 = bf16[1,64,8,512]{3,2,1,0:T(8,128)(2,1)S(1)} copy-done((bf16[1,64,8,512]{3,2,1,0:T(8,128)(2,1)S(1)}, bf16[1,64,8,512]{3,2,1,0:T(8,128)(2,1)}, u32[]{:S(2)}) %copy-start.2) | copy-done | bytes 524312
  1.7 1.2 %shard_map.112 = bf16[8,256,128]{2,1,0:T(8,128)(2,1)} custom-call(bf16[512,512]{1,0:T(8,128)(2,1)S(1)} %bitcast.15), custom_call_target="tpu_custom_call" | custom-call | tf_op jit(solution)/shard_map/pallas_call | solution.py:47
  2.9 9.3 %all-to-all-start = ((bf16[8,256,128]{2,1,0:T(8,128)(2,1)}), bf16[8,256,128]{2,1,0:T(8,128)(2,1)S(1)}, u32[]{:S(2)}, u32[]{:S(2)}) async-start(bf16[8,256,128]{2,1,0:T(8,128)(2,1)} %shard_map.112), calls=%async_computation | async-start | bytes 1048576 | tf_op jit(solution)/shard_map/all_to_all | solution.py:171
  12.2 0.0 copy-done.10
  12.2 0.2 convert_reduce_fusion
  12.4 8.7 %all-to-all-done.parts_ref = bf16[8,256,128]{2,1,0:T(8,128)(2,1)S(1)} async-done(((bf16[8,256,128]{2,1,0:T(8,128)(2,1)}), bf16[8,256,128]{2,1,0:T(8,128)(2,1)S(1)}, u32[]{:S(2)}, u32[]{:S(2)}) %all-to-all-start) | async-done | bytes 524320 | tf_op jit(solution)/shard_map/all_to_all | solution.py:171
  21.1 0.2 shard_map.113.after_ref
  21.4 0.1 reshape.45
  21.4 0.0 copy-start.7
  21.4 0.0 copy-start.9
  21.4 25.4 %all_to_all.25 = bf16[64,2,768]{2,1,0:T(2,128)(2,1)S(1)} all-to-all(bf16[64,2,768]{2,1,0:T(2,128)(2,1)S(1)} %reshape.45), channel_id=1, replica_groups=mesh['fsdp'=64,'x'=4,'core'=2] {'fsdp'}, dimensions={0} | all-to-all | bytes 393216 | tf_op jit(solution)/shard_map/all_to_all | solution.py:171
  46.8 0.0 copy-start.6
  46.8 0.0 copy-start.8
  46.8 0.4 broadcast_in_dim.6
  47.3 13.0 %all_to_all.26 = bf16[256,2,768]{2,1,0:T(2,128)(2,1)S(1)} all-to-all(bf16[256,2,768]{2,1,0:T(2,128)(2,1)S(1)} %bitcast.18), channel_id=1, replica_groups=mesh['fsdp'=64,'x'=4,'core'=2] {'x'}, dimensions={0} | all-to-all | bytes 1572864 | tf_op jit(solution)/shard_map/all_to_all | solution.py:171
  60.3 1.9 %collective-permute-start = (bf16[256,2,768]{2,1,0:T(2,128)(2,1)S(1)}, bf16[256,2,768]{2,1,0:T(2,128)(2,1)}, u32[]{:S(2)}, u32[]{:S(2)}) collective-permute-start(bf16[256,2,768]{2,1,0:T(2,128)(2,1)S(1)} %all_to_all.26), channel_id=1, source_target_pairs={{0,1},{1,0},{2,3},{3,2},{4,5},{5,4},{6,7},{7,6},{8,9},{9,8},{10,11... | collective-permute-start | bytes 2359304 | tf_op jit(solution)/shard_map/ppermute | solution.py:204
  62.2 0.0 copy-done.7
  62.2 0.0 copy-done.9
  62.2 0.1 multiply_convert_fusion.1.rf_ref
  62.3 0.0 copy-done.6
  62.4 0.0 copy-done.8
  62.4 0.4 multiply_convert_fusion.lf_ref
  62.7 1.8 %shard_map.114.left_ref = bf16[3,512,512]{2,1,0:T(8,128)(2,1)S(1)} custom-call(s32[1]{0:T(128)} %bitcast.3.core_ref, bf16[3,512,512]{2,1,0:T(8,128)(2,1)S(1)} %multiply_convert_fusion.lf_ref, bf16[64,1536]{1,0:T(8,128)(2,1)S(1)} %shard_map.113.after_ref), custom_call_target="tpu_custom_call" | custom-call | tf_op jit(solution)/shard_map/pallas_call | solution.py:47
  64.6 1.4 %reshape.47.own_ref = bf16[4,64,1536]{2,1,0:T(8,128)(2,1)} reshape(bf16[256,2,768]{2,1,0:T(2,128)(2,1)S(1)} %all_to_all.26) | data formatting | bytes 1572864 | tf_op jit(solution)/shard_map/reshape | solution.py:214
  66.0 0.0 collective-permute-done
  66.0 3.1 %reshape.48.other_ref = bf16[4,64,1536]{2,1,0:T(8,128)(2,1)} reshape(bf16[256,2,768]{2,1,0:T(2,128)(2,1)} %collective-permute-done) | data formatting | bytes 1572864 | tf_op jit(solution)/shard_map/reshape | solution.py:214
  69.2 0.0 copy-start
  69.2 1.1 %copy-done = bf16[4,64,1536]{2,1,0:T(8,128)(2,1)S(1)} copy-done((bf16[4,64,1536]{2,1,0:T(8,128)(2,1)S(1)}, bf16[4,64,1536]{2,1,0:T(8,128)(2,1)}, u32[]{:S(2)}) %copy-start) | copy-done | bytes 786456
  70.3 0.0 copy-start.1
  70.3 1.1 %copy-done.1 = bf16[4,64,1536]{2,1,0:T(8,128)(2,1)S(1)} copy-done((bf16[4,64,1536]{2,1,0:T(8,128)(2,1)S(1)}, bf16[4,64,1536]{2,1,0:T(8,128)(2,1)}, u32[]{:S(2)}) %copy-start.1) | copy-done | bytes 786456
  71.4 1.8 %shard_map.115 = (bf16[3,512,512]{2,1,0:T(8,128)(2,1)S(1)}, f32[64,1536]{1,0:T(8,128)S(1)}, f32[8,128]{1,0:T(8,128)S(1)}, f32[8,128]{1,0:T(8,128)S(1)}) custom-call(bf16[4,64,1536]{2,1,0:T(8,128)(2,1)S(1)} %copy-done, bf16[4,64,1536]{2,1,0:T(8,128)(2,1)S(1)} %copy-done.1, bf16[3,64,512]{2,1,0:T(8,128)(2,1)S(1)} %multiply_convert_fusion.1.rf_ref, ...), custom_call_target="tpu_custom_call" | custom-call | tf_op jit(solution)/shard_map/pallas_call | solution.py:47
  73.2 0.0 copy-start.3
  73.2 7.8 %all_to_all.27 = f32[8,1,128]{2,1,0:T(1,128)S(1)} all-to-all(f32[8,1,128]{2,1,0:T(1,128)S(1)} %bitcast.17), channel_id=1, replica_groups=mesh['fsdp'=64,'x'=4,'core'=2] {'x','core'}, dimensions={0} | all-to-all | bytes 8192 | tf_op jit(solution)/shard_map/all_to_all | solution.py:171
  81.0 0.1 shard_map.116.after_ref
  81.2 0.0 copy-start.4
  81.2 0.7 reshape.51
  81.9 5.3 %all-to-all-start.4 = ((bf16[64,2,768]{2,1,0:T(2,128)(2,1)}), bf16[64,2,768]{2,1,0:T(2,128)(2,1)S(1)}, u32[]{:S(2)}, u32[]{:S(2)}) async-start(bf16[64,2,768]{2,1,0:T(2,128)(2,1)} %reshape.51), calls=%async_computation.4 | async-start | bytes 393216 | tf_op jit(solution)/shard_map/all_to_all | solution.py:171
  87.2 0.1 copy.16.slot_ref
  87.3 0.0 copy-done.3
  87.3 1.8 %shard_map.119 = f32[3,64,512]{2,1,0:T(8,128)} custom-call(s32[1]{0:T(128)} %bitcast.8.replica_ref, bf16[3,512,512]{2,1,0:T(8,128)(2,1)S(1)} %get-tuple-element.10.g_ref, f32[3,64,512]{2,1,0:T(8,128)S(1)} %copy-done.3), custom_call_target="tpu_custom_call" | custom-call | tf_op jit(solution)/shard_map/pallas_call | solution.py:47
  89.1 0.0 copy-done.4
  89.1 0.0 copy-start.5
  89.1 2.6 %shard_map.118 = f32[3,64,512]{2,1,0:T(8,128)} custom-call(s32[1]{0:T(128)} %bitcast.8.replica_ref, s32[1]{0:T(128)} %bitcast.3.core_ref, bf16[3,512,512]{2,1,0:T(8,128)(2,1)S(1)} %get-tuple-element.10.g_ref, f32[3,64,512]{2,1,0:T(8,128)S(1)} %copy-done.4, bf16[64,1536]{1,0:T(8,128)(2,1)S(1)} %shard_map.116.after_ref), custom_call_target="tpu_custom_call" | custom-call | tf_op jit(solution)/shard_map/pallas_call | solution.py:47
  91.7 9.2 %all-to-all-done.4 = bf16[64,2,768]{2,1,0:T(2,128)(2,1)S(1)} async-done(((bf16[64,2,768]{2,1,0:T(2,128)(2,1)}), bf16[64,2,768]{2,1,0:T(2,128)(2,1)S(1)}, u32[]{:S(2)}, u32[]{:S(2)}) %all-to-all-start.4) | async-done | bytes 196640 | tf_op jit(solution)/shard_map/all_to_all | solution.py:171
  100.9 0.0 copy-done.5
  101.0 1.4 %shard_map.117 = f32[64,8,64]{2,1,0:T(8,128)} custom-call(bf16[64,1536]{1,0:T(8,128)(2,1)S(1)} %bitcast.14, s32[64,1]{1,0:T(8,128)S(1)} %copy.16.slot_ref, f32[64,8,64]{2,1,0:T(8,128)S(1)} %copy-done.5), custom_call_target="tpu_custom_call" | custom-call | tf_op jit(solution)/shard_map/pallas_call | solution.py:47
  (2 shorter events, 0.0 us)
Async XLA Ops:
  0.6 11.6 %copy-start.10 = (s32[64]{0:T(128)S(1)}, s32[64]{0:T(128)}, u32[]{:S(2)}) copy-start(s32[64]{0:T(128)} %param.17) | copy-start | bytes 772
  0.6 1.0 %copy-start.2 = (bf16[1,64,8,512]{3,2,1,0:T(8,128)(2,1)S(1)}, bf16[1,64,8,512]{3,2,1,0:T(8,128)(2,1)}, u32[]{:S(2)}) copy-start(bf16[1,64,8,512]{3,2,1,0:T(8,128)(2,1)} %param.9) | copy-start | bytes 1572868
  2.9 18.2 %all-to-all-start = ((bf16[8,256,128]{2,1,0:T(8,128)(2,1)}), bf16[8,256,128]{2,1,0:T(8,128)(2,1)S(1)}, u32[]{:S(2)}, u32[]{:S(2)}) async-start(bf16[8,256,128]{2,1,0:T(8,128)(2,1)} %shard_map.112), calls=%async_computation | async-start | bytes 1048576 | tf_op jit(solution)/shard_map/all_to_all | solution.py:171
  21.4 40.8 %copy-start.7 = (bf16[3,64,512]{2,1,0:T(8,128)(2,1)S(1)}, bf16[3,64,512]{2,1,0:T(8,128)(2,1)}, u32[]{:S(2)}) copy-start(bf16[3,64,512]{2,1,0:T(8,128)(2,1)} %param.14) | copy-start | bytes 589828
  21.4 40.8 %copy-start.9 = (f32[3,64]{1,0:T(4,128)S(1)}, f32[3,64]{1,0:T(4,128)}, u32[]{:S(2)}) copy-start(f32[3,64]{1,0:T(4,128)} %param.16) | copy-start | bytes 2308
  46.8 15.5 %copy-start.6 = (bf16[3,512,512]{2,1,0:T(8,128)(2,1)S(1)}, bf16[3,512,512]{2,1,0:T(8,128)(2,1)}, u32[]{:S(2)}) copy-start(bf16[3,512,512]{2,1,0:T(8,128)(2,1)} %param.13) | copy-start | bytes 4718596
  46.8 15.5 %copy-start.8 = (f32[3,512]{1,0:T(4,128)S(1)}, f32[3,512]{1,0:T(4,128)}, u32[]{:S(2)}) copy-start(f32[3,512]{1,0:T(4,128)} %param.15) | copy-start | bytes 18436
  60.3 5.7 %collective-permute-start = (bf16[256,2,768]{2,1,0:T(2,128)(2,1)S(1)}, bf16[256,2,768]{2,1,0:T(2,128)(2,1)}, u32[]{:S(2)}, u32[]{:S(2)}) collective-permute-start(bf16[256,2,768]{2,1,0:T(2,128)(2,1)S(1)} %all_to_all.26), channel_id=1, source_target_pairs={{0,1},{1,0},{2,3},{3,2},{4,5},{5,4},{6,7},{7,6},{8,9},{9,8},{10,11... | collective-permute-start | bytes 2359304 | tf_op jit(solution)/shard_map/ppermute | solution.py:204
  69.2 1.1 %copy-start = (bf16[4,64,1536]{2,1,0:T(8,128)(2,1)S(1)}, bf16[4,64,1536]{2,1,0:T(8,128)(2,1)}, u32[]{:S(2)}) copy-start(bf16[4,64,1536]{2,1,0:T(8,128)(2,1)} %reshape.47.own_ref) | copy-start | bytes 2359300
  70.3 1.1 %copy-start.1 = (bf16[4,64,1536]{2,1,0:T(8,128)(2,1)S(1)}, bf16[4,64,1536]{2,1,0:T(8,128)(2,1)}, u32[]{:S(2)}) copy-start(bf16[4,64,1536]{2,1,0:T(8,128)(2,1)} %reshape.48.other_ref) | copy-start | bytes 2359300
  73.2 14.1 %copy-start.3 = (f32[3,64,512]{2,1,0:T(8,128)S(1)}, f32[3,64,512]{2,1,0:T(8,128)}, u32[]{:S(2)}) copy-start(f32[3,64,512]{2,1,0:T(8,128)} %stat_ref.3) | copy-start | bytes 1179652
  81.2 8.0 %copy-start.4 = (f32[3,64,512]{2,1,0:T(8,128)S(1)}, f32[3,64,512]{2,1,0:T(8,128)}, u32[]{:S(2)}) copy-start(f32[3,64,512]{2,1,0:T(8,128)} %stat_ref.2) | copy-start | bytes 1179652
  81.9 19.0 %all-to-all-start.4 = ((bf16[64,2,768]{2,1,0:T(2,128)(2,1)}), bf16[64,2,768]{2,1,0:T(2,128)(2,1)S(1)}, u32[]{:S(2)}, u32[]{:S(2)}) async-start(bf16[64,2,768]{2,1,0:T(2,128)(2,1)} %reshape.51), calls=%async_computation.4 | async-start | bytes 393216 | tf_op jit(solution)/shard_map/all_to_all | solution.py:171
  89.1 11.8 %copy-start.5 = (f32[64,8,64]{2,1,0:T(8,128)S(1)}, f32[64,8,64]{2,1,0:T(8,128)}, u32[]{:S(2)}) copy-start(f32[64,8,64]{2,1,0:T(8,128)} %w_ref.1) | copy-start | bytes 393220

commit v2 on v1

--- a/solution.py
+++ b/solution.py
@@ -58,14 +58,55 @@
     return jax.ShapeDtypeStruct(shape, dtype)
 
 
-def split_kernel(x_ref, out_ref):
-    rows = x_ref.shape[0]
-    target = natural_row(iota((rows, rows), 0), 0)
-    perm = onehot(target == iota((rows, rows), 1))
-    moved = dot(perm, x_ref[...]).astype(bf16)
-    for x in range(4):
-        for c in range(2):
-            out_ref[2 * x + c] = moved[256 * c : 256 * c + 256, LANES * x : LANES * x + LANES]
+CHUNKS = 4
+
+
+def split_kernel(x_ref, out_ref, x_buf, out_buf, in_sem, out_sem):
+    rows = x_buf.shape[1]
+    per = rows // 8
+
+    def arrival(i):
+        return pltpu.make_async_copy(x_ref.at[pl.ds(rows * i, rows)], x_buf.at[i], in_sem.at[i])
+
+    def leaving(i):
+        target = out_ref.at[:, :, pl.ds(per * i, per)]
+        return pltpu.make_async_copy(out_buf.at[i], target, out_sem.at[i])
+
+    for i in range(CHUNKS):
+        arrival(i).start()
+    order = iota((rows, rows), 0)
+    half, r, block = order // (4 * per), (order // per) % 4, order % per
+    perm = onehot(8 * block + 4 * half + r == iota((rows, rows), 1))
+    for i in range(CHUNKS):
+        arrival(i).wait()
+        moved = dot(perm, x_buf[i]).astype(bf16)
+        for x in range(4):
+            for c in range(2):
+                for r in range(4):
+                    at = (4 * c + r) * per
+                    piece = moved[at : at + per, LANES * x : LANES * x + LANES]
+                    out_buf[i, 2 * x + c, r] = piece
+        leaving(i).start()
+    for i in range(CHUNKS):
+        leaving(i).wait()
+
+
+def split(x):
+    rows = 512 // CHUNKS
+    hbm = pl.BlockSpec(memory_space=pltpu.HBM)
+    return pl.pallas_call(
+        split_kernel,
+        out_shape=sds((8, 4, 64, 128), bf16),
+        in_specs=[hbm],
+        out_specs=hbm,
+        scratch_shapes=[
+            pltpu.VMEM((CHUNKS, rows, 512), bf16),
+            pltpu.VMEM((CHUNKS, 8, 4, rows // 8, 128), bf16),
+            pltpu.SemaphoreType.DMA((CHUNKS,)),
+            pltpu.SemaphoreType.DMA((CHUNKS,)),
+        ],
+        compiler_params=pltpu.CompilerParams(vmem_limit_bytes=VMEM_GRANT),
+    )(x).reshape(8, 256, 128)
 
 
 def route_kernel(parts_ref, slot_ref, out_ref):
@@ -187,12 +228,11 @@
     core = core[None]
     slot_of = slot_table(owners, 3)
 
-    split = call(split_kernel, vmem(1), sds((8, 256, 128), bf16), (grad_parts.reshape(512, 512),))
-    parts = exchange(split, ("x", "core"))
+    parts = exchange(split(grad_parts.reshape(512, 512)), ("x", "core"))
     routed = call(
         route_kernel, vmem(2), sds((64, 1536), bf16), (parts, slot_of.reshape(1, 64))
     )
-    arrived = exchange(routed.reshape(64, 2, 768), "fsdp")
+    arrived = exchange(routed.reshape(64, 2, 768), "fsdp").reshape(64, 1536)
 
     left_factor = (left_codes.astype(f32) * left_scales[:, :, None]).astype(bf16)
     right_factor = (right_codes.astype(f32) * right_scales[:, :, None]).astype(bf16)
@@ -200,7 +240,7 @@
         left_kernel, [SMEM, *vmem(1), ANY], sds((3, 512, 512), bf16), (core, left_factor, routed)
     )
 
-    own = exchange(jnp.broadcast_to(arrived, (4, 64, 2, 768)).reshape(256, 2, 768), "x")
+    own = exchange(jnp.broadcast_to(arrived, (4, 64, 1536)), "x")
     other = lax.ppermute(own, "core", [(0, 1), (1, 0)])
     grad, pre, squares, grad_squares = call(
         main_kernel,
@@ -211,7 +251,7 @@
             sds((8, 128), f32),
             sds((8, 128), f32),
         ],
-        (own.reshape(4, 64, 1536), other.reshape(4, 64, 1536), right_factor, left),
+        (own, other, right_factor, left),
     )
     all_squares = exchange(squares.reshape(8, 1, 128), ("x", "core")).reshape(8, 128)
     right_new = call(

time: 103 us -> 97.7 us (0.949)
  local copies, waits for them, and re-layouts: 9.21 us -> 2.05 us
  other arithmetic: 0.65 us -> 2.07 us
    reshape x3 -> x1, local copies, waits for them, and re-layouts: 4.61 us -> 0.05 us  [local(): arrived = exchange(routed.reshape(64, 2, 768), 'fsdp').reshape(64, 1536)]
    unnamed x23 -> x18, local copies, waits for them, and re-layouts: 3.37 us -> 1.12 us
    pallas_call x0 -> x1, Pallas kernels: none -> 2.09 us  [split(): pl.pallas_call(split_kernel, out_shape=sds((8, 4, 64, 128), bf16), in_spe...]
    convert_element_type x1, other arithmetic: 0.38 us -> 1.8 us  [local(): (left_codes.astype(f32) * left_scales[:, :, None]).astype(bf16)]
    pallas_call x8 -> x7, Pallas kernels: 11.1 us -> 9.86 us  [call(): pl.pallas_call(kernel, out_shape=shapes, in_specs=ins, out_specs=vmem(len...]
where the time goes in v2:
time: 97.7 us; the launch traced here: 97.3 us
  blocking collectives  46 us (47%)
  waiting for transfers between devices  17.9 us (18%)
  starting transfers between devices  16.5 us (17%)
  Pallas kernels  12 us (12%)
  other arithmetic  2.07 us (2%)
  local copies, waits for them, and re-layouts  2.05 us (2%)
    all_to_all x3, blocking collectives, exchange(): return lax.all_to_all(x, axis, split_axis=0, concat_axis=0, tiled=True)  46 us
    all_to_all x2, waiting for transfers between devices, exchange(): return lax.all_to_all(x, axis, split_axis=0, concat_axis=0, tiled=True)  17.9 us
    all_to_all x2, starting transfers between devices, exchange(): return lax.all_to_all(x, axis, split_axis=0, concat_axis=0, tiled=True)  14.6 us
    pallas_call x7, Pallas kernels, call(): pl.pallas_call(kernel, out_shape=shapes, in_specs=ins, out_specs=vmem(len...  9.86 us
    pallas_call x1, Pallas kernels, split(): pl.pallas_call(split_kernel, out_shape=sds((8, 4, 64, 128), bf16), in_spe...  2.09 us
  transfers between devices with their start and end apart: 3, of which 2 were waited for; matrix products, arithmetic and copies ran while one was open for 2% of the time, Pallas kernels for 6%

profile of v2, /device:TPU:2, one launch (start us, length us, event | category | flops | bytes accessed | tf_op | source)
XLA Modules:
  0.0 97.3 jit_solution(11234390098308607835)
XLA Ops:
  0.6 0.0 copy-start.7
  0.6 0.0 copy-start
  0.6 1.0 %copy-done = bf16[1,64,8,512]{3,2,1,0:T(8,128)(2,1)S(1)} copy-done((bf16[1,64,8,512]{3,2,1,0:T(8,128)(2,1)S(1)}, bf16[1,64,8,512]{3,2,1,0:T(8,128)(2,1)}, u32[]{:S(2)}) %copy-start) | copy-done | bytes 524312
  1.7 2.1 %shard_map.112 = bf16[8,4,64,128]{3,2,1,0:T(8,128)(2,1)} custom-call(bf16[512,512]{1,0:T(8,128)(2,1)S(1)} %bitcast.17), custom_call_target="tpu_custom_call" | custom-call | tf_op jit(solution)/shard_map/pallas_call | solution.py:97
  3.8 9.3 %all-to-all-start = ((bf16[8,256,128]{2,1,0:T(8,128)(2,1)}), bf16[8,256,128]{2,1,0:T(8,128)(2,1)S(1)}, u32[]{:S(2)}, u32[]{:S(2)}) async-start(bf16[8,256,128]{2,1,0:T(8,128)(2,1)} %bitcast.1), calls=%async_computation | async-start | bytes 1048576 | tf_op jit(solution)/shard_map/all_to_all | solution.py:212
  13.1 0.0 copy-done.7
  13.1 0.2 convert_reduce_fusion
  13.3 8.7 %all-to-all-done.parts_ref = bf16[8,256,128]{2,1,0:T(8,128)(2,1)S(1)} async-done(((bf16[8,256,128]{2,1,0:T(8,128)(2,1)}), bf16[8,256,128]{2,1,0:T(8,128)(2,1)S(1)}, u32[]{:S(2)}, u32[]{:S(2)}) %all-to-all-start) | async-done | bytes 524320 | tf_op jit(solution)/shard_map/all_to_all | solution.py:212
  22.0 0.2 shard_map.113.after_ref
  22.2 0.1 reshape.43
  22.3 25.3 %all_to_all.25 = bf16[64,2,768]{2,1,0:T(2,128)(2,1)S(1)} all-to-all(bf16[64,2,768]{2,1,0:T(2,128)(2,1)S(1)} %reshape.43), channel_id=1, replica_groups=mesh['fsdp'=64,'x'=4,'core'=2] {'fsdp'}, dimensions={0} | all-to-all | bytes 393216 | tf_op jit(solution)/shard_map/all_to_all | solution.py:212
  47.5 0.0 copy-start.4
  47.5 0.0 copy-start.6
  47.6 0.0 copy-start.5
  47.6 0.1 broadcast_in_dim.6
  47.7 13.0 %all_to_all.26.own_ref = bf16[4,64,1536]{2,1,0:T(8,128)(2,1)S(1)} all-to-all(bf16[4,64,1536]{2,1,0:T(8,128)(2,1)S(1)} %broadcast_in_dim.6), channel_id=1, replica_groups=mesh['fsdp'=64,'x'=4,'core'=2] {'x'}, dimensions={0} | all-to-all | bytes 1572864 | tf_op jit(solution)/shard_map/all_to_all | solution.py:212
  60.7 1.9 %collective-permute-start = (bf16[4,64,1536]{2,1,0:T(8,128)(2,1)S(1)}, bf16[4,64,1536]{2,1,0:T(8,128)(2,1)S(1)}, u32[]{:S(2)}, u32[]{:S(2)}) collective-permute-start(bf16[4,64,1536]{2,1,0:T(8,128)(2,1)S(1)} %all_to_all.26.own_ref), channel_id=1, source_target_pairs={{0,1},{1,0},{2,3},{3,2},{4,5},{5,4},{6,7},{7,6},{8,9},{9,8},{10,11... | collective-permute-start | bytes 2359304 | tf_op jit(solution)/shard_map/ppermute | solution.py:244
  62.6 0.0 copy-done.4
  62.6 0.0 copy-done.6
  62.6 0.1 multiply_convert_fusion.1.rf_ref
  62.7 0.0 copy-done.5
  62.7 1.8 %multiply_convert_fusion.lf_ref = bf16[3,512,512]{2,1,0:T(8,128)(2,1)S(1)} fusion(bf16[3,512,512]{2,1,0:T(8,128)(2,1)} %param.13, f32[3,512]{1,0:T(4,128)S(1)} %copy-done.5), kind=kLoop, calls=%fused_computation | loop fusion | flops 2359296 | bytes 3151872 | tf_op jit(solution)/shard_map/convert_element_type | solution.py:237
  64.6 1.8 %shard_map.114.left_ref = bf16[3,512,512]{2,1,0:T(8,128)(2,1)S(1)} custom-call(s32[1]{0:T(128)} %bitcast.3.core_ref, bf16[3,512,512]{2,1,0:T(8,128)(2,1)S(1)} %multiply_convert_fusion.lf_ref, bf16[64,1536]{1,0:T(8,128)(2,1)S(1)} %shard_map.113.after_ref), custom_call_target="tpu_custom_call" | custom-call | tf_op jit(solution)/shard_map/pallas_call | solution.py:47
  66.4 0.0 copy-start.1
  66.4 0.0 collective-permute-done.other_ref
  66.4 1.8 %shard_map.115 = (bf16[3,512,512]{2,1,0:T(8,128)(2,1)S(1)}, f32[64,1536]{1,0:T(8,128)S(1)}, f32[8,128]{1,0:T(8,128)S(1)}, f32[8,128]{1,0:T(8,128)S(1)}) custom-call(bf16[4,64,1536]{2,1,0:T(8,128)(2,1)S(1)} %all_to_all.26.own_ref, bf16[4,64,1536]{2,1,0:T(8,128)(2,1)S(1)} %collective-permute-done.other_ref, ...), custom_call_target="tpu_custom_call" | custom-call | tf_op jit(solution)/shard_map/pallas_call | solution.py:47
  68.2 7.7 %all_to_all.27 = f32[8,1,128]{2,1,0:T(1,128)S(1)} all-to-all(f32[8,1,128]{2,1,0:T(1,128)S(1)} %bitcast.19), channel_id=1, replica_groups=mesh['fsdp'=64,'x'=4,'core'=2] {'x','core'}, dimensions={0} | all-to-all | bytes 8192 | tf_op jit(solution)/shard_map/all_to_all | solution.py:212
  75.9 0.1 shard_map.116.after_ref
  76.0 0.0 copy-start.2
  76.1 0.7 reshape.47
  76.8 5.3 %all-to-all-start.4 = ((bf16[64,2,768]{2,1,0:T(2,128)(2,1)}), bf16[64,2,768]{2,1,0:T(2,128)(2,1)S(1)}, u32[]{:S(2)}, u32[]{:S(2)}) async-start(bf16[64,2,768]{2,1,0:T(2,128)(2,1)} %reshape.47), calls=%async_computation.4 | async-start | bytes 393216 | tf_op jit(solution)/shard_map/all_to_all | solution.py:212
  82.1 0.1 copy.16.slot_ref
  82.2 0.0 copy-done.1
  82.2 1.8 %shard_map.119 = f32[3,64,512]{2,1,0:T(8,128)} custom-call(s32[1]{0:T(128)} %bitcast.8.replica_ref, bf16[3,512,512]{2,1,0:T(8,128)(2,1)S(1)} %get-tuple-element.10.g_ref, f32[3,64,512]{2,1,0:T(8,128)S(1)} %copy-done.1), custom_call_target="tpu_custom_call" | custom-call | tf_op jit(solution)/shard_map/pallas_call | solution.py:47
  84.0 0.0 copy-done.2
  84.0 0.0 copy-start.3
  84.0 2.6 %shard_map.118 = f32[3,64,512]{2,1,0:T(8,128)} custom-call(s32[1]{0:T(128)} %bitcast.8.replica_ref, s32[1]{0:T(128)} %bitcast.3.core_ref, bf16[3,512,512]{2,1,0:T(8,128)(2,1)S(1)} %get-tuple-element.10.g_ref, f32[3,64,512]{2,1,0:T(8,128)S(1)} %copy-done.2, bf16[64,1536]{1,0:T(8,128)(2,1)S(1)} %shard_map.116.after_ref), custom_call_target="tpu_custom_call" | custom-call | tf_op jit(solution)/shard_map/pallas_call | solution.py:47
  86.6 9.2 %all-to-all-done.4 = bf16[64,2,768]{2,1,0:T(2,128)(2,1)S(1)} async-done(((bf16[64,2,768]{2,1,0:T(2,128)(2,1)}), bf16[64,2,768]{2,1,0:T(2,128)(2,1)S(1)}, u32[]{:S(2)}, u32[]{:S(2)}) %all-to-all-start.4) | async-done | bytes 196640 | tf_op jit(solution)/shard_map/all_to_all | solution.py:212
  95.8 0.0 copy-done.3
  95.8 1.4 %shard_map.117 = f32[64,8,64]{2,1,0:T(8,128)} custom-call(bf16[64,1536]{1,0:T(8,128)(2,1)S(1)} %bitcast.16, s32[64,1]{1,0:T(8,128)S(1)} %copy.16.slot_ref, f32[64,8,64]{2,1,0:T(8,128)S(1)} %copy-done.3), custom_call_target="tpu_custom_call" | custom-call | tf_op jit(solution)/shard_map/pallas_call | solution.py:47
  (3 shorter events, 0.1 us)
Async XLA Ops:
  0.6 12.5 %copy-start.7 = (s32[64]{0:T(128)S(1)}, s32[64]{0:T(128)}, u32[]{:S(2)}) copy-start(s32[64]{0:T(128)} %param.17) | copy-start | bytes 772
  0.6 1.0 %copy-start = (bf16[1,64,8,512]{3,2,1,0:T(8,128)(2,1)S(1)}, bf16[1,64,8,512]{3,2,1,0:T(8,128)(2,1)}, u32[]{:S(2)}) copy-start(bf16[1,64,8,512]{3,2,1,0:T(8,128)(2,1)} %param.9) | copy-start | bytes 1572868
  3.8 18.2 %all-to-all-start = ((bf16[8,256,128]{2,1,0:T(8,128)(2,1)}), bf16[8,256,128]{2,1,0:T(8,128)(2,1)S(1)}, u32[]{:S(2)}, u32[]{:S(2)}) async-start(bf16[8,256,128]{2,1,0:T(8,128)(2,1)} %bitcast.1), calls=%async_computation | async-start | bytes 1048576 | tf_op jit(solution)/shard_map/all_to_all | solution.py:212
  47.5 15.1 %copy-start.4 = (bf16[3,64,512]{2,1,0:T(8,128)(2,1)S(1)}, bf16[3,64,512]{2,1,0:T(8,128)(2,1)}, u32[]{:S(2)}) copy-start(bf16[3,64,512]{2,1,0:T(8,128)(2,1)} %param.14) | copy-start | bytes 589828
  47.5 15.1 %copy-start.6 = (f32[3,64]{1,0:T(4,128)S(1)}, f32[3,64]{1,0:T(4,128)}, u32[]{:S(2)}) copy-start(f32[3,64]{1,0:T(4,128)} %param.16) | copy-start | bytes 2308
  47.6 15.2 %copy-start.5 = (f32[3,512]{1,0:T(4,128)S(1)}, f32[3,512]{1,0:T(4,128)}, u32[]{:S(2)}) copy-start(f32[3,512]{1,0:T(4,128)} %param.15) | copy-start | bytes 18436
  60.7 5.7 %collective-permute-start = (bf16[4,64,1536]{2,1,0:T(8,128)(2,1)S(1)}, bf16[4,64,1536]{2,1,0:T(8,128)(2,1)S(1)}, u32[]{:S(2)}, u32[]{:S(2)}) collective-permute-start(bf16[4,64,1536]{2,1,0:T(8,128)(2,1)S(1)} %all_to_all.26.own_ref), channel_id=1, source_target_pairs={{0,1},{1,0},{2,3},{3,2},{4,5},{5,4},{6,7},{7,6},{8,9},{9,8},{10,11... | collective-permute-start | bytes 2359304 | tf_op jit(solution)/shard_map/ppermute | solution.py:244
  66.4 15.8 %copy-start.1 = (f32[3,64,512]{2,1,0:T(8,128)S(1)}, f32[3,64,512]{2,1,0:T(8,128)}, u32[]{:S(2)}) copy-start(f32[3,64,512]{2,1,0:T(8,128)} %stat_ref.3) | copy-start | bytes 1179652
  76.0 8.0 %copy-start.2 = (f32[3,64,512]{2,1,0:T(8,128)S(1)}, f32[3,64,512]{2,1,0:T(8,128)}, u32[]{:S(2)}) copy-start(f32[3,64,512]{2,1,0:T(8,128)} %stat_ref.2) | copy-start | bytes 1179652
  76.8 19.0 %all-to-all-start.4 = ((bf16[64,2,768]{2,1,0:T(2,128)(2,1)}), bf16[64,2,768]{2,1,0:T(2,128)(2,1)S(1)}, u32[]{:S(2)}, u32[]{:S(2)}) async-start(bf16[64,2,768]{2,1,0:T(2,128)(2,1)} %reshape.47), calls=%async_computation.4 | async-start | bytes 393216 | tf_op jit(solution)/shard_map/all_to_all | solution.py:212
  84.0 11.8 %copy-start.3 = (f32[64,8,64]{2,1,0:T(8,128)S(1)}, f32[64,8,64]{2,1,0:T(8,128)}, u32[]{:S(2)}) copy-start(f32[64,8,64]{2,1,0:T(8,128)} %w_ref.1) | copy-start | bytes 393220

commit v3 on v2

--- a/solution.py
+++ b/solution.py
@@ -61,55 +61,44 @@
 CHUNKS = 4
 
 
-def split_kernel(x_ref, out_ref, x_buf, out_buf, in_sem, out_sem):
-    rows = x_buf.shape[1]
+def split_kernel(x_ref, out_ref, buf, sem):
+    rows = 512 // CHUNKS
     per = rows // 8
 
-    def arrival(i):
-        return pltpu.make_async_copy(x_ref.at[pl.ds(rows * i, rows)], x_buf.at[i], in_sem.at[i])
-
     def leaving(i):
-        target = out_ref.at[:, :, pl.ds(per * i, per)]
-        return pltpu.make_async_copy(out_buf.at[i], target, out_sem.at[i])
-
-    for i in range(CHUNKS):
-        arrival(i).start()
+        return pltpu.make_async_copy(buf.at[i], out_ref.at[:, :, pl.ds(per * i, per)], sem.at[i])
+
     order = iota((rows, rows), 0)
     half, r, block = order // (4 * per), (order // per) % 4, order % per
     perm = onehot(8 * block + 4 * half + r == iota((rows, rows), 1))
     for i in range(CHUNKS):
-        arrival(i).wait()
-        moved = dot(perm, x_buf[i]).astype(bf16)
+        moved = dot(perm, x_ref[rows * i : rows * i + rows]).astype(bf16)
         for x in range(4):
             for c in range(2):
                 for r in range(4):
                     at = (4 * c + r) * per
                     piece = moved[at : at + per, LANES * x : LANES * x + LANES]
-                    out_buf[i, 2 * x + c, r] = piece
+                    buf[i, 2 * x + c, r] = piece
         leaving(i).start()
     for i in range(CHUNKS):
         leaving(i).wait()
 
 
 def split(x):
-    rows = 512 // CHUNKS
-    hbm = pl.BlockSpec(memory_space=pltpu.HBM)
     return pl.pallas_call(
         split_kernel,
         out_shape=sds((8, 4, 64, 128), bf16),
-        in_specs=[hbm],
-        out_specs=hbm,
+        in_specs=vmem(1),
+        out_specs=ANY,
         scratch_shapes=[
-            pltpu.VMEM((CHUNKS, rows, 512), bf16),
-            pltpu.VMEM((CHUNKS, 8, 4, rows // 8, 128), bf16),
-            pltpu.SemaphoreType.DMA((CHUNKS,)),
+            pltpu.VMEM((CHUNKS, 8, 4, 64 // CHUNKS, 128), bf16),
             pltpu.SemaphoreType.DMA((CHUNKS,)),
         ],
         compiler_params=pltpu.CompilerParams(vmem_limit_bytes=VMEM_GRANT),
-    )(x).reshape(8, 256, 128)
-
-
-def route_kernel(parts_ref, slot_ref, out_ref):
+    )(x)
+
+
+def route_kernel(parts_ref, slot_ref, after_ref, out_ref):
     total = parts_ref[0].astype(f32)
     for s in range(1, 8):
         total = total + parts_ref[s].astype(f32)
@@ -129,32 +118,59 @@
         out_ref[k] = dot(rows, cols).astype(bf16)
 
 
-def main_kernel(own_ref, other_ref, rf_ref, left_ref, g_ref, p_ref, sq_ref, gs_ref):
+def spread_kernel(piece_ref, out_ref):
+    for q in range(4):
+        for kr in range(12):
+            tile = piece_ref[16 * q : 16 * q + 16, LANES * kr : LANES * kr + LANES]
+            for x in range(4):
+                at = 192 * q + 16 * kr
+                out_ref[x, at : at + 16] = tile
+
+
+def half_products(at, src_ref, rf_ref, left_ref, g_ref):
     lane = iota((8, LANES), 1)
-    squares = jnp.zeros((8, LANES), f32)
     grad_squares = jnp.zeros((8, LANES), f32)
-    for k in range(3):
-        for s, src in enumerate((own_ref, other_ref)):
-            for r in range(4):
-                at = LANES * (4 * k + r)
-                for x in range(4):
-                    row = 256 * s + 64 * r
-                    g_ref[k, row : row + 64, LANES * x : LANES * x + LANES] = src[
-                        x, :, at : at + LANES
+    products = []
+    for k in range(3):
+        for x in range(4):
+            for q in range(4):
+                for r in range(4):
+                    row = 64 * r + 16 * q
+                    g_ref[k, row : row + 16, LANES * x : LANES * x + LANES] = src_ref[
+                        x, pl.ds(192 * q + 16 * (4 * k + r), 16)
                     ]
         g = g_ref[k]
         rf = rf_ref[k]
         wide = jnp.concatenate([rf, jnp.zeros((128, 512), bf16), rf], axis=0)
         mixed = dot(g, wide, 1, 1).astype(bf16)
-        pre = dot(left_ref[k, :256], mixed[:, :128]) + dot(left_ref[k, 256:], mixed[:, 128:])
+        pre = dot(left_ref[k, :256, at : at + 256], mixed[:, :128])
+        products.append(pre + dot(left_ref[k, 256:, at : at + 256], mixed[:, 128:]))
+        gf = g.astype(f32)
+        grad_squares = jnp.where(lane == k, jnp.sum(gf * gf), grad_squares)
+    return products, grad_squares
+
+
+def own_kernel(own_ref, rf_ref, left_ref, g_ref, p_ref, gs_ref):
+    products, grad_squares = half_products(0, own_ref, rf_ref, left_ref, g_ref)
+    for k in range(3):
+        p_ref[k] = products[k]
+    gs_ref[...] = grad_squares
+
+
+def other_kernel(
+    other_ref, rf_ref, left_ref, own_p_ref, own_gs_ref, g_ref, p_ref, sq_ref, gs_ref
+):
+    products, grad_squares = half_products(256, other_ref, rf_ref, left_ref, g_ref)
+    lane = iota((8, LANES), 1)
+    squares = jnp.zeros((8, LANES), f32)
+    for k in range(3):
+        pre = own_p_ref[k] + products[k]
         for t in range(4):
             at = 512 * k + LANES * t
             p_ref[:, at : at + LANES] = pre[64 * t : 64 * t + 64]
         squares = jnp.where(lane == k, jnp.sum(pre * pre), squares)
-        gf = g.astype(f32)
-        grad_squares = jnp.where(lane == k, jnp.sum(gf * gf), grad_squares)
     sq_ref[...] = squares
-    gs_ref[...] = grad_squares
+    gs_ref[...] = own_gs_ref[...] + grad_squares
 
 
 def scale_kernel(sq_ref, gs_ref, p_ref, out_ref):
@@ -165,15 +181,17 @@
         out_ref[:, span] = (p_ref[:, span] * ratio[:, k : k + 1]).astype(bf16)
 
 
-def right_kernel(replica_ref, g_ref, stat_ref, out_ref):
+def right_kernel(replica_ref, own_ref, other_ref, stat_ref, out_ref):
     pick = onehot(iota((64, 512), 1) == 64 * replica_ref[0] + iota((64, 512), 0))
     for k in range(3):
-        g = g_ref[k]
+        g = jnp.concatenate([own_ref[k], other_ref[k]], axis=0)
         cols = dot(pick, g, 1, 1).astype(bf16)
         out_ref[k] = stat_decay * stat_ref[k] + (1.0 - stat_decay) * dot(cols, g)
 
 
-def gram_left_kernel(replica_ref, core_ref, g_ref, stat_ref, after_ref, out_ref):
+def gram_left_kernel(
+    replica_ref, core_ref, own_ref, other_ref, stat_ref, after_ref, out_ref
+):
     core = core_ref[0]
     order = natural_row(iota((512, 512), 1), core)
     back = onehot(order == iota((512, 512), 0))
@@ -181,7 +199,7 @@
         natural_row(iota((64, 512), 1), core) == 64 * replica_ref[0] + iota((64, 512), 0)
     )
     for k in range(3):
-        g = g_ref[k]
+        g = jnp.concatenate([own_ref[k], other_ref[k]], axis=0)
         rows = dot(mine, g).astype(bf16)
         whole = dot(back, g).astype(bf16)
         out_ref[k] = stat_decay * stat_ref[k] + (1.0 - stat_decay) * dot(rows, whole, 1, 1)
@@ -228,34 +246,42 @@
     core = core[None]
     slot_of = slot_table(owners, 3)
 
-    parts = exchange(split(grad_parts.reshape(512, 512)), ("x", "core"))
-    routed = call(
-        route_kernel, vmem(2), sds((64, 1536), bf16), (parts, slot_of.reshape(1, 64))
-    )
-    arrived = exchange(routed.reshape(64, 2, 768), "fsdp").reshape(64, 1536)
-
+    pieces = split(grad_parts.reshape(512, 512))
     left_factor = (left_codes.astype(f32) * left_scales[:, :, None]).astype(bf16)
     right_factor = (right_codes.astype(f32) * right_scales[:, :, None]).astype(bf16)
     left = call(
-        left_kernel, [SMEM, *vmem(1), ANY], sds((3, 512, 512), bf16), (core, left_factor, routed)
-    )
-
-    own = exchange(jnp.broadcast_to(arrived, (4, 64, 1536)), "x")
+        left_kernel, [SMEM, *vmem(1), ANY], sds((3, 512, 512), bf16), (core, left_factor, pieces)
+    )
+    parts = exchange(pieces.reshape(8, 256, 128), ("x", "core"))
+    routed = call(
+        route_kernel,
+        [*vmem(2), ANY],
+        sds((64, 1536), bf16),
+        (parts, slot_of.reshape(1, 64), left),
+    )
+    arrived = exchange(routed.reshape(64, 2, 768), "fsdp").reshape(64, 1536)
+    own = exchange(call(spread_kernel, vmem(1), sds((4, 768, 128), bf16), (arrived,)), "x")
     other = lax.ppermute(own, "core", [(0, 1), (1, 0)])
-    grad, pre, squares, grad_squares = call(
-        main_kernel,
-        vmem(4),
-        [
-            sds((3, 512, 512), bf16),
-            sds((64, 1536), f32),
-            sds((8, 128), f32),
-            sds((8, 128), f32),
-        ],
-        (own, other, right_factor, left),
+    half_grad = sds((3, 256, 512), bf16)
+    small = sds((8, 128), f32)
+    own_grad, own_pre, own_squares = call(
+        own_kernel,
+        vmem(3),
+        [half_grad, sds((3, 256, 128), f32), small],
+        (own, right_factor, left),
+    )
+    other_grad, pre, squares, grad_squares = call(
+        other_kernel,
+        vmem(5),
+        [half_grad, sds((64, 1536), f32), small, small],
+        (other, right_factor, left, own_pre, own_squares),
     )
     all_squares = exchange(squares.reshape(8, 1, 128), ("x", "core")).reshape(8, 128)
     right_new = call(
-        right_kernel, [SMEM, *vmem(2)], sds((3, 64, 512), f32), (replica, grad, right_stat)
+        right_kernel,
+        [SMEM, *vmem(3)],
+        sds((3, 64, 512), f32),
+        (replica, own_grad, other_grad, right_stat),
     )
     scaled = call(
         scale_kernel, vmem(3), sds((64, 1536), bf16), (all_squares, grad_squares, pre)
@@ -263,9 +289,9 @@
     returned = exchange(scaled.reshape(64, 2, 768), "fsdp").reshape(64, 1536)
     left_new = call(
         gram_left_kernel,
-        [SMEM, SMEM, *vmem(2), ANY],
+        [SMEM, SMEM, *vmem(3), ANY],
         sds((3, 64, 512), f32),
-        (replica, core, grad, left_stat, scaled),
+        (replica, core, own_grad, other_grad, left_stat, scaled),
     )
     new_weights = call(
         final_kernel,

time: 97.7 us -> 95.6 us (0.979)
  other arithmetic: 2.07 us -> 0.65 us
  waiting for transfers between devices: 17.9 us -> 16.8 us
    all_to_all x2, waiting for transfers between devices: 17.9 us -> 15.7 us  [exchange(): return lax.all_to_all(x, axis, split_axis=0, concat_axis=0, tiled=True)]
    pallas_call x7 -> x9, Pallas kernels: 9.86 us -> 11.6 us  [call(): pl.pallas_call(kernel, out_shape=shapes, in_specs=ins, out_specs=vmem(len...]
    convert_element_type x1, other arithmetic: 1.8 us -> 0.38 us  [local(): (left_codes.astype(f32) * left_scales[:, :, None]).astype(bf16)]
    pallas_call x1, Pallas kernels: 2.09 us -> 1.03 us  [split(): pl.pallas_call(split_kernel, out_shape=sds((8, 4, 64, 128), bf16), in_spe...]
    ppermute x1, waiting for transfers between devices: 0.01 us -> 1.04 us  [local(): other = lax.ppermute(own, 'core', [(0, 1), (1, 0)])]
  transfers between devices with their start and end apart: 3 -> 3, of which waited for: 2 -> 3; matrix products, arithmetic and copies ran while one was open for 2% -> 1% of each run, Pallas kernels for 6% -> 8%
where the time goes in v3:
time: 95.6 us; the launch traced here: 95.1 us
  blocking collectives  45.2 us (47%)
  starting transfers between devices  17.1 us (18%)
  waiting for transfers between devices  16.8 us (18%)
  Pallas kernels  12.6 us (13%)
  local copies, waits for them, and re-layouts  1.99 us (2%)
    all_to_all x3, blocking collectives, exchange(): return lax.all_to_all(x, axis, split_axis=0, concat_axis=0, tiled=True)  45.2 us
    all_to_all x2, waiting for transfers between devices, exchange(): return lax.all_to_all(x, axis, split_axis=0, concat_axis=0, tiled=True)  15.7 us
    all_to_all x2, starting transfers between devices, exchange(): return lax.all_to_all(x, axis, split_axis=0, concat_axis=0, tiled=True)  15.2 us
    pallas_call x9, Pallas kernels, call(): pl.pallas_call(kernel, out_shape=shapes, in_specs=ins, out_specs=vmem(len...  11.6 us
  transfers between devices with their start and end apart: 3, of which 3 were waited for; matrix products, arithmetic and copies ran while one was open for 1% of the time, Pallas kernels for 8%

profile of v3, /device:TPU:2, one launch (start us, length us, event | category | flops | bytes accessed | tf_op | source)
XLA Modules:
  0.0 95.1 jit_solution(15558573709949029950)
XLA Ops:
  0.6 0.0 copy-start
  0.6 1.0 %copy-done = bf16[1,64,8,512]{3,2,1,0:T(8,128)(2,1)S(1)} copy-done((bf16[1,64,8,512]{3,2,1,0:T(8,128)(2,1)S(1)}, bf16[1,64,8,512]{3,2,1,0:T(8,128)(2,1)}, u32[]{:S(2)}) %copy-start) | copy-done | bytes 524312
  1.7 0.0 copy-start.4
  1.7 0.0 copy-start.6
  1.7 1.0 %shard_map.112.after_ref = bf16[8,4,64,128]{3,2,1,0:T(8,128)(2,1)} custom-call(bf16[512,512]{1,0:T(8,128)(2,1)S(1)} %bitcast.18), custom_call_target="tpu_custom_call" | custom-call | tf_op jit(solution)/shard_map/pallas_call | solution.py:88
  2.7 9.9 %all-to-all-start = ((bf16[8,256,128]{2,1,0:T(8,128)(2,1)}), bf16[8,256,128]{2,1,0:T(8,128)(2,1)}, u32[]{:S(2)}, u32[]{:S(2)}) async-start(bf16[8,256,128]{2,1,0:T(8,128)(2,1)} %bitcast.1), calls=%async_computation | async-start | bytes 1048576 | tf_op jit(solution)/shard_map/all_to_all | solution.py:230
  12.6 0.0 copy-done.4
  12.6 0.0 copy-done.6
  12.6 0.4 multiply_convert_fusion.lf_ref
  13.0 0.0 copy-start.8
  13.0 1.9 %shard_map.113.after_ref.left_ref = bf16[3,512,512]{2,1,0:T(8,128)(2,1)S(1)} custom-call(s32[1]{0:T(128)} %bitcast.3.core_ref, bf16[3,512,512]{2,1,0:T(8,128)(2,1)S(1)} %multiply_convert_fusion.lf_ref, bf16[8,4,64,128]{3,2,1,0:T(8,128)(2,1)} %shard_map.112.after_ref), custom_call_target="tpu_custom_call" | custom-call | tf_op jit(solution)/shard_map/pallas_call | solution.py:47
  14.9 0.0 copy-done.8
  14.9 0.2 convert_reduce_fusion
  15.1 6.5 %all-to-all-done.parts_ref = bf16[8,256,128]{2,1,0:T(8,128)(2,1)} async-done(((bf16[8,256,128]{2,1,0:T(8,128)(2,1)}), bf16[8,256,128]{2,1,0:T(8,128)(2,1)}, u32[]{:S(2)}, u32[]{:S(2)}) %all-to-all-start) | async-done | bytes 524320 | tf_op jit(solution)/shard_map/all_to_all | solution.py:230
  21.6 1.3 %shard_map.114 = bf16[64,1536]{1,0:T(8,128)(2,1)S(1)} custom-call(bf16[8,256,128]{2,1,0:T(8,128)(2,1)} %all-to-all-done.parts_ref, s32[1,64]{1,0:T(1,128)S(1)} %get-tuple-element.18.slot_ref, bf16[3,512,512]{2,1,0:T(8,128)(2,1)S(1)} %shard_map.113.after_ref.left_ref), custom_call_target="tpu_custom_call" | custom-call | tf_op jit(solution)/shard_map/pallas_call | solution.py:47
  22.9 0.1 reshape.43
  23.0 24.6 %all_to_all.25 = bf16[64,2,768]{2,1,0:T(2,128)(2,1)S(1)} all-to-all(bf16[64,2,768]{2,1,0:T(2,128)(2,1)S(1)} %reshape.43), channel_id=1, replica_groups=mesh['fsdp'=64,'x'=4,'core'=2] {'fsdp'}, dimensions={0} | all-to-all | bytes 393216 | tf_op jit(solution)/shard_map/all_to_all | solution.py:230
  47.6 0.0 copy-start.5
  47.6 0.0 copy-start.7
  47.6 0.1 shard_map.115
  47.8 12.9 %all_to_all.26.own_ref = bf16[4,768,128]{2,1,0:T(8,128)(2,1)S(1)} all-to-all(bf16[4,768,128]{2,1,0:T(8,128)(2,1)S(1)} %shard_map.115), channel_id=1, replica_groups=mesh['fsdp'=64,'x'=4,'core'=2] {'x'}, dimensions={0} | all-to-all | bytes 1572864 | tf_op jit(solution)/shard_map/all_to_all | solution.py:230
  60.7 1.9 %collective-permute-start = (bf16[4,768,128]{2,1,0:T(8,128)(2,1)S(1)}, bf16[4,768,128]{2,1,0:T(8,128)(2,1)S(1)}, u32[]{:S(2)}, u32[]{:S(2)}) collective-permute-start(bf16[4,768,128]{2,1,0:T(8,128)(2,1)S(1)} %all_to_all.26.own_ref), channel_id=1, source_target_pairs={{0,1},{1,0},{2,3},{3,2},{4,5},{5,4},{6,7},{7,6},{8,9},{9,8},{10,11... | collective-permute-start | bytes 2359304 | tf_op jit(solution)/shard_map/ppermute | solution.py:264
  62.6 0.0 copy-done.5
  62.6 0.0 copy-done.7
  62.6 0.1 multiply_convert_fusion.1.rf_ref
  62.7 1.1 %shard_map.116 = (bf16[3,256,512]{2,1,0:T(8,128)(2,1)S(1)}, f32[3,256,128]{2,1,0:T(8,128)S(1)}, f32[8,128]{1,0:T(8,128)S(1)}) custom-call(bf16[4,768,128]{2,1,0:T(8,128)(2,1)S(1)} %all_to_all.26.own_ref, bf16[3,64,512]{2,1,0:T(8,128)(2,1)S(1)} %multiply_convert_fusion.1.rf_ref, bf16[3,512,512]{2,1,0:T(8,128)(2,1)S(1)} %shard_map.113.after_ref.left_ref), custom_call_target="tpu_custom_call" | custom-call | tf_op jit(solution)/shard_map/pallas_call | solution.py:47
  63.8 1.0 %collective-permute-done.other_ref = bf16[4,768,128]{2,1,0:T(8,128)(2,1)S(1)} collective-permute-done((bf16[4,768,128]{2,1,0:T(8,128)(2,1)S(1)}, bf16[4,768,128]{2,1,0:T(8,128)(2,1)S(1)}, u32[]{:S(2)}, u32[]{:S(2)}) %collective-permute-start) | collective-permute-done | bytes 786464 | tf_op jit(solution)/shard_map/ppermute | solution.py:264
  64.8 0.0 copy-start.1
  64.8 1.3 %shard_map.117 = (bf16[3,256,512]{2,1,0:T(8,128)(2,1)S(1)}, f32[64,1536]{1,0:T(8,128)S(1)}, f32[8,128]{1,0:T(8,128)S(1)}, f32[8,128]{1,0:T(8,128)S(1)}) custom-call(bf16[4,768,128]{2,1,0:T(8,128)(2,1)S(1)} %collective-permute-done.other_ref, bf16[3,64,512]{2,1,0:T(8,128)(2,1)S(1)} %multiply_convert_fusion.1.rf_ref, ...), custom_call_target="tpu_custom_call" | custom-call | tf_op jit(solution)/shard_map/pallas_call | solution.py:47
  66.1 7.7 %all_to_all.27 = f32[8,1,128]{2,1,0:T(1,128)S(1)} all-to-all(f32[8,1,128]{2,1,0:T(1,128)S(1)} %bitcast.20), channel_id=1, replica_groups=mesh['fsdp'=64,'x'=4,'core'=2] {'x','core'}, dimensions={0} | all-to-all | bytes 8192 | tf_op jit(solution)/shard_map/all_to_all | solution.py:230
  73.8 0.1 shard_map.118.after_ref
  73.9 0.0 copy-start.2
  73.9 0.7 reshape.47
  74.6 5.3 %all-to-all-start.4 = ((bf16[64,2,768]{2,1,0:T(2,128)(2,1)}), bf16[64,2,768]{2,1,0:T(2,128)(2,1)S(1)}, u32[]{:S(2)}, u32[]{:S(2)}) async-start(bf16[64,2,768]{2,1,0:T(2,128)(2,1)} %reshape.47), calls=%async_computation.4 | async-start | bytes 393216 | tf_op jit(solution)/shard_map/all_to_all | solution.py:230
  80.0 0.1 copy.16.slot_ref
  80.1 0.0 copy-done.1
  80.1 1.8 %shard_map.121 = f32[3,64,512]{2,1,0:T(8,128)} custom-call(s32[1]{0:T(128)} %bitcast.8.replica_ref, bf16[3,256,512]{2,1,0:T(8,128)(2,1)S(1)} %get-tuple-element.15.own_ref, bf16[3,256,512]{2,1,0:T(8,128)(2,1)S(1)} %get-tuple-element.16.other_ref, f32[3,64,512]{2,1,0:T(8,128)S(1)} %copy-done.1), custom_call_target="tpu_custom_call" | custom-call | tf_op jit(solution)/shard_map/pallas_call | solution.py:47
  81.9 0.0 copy-done.2
  81.9 0.0 copy-start.3
  81.9 2.6 %shard_map.120 = f32[3,64,512]{2,1,0:T(8,128)} custom-call(s32[1]{0:T(128)} %bitcast.8.replica_ref, s32[1]{0:T(128)} %bitcast.3.core_ref, bf16[3,256,512]{2,1,0:T(8,128)(2,1)S(1)} %get-tuple-element.15.own_ref, bf16[3,256,512]{2,1,0:T(8,128)(2,1)S(1)} %get-tuple-element.16.other_ref, f32[3,64,512]{2,1,0:T(8,128)S(1)} %copy-done.2, ...), custom_call_target="tpu_custom_call" | custom-call | tf_op jit(solution)/shard_map/pallas_call | solution.py:47
  84.5 9.2 %all-to-all-done.4 = bf16[64,2,768]{2,1,0:T(2,128)(2,1)S(1)} async-done(((bf16[64,2,768]{2,1,0:T(2,128)(2,1)}), bf16[64,2,768]{2,1,0:T(2,128)(2,1)S(1)}, u32[]{:S(2)}, u32[]{:S(2)}) %all-to-all-start.4) | async-done | bytes 196640 | tf_op jit(solution)/shard_map/all_to_all | solution.py:230
  93.7 0.0 copy-done.3
  93.7 1.4 %shard_map.119 = f32[64,8,64]{2,1,0:T(8,128)} custom-call(bf16[64,1536]{1,0:T(8,128)(2,1)S(1)} %bitcast.16, s32[64,1]{1,0:T(8,128)S(1)} %copy.16.slot_ref, f32[64,8,64]{2,1,0:T(8,128)S(1)} %copy-done.3), custom_call_target="tpu_custom_call" | custom-call | tf_op jit(solution)/shard_map/pallas_call | solution.py:47
  (3 shorter events, 0.1 us)
Async XLA Ops:
  0.6 1.0 %copy-start = (bf16[1,64,8,512]{3,2,1,0:T(8,128)(2,1)S(1)}, bf16[1,64,8,512]{3,2,1,0:T(8,128)(2,1)}, u32[]{:S(2)}) copy-start(bf16[1,64,8,512]{3,2,1,0:T(8,128)(2,1)} %param.9) | copy-start | bytes 1572868
  1.7 11.0 %copy-start.4 = (bf16[3,512,512]{2,1,0:T(8,128)(2,1)S(1)}, bf16[3,512,512]{2,1,0:T(8,128)(2,1)}, u32[]{:S(2)}) copy-start(bf16[3,512,512]{2,1,0:T(8,128)(2,1)} %param.13) | copy-start | bytes 4718596
  1.7 11.0 %copy-start.6 = (f32[3,512]{1,0:T(4,128)S(1)}, f32[3,512]{1,0:T(4,128)}, u32[]{:S(2)}) copy-start(f32[3,512]{1,0:T(4,128)} %param.15) | copy-start | bytes 18436
  2.7 18.9 %all-to-all-start = ((bf16[8,256,128]{2,1,0:T(8,128)(2,1)}), bf16[8,256,128]{2,1,0:T(8,128)(2,1)}, u32[]{:S(2)}, u32[]{:S(2)}) async-start(bf16[8,256,128]{2,1,0:T(8,128)(2,1)} %bitcast.1), calls=%async_computation | async-start | bytes 1048576 | tf_op jit(solution)/shard_map/all_to_all | solution.py:230
  13.0 1.9 %copy-start.8 = (s32[64]{0:T(128)S(1)}, s32[64]{0:T(128)}, u32[]{:S(2)}) copy-start(s32[64]{0:T(128)} %param.17) | copy-start | bytes 772
  47.6 15.0 %copy-start.5 = (bf16[3,64,512]{2,1,0:T(8,128)(2,1)S(1)}, bf16[3,64,512]{2,1,0:T(8,128)(2,1)}, u32[]{:S(2)}) copy-start(bf16[3,64,512]{2,1,0:T(8,128)(2,1)} %param.14) | copy-start | bytes 589828
  47.6 15.0 %copy-start.7 = (f32[3,64]{1,0:T(4,128)S(1)}, f32[3,64]{1,0:T(4,128)}, u32[]{:S(2)}) copy-start(f32[3,64]{1,0:T(4,128)} %param.16) | copy-start | bytes 2308
  60.7 4.2 %collective-permute-start = (bf16[4,768,128]{2,1,0:T(8,128)(2,1)S(1)}, bf16[4,768,128]{2,1,0:T(8,128)(2,1)S(1)}, u32[]{:S(2)}, u32[]{:S(2)}) collective-permute-start(bf16[4,768,128]{2,1,0:T(8,128)(2,1)S(1)} %all_to_all.26.own_ref), channel_id=1, source_target_pairs={{0,1},{1,0},{2,3},{3,2},{4,5},{5,4},{6,7},{7,6},{8,9},{9,8},{10,11... | collective-permute-start | bytes 2359304 | tf_op jit(solution)/shard_map/ppermute | solution.py:264
  64.8 15.2 %copy-start.1 = (f32[3,64,512]{2,1,0:T(8,128)S(1)}, f32[3,64,512]{2,1,0:T(8,128)}, u32[]{:S(2)}) copy-start(f32[3,64,512]{2,1,0:T(8,128)} %stat_ref.3) | copy-start | bytes 1179652
  73.9 8.0 %copy-start.2 = (f32[3,64,512]{2,1,0:T(8,128)S(1)}, f32[3,64,512]{2,1,0:T(8,128)}, u32[]{:S(2)}) copy-start(f32[3,64,512]{2,1,0:T(8,128)} %stat_ref.2) | copy-start | bytes 1179652
  74.6 19.0 %all-to-all-start.4 = ((bf16[64,2,768]{2,1,0:T(2,128)(2,1)}), bf16[64,2,768]{2,1,0:T(2,128)(2,1)S(1)}, u32[]{:S(2)}, u32[]{:S(2)}) async-start(bf16[64,2,768]{2,1,0:T(2,128)(2,1)} %reshape.47), calls=%async_computation.4 | async-start | bytes 393216 | tf_op jit(solution)/shard_map/all_to_all | solution.py:230
  81.9 11.8 %copy-start.3 = (f32[64,8,64]{2,1,0:T(8,128)S(1)}, f32[64,8,64]{2,1,0:T(8,128)}, u32[]{:S(2)}) copy-start(f32[64,8,64]{2,1,0:T(8,128)} %w_ref.1) | copy-start | bytes 393220

commit v4 on v3

--- a/solution.py
+++ b/solution.py
@@ -61,40 +61,49 @@
 CHUNKS = 4
 
 
-def split_kernel(x_ref, out_ref, buf, sem):
-    rows = 512 // CHUNKS
+def split_kernel(x_ref, out_ref, x_buf, out_buf, in_sem, out_sem):
+    rows = x_buf.shape[1]
     per = rows // 8
 
+    def arrival(i):
+        return pltpu.make_async_copy(x_ref.at[pl.ds(rows * i, rows)], x_buf.at[i], in_sem.at[i])
+
     def leaving(i):
-        return pltpu.make_async_copy(buf.at[i], out_ref.at[:, :, pl.ds(per * i, per)], sem.at[i])
-
+        target = out_ref.at[:, :, pl.ds(per * i, per)]
+        return pltpu.make_async_copy(out_buf.at[i], target, out_sem.at[i])
+
+    for i in range(CHUNKS):
+        arrival(i).start()
     order = iota((rows, rows), 0)
     half, r, block = order // (4 * per), (order // per) % 4, order % per
     perm = onehot(8 * block + 4 * half + r == iota((rows, rows), 1))
     for i in range(CHUNKS):
-        moved = dot(perm, x_ref[rows * i : rows * i + rows]).astype(bf16)
+        arrival(i).wait()
+        moved = dot(perm, x_buf[i]).astype(bf16)
         for x in range(4):
             for c in range(2):
                 for r in range(4):
                     at = (4 * c + r) * per
                     piece = moved[at : at + per, LANES * x : LANES * x + LANES]
-                    buf[i, 2 * x + c, r] = piece
+                    out_buf[i, 2 * x + c, r] = piece
         leaving(i).start()
     for i in range(CHUNKS):
         leaving(i).wait()
 
 
 def split(x):
+    rows = 512 // CHUNKS
     return pl.pallas_call(
         split_kernel,
         out_shape=sds((8, 4, 64, 128), bf16),
-        in_specs=vmem(1),
+        in_specs=[ANY],
         out_specs=ANY,
         scratch_shapes=[
-            pltpu.VMEM((CHUNKS, 8, 4, 64 // CHUNKS, 128), bf16),
+            pltpu.VMEM((CHUNKS, rows, 512), bf16),
+            pltpu.VMEM((CHUNKS, 8, 4, rows // 8, 128), bf16),
+            pltpu.SemaphoreType.DMA((CHUNKS,)),
             pltpu.SemaphoreType.DMA((CHUNKS,)),
         ],
-        compiler_params=pltpu.CompilerParams(vmem_limit_bytes=VMEM_GRANT),
     )(x)
 
 
@@ -110,12 +119,14 @@
         out_ref[:, 512 * k : 512 * k + 512] = dot(pick, wide).astype(bf16)
 
 
-def left_kernel(core_ref, lf_ref, after_ref, out_ref):
+def left_kernel(core_ref, lc_ref, ls_ref, rc_ref, rs_ref, out_ref, rf_ref):
     back = onehot(natural_row(iota((512, 512), 0), 0) == iota((512, 512), 1))
     cols = onehot(natural_row(iota((512, 512), 1), core_ref[0]) == iota((512, 512), 0))
     for k in range(3):
-        rows = dot(back, lf_ref[k]).astype(bf16)
+        factor = (lc_ref[k].astype(f32) * ls_ref[:, k : k + 1]).astype(bf16)
+        rows = dot(back, factor).astype(bf16)
         out_ref[k] = dot(rows, cols).astype(bf16)
+        rf_ref[k] = (rc_ref[k].astype(f32) * rs_ref[:, k : k + 1]).astype(bf16)
 
 
 def spread_kernel(piece_ref, out_ref):
@@ -205,17 +216,28 @@
         out_ref[k] = stat_decay * stat_ref[k] + (1.0 - stat_decay) * dot(rows, whole, 1, 1)
 
 
-def final_kernel(ret_ref, slot_ref, w_ref, out_ref):
+def final_kernel(ret_ref, slot_ref, w_ref, out_ref, buf, sem):
     slot = slot_ref[...]
     update = jnp.zeros((64, 512), f32)
     for k in range(3):
         pick = onehot(slot == 3 * iota((64, 64), 1) + k)
         update = update + dot(pick, ret_ref[:, 512 * k : 512 * k + 512])
-    for t in range(4):
-        for half in range(2):
-            row = 4 * half + t
-            at = LANES * t + 64 * half
-            out_ref[:, row, :] = w_ref[:, row, :] - update[:, at : at + 64]
+    per = 64 // CHUNKS
+
+    def leaving(i):
+        part = pl.ds(per * i, per)
+        return pltpu.make_async_copy(buf.at[part], out_ref.at[part], sem.at[i])
+
+    for i in range(CHUNKS):
+        part = slice(per * i, per * i + per)
+        for t in range(4):
+            for half in range(2):
+                row = 4 * half + t
+                at = LANES * t + 64 * half
+                buf[part, row, :] = w_ref[part, row, :] - update[part, at : at + 64]
+        leaving(i).start()
+    for i in range(CHUNKS):
+        leaving(i).wait()
 
 
 def slot_table(owners, capacity):
@@ -247,10 +269,11 @@
     slot_of = slot_table(owners, 3)
 
     pieces = split(grad_parts.reshape(512, 512))
-    left_factor = (left_codes.astype(f32) * left_scales[:, :, None]).astype(bf16)
-    right_factor = (right_codes.astype(f32) * right_scales[:, :, None]).astype(bf16)
-    left = call(
-        left_kernel, [SMEM, *vmem(1), ANY], sds((3, 512, 512), bf16), (core, left_factor, pieces)
+    left, right_factor = call(
+        left_kernel,
+        [SMEM, *vmem(4)],
+        [sds((3, 512, 512), bf16), sds((3, 64, 512), bf16)],
+        (core, left_codes, left_scales.T, right_codes, right_scales.T),
     )
     parts = exchange(pieces.reshape(8, 256, 128), ("x", "core"))
     routed = call(
@@ -293,12 +316,14 @@
         sds((3, 64, 512), f32),
         (replica, core, own_grad, other_grad, left_stat, scaled),
     )
-    new_weights = call(
+    new_weights = pl.pallas_call(
         final_kernel,
-        vmem(3),
-        sds((64, 8, 64), f32),
-        (returned, slot_of.reshape(64, 1), weights),
-    )
+        out_shape=sds((64, 8, 64), f32),
+        in_specs=vmem(3),
+        out_specs=ANY,
+        scratch_shapes=[pltpu.VMEM((64, 8, 64), f32), pltpu.SemaphoreType.DMA((CHUNKS,))],
+        compiler_params=pltpu.CompilerParams(vmem_limit_bytes=VMEM_GRANT),
+    )(returned, slot_of.reshape(64, 1), weights)
     return (new_weights, left_new, right_new)
 
 

time: 95.6 us -> 94.9 us (level)
  waiting for transfers between devices: 16.8 us -> 15.4 us
    pallas_call x9 -> x8, Pallas kernels: 11.6 us -> 9.22 us  [call(): pl.pallas_call(kernel, out_shape=shapes, in_specs=ins, out_specs=vmem(len...]
    all_to_all x2, waiting for transfers between devices: 15.7 us -> 14.2 us  [exchange(): return lax.all_to_all(x, axis, split_axis=0, concat_axis=0, tiled=True)]
    pallas_call x0 -> x1, Pallas kernels: none -> 1.43 us  [local(): pl.pallas_call(final_kernel, out_shape=sds((64, 8, 64), f32), in_specs=vm...]
    pallas_call x1, Pallas kernels: 1.03 us -> 2.37 us  [split(): pl.pallas_call(split_kernel, out_shape=sds((8, 4, 64, 128), bf16), in_spe...]
where the time goes in v4:
time: 94.9 us; the launch traced here: 94.5 us
  blocking collectives  46 us (48%)
  starting transfers between devices  16.5 us (17%)
  waiting for transfers between devices  15.4 us (16%)
  Pallas kernels  13 us (14%)
  local copies, waits for them, and re-layouts  2.6 us (3%)
    all_to_all x3, blocking collectives, exchange(): return lax.all_to_all(x, axis, split_axis=0, concat_axis=0, tiled=True)  46 us
    all_to_all x2, starting transfers between devices, exchange(): return lax.all_to_all(x, axis, split_axis=0, concat_axis=0, tiled=True)  14.6 us
    all_to_all x2, waiting for transfers between devices, exchange(): return lax.all_to_all(x, axis, split_axis=0, concat_axis=0, tiled=True)  14.2 us
    pallas_call x8, Pallas kernels, call(): pl.pallas_call(kernel, out_shape=shapes, in_specs=ins, out_specs=vmem(len...  9.22 us
    pallas_call x1, Pallas kernels, split(): pl.pallas_call(split_kernel, out_shape=sds((8, 4, 64, 128), bf16), in_spe...  2.37 us
    ppermute x1, starting transfers between devices, local(): other = lax.ppermute(own, 'core', [(0, 1), (1, 0)])  1.91 us
  transfers between devices with their start and end apart: 3, of which 3 were waited for; matrix products, arithmetic and copies ran while one was open for 1% of the time, Pallas kernels for 8%

profile of v4, /device:TPU:2, one launch (start us, length us, event | category | flops | bytes accessed | tf_op | source)
XLA Modules:
  0.0 94.5 jit_solution(15098476021698973028)
XLA Ops:
  0.6 0.0 copy-start.5
  0.6 0.0 copy-start.6
  0.7 0.0 copy-start.4
  0.7 2.4 %shard_map.112 = bf16[8,4,64,128]{3,2,1,0:T(8,128)(2,1)} custom-call(bf16[512,512]{1,0:T(8,128)(2,1)} %bitcast.27), custom_call_target="tpu_custom_call" | custom-call | tf_op jit(solution)/shard_map/pallas_call | solution.py:96
  3.0 0.0 copy-start.7
  3.0 9.3 %all-to-all-start = ((bf16[8,256,128]{2,1,0:T(8,128)(2,1)}), bf16[8,256,128]{2,1,0:T(8,128)(2,1)S(1)}, u32[]{:S(2)}, u32[]{:S(2)}) async-start(bf16[8,256,128]{2,1,0:T(8,128)(2,1)} %bitcast.24), calls=%async_computation | async-start | bytes 1048576 | tf_op jit(solution)/shard_map/all_to_all | solution.py:252
  12.3 0.0 copy-done.5
  12.3 0.1 copy.19
  12.5 0.0 copy-done.6
  12.5 0.1 copy.20
  12.6 0.0 copy-done.4
  12.6 0.0 copy-start
  12.6 1.4 %copy-done = bf16[3,512,512]{2,1,0:T(8,128)(2,1)S(1)} copy-done((bf16[3,512,512]{2,1,0:T(8,128)(2,1)S(1)}, bf16[3,512,512]{2,1,0:T(8,128)(2,1)}, u32[]{:S(2)}) %copy-start) | copy-done | bytes 1572888
  14.0 2.0 %shard_map.113 = (bf16[3,512,512]{2,1,0:T(8,128)(2,1)S(1)}, bf16[3,64,512]{2,1,0:T(8,128)(2,1)S(1)}) custom-call(s32[1]{0:T(128)} %bitcast.3.core_ref, bf16[3,512,512]{2,1,0:T(8,128)(2,1)S(1)} %copy-done, f32[512,3]{1,0:T(8,128)S(1)} %bitcast.18, bf16[3,64,512]{2,1,0:T(8,128)(2,1)S(1)} %copy-done.4, f32[64,3]{1,0:T(8,128)S(1)} %bitcast.21), custom_call_target="tpu_custom_call" | custom-call | tf_op jit(solution)/shard_map/pallas_call | solution.py:47
  16.0 0.0 copy-done.7
  16.0 0.2 convert_reduce_fusion
  16.2 5.0 %all-to-all-done.parts_ref = bf16[8,256,128]{2,1,0:T(8,128)(2,1)S(1)} async-done(((bf16[8,256,128]{2,1,0:T(8,128)(2,1)}), bf16[8,256,128]{2,1,0:T(8,128)(2,1)S(1)}, u32[]{:S(2)}, u32[]{:S(2)}) %all-to-all-start) | async-done | bytes 524320 | tf_op jit(solution)/shard_map/all_to_all | solution.py:252
  21.2 0.2 shard_map.114
  21.5 0.1 reshape.41
  21.5 25.3 %all_to_all.25 = bf16[64,2,768]{2,1,0:T(2,128)(2,1)S(1)} all-to-all(bf16[64,2,768]{2,1,0:T(2,128)(2,1)S(1)} %reshape.41), channel_id=1, replica_groups=mesh['fsdp'=64,'x'=4,'core'=2] {'fsdp'}, dimensions={0} | all-to-all | bytes 393216 | tf_op jit(solution)/shard_map/all_to_all | solution.py:252
  46.8 0.1 shard_map.115
  46.9 12.9 %all_to_all.26.own_ref = bf16[4,768,128]{2,1,0:T(8,128)(2,1)S(1)} all-to-all(bf16[4,768,128]{2,1,0:T(8,128)(2,1)S(1)} %shard_map.115), channel_id=1, replica_groups=mesh['fsdp'=64,'x'=4,'core'=2] {'x'}, dimensions={0} | all-to-all | bytes 1572864 | tf_op jit(solution)/shard_map/all_to_all | solution.py:252
  59.9 1.9 %collective-permute-start = (bf16[4,768,128]{2,1,0:T(8,128)(2,1)S(1)}, bf16[4,768,128]{2,1,0:T(8,128)(2,1)S(1)}, u32[]{:S(2)}, u32[]{:S(2)}) collective-permute-start(bf16[4,768,128]{2,1,0:T(8,128)(2,1)S(1)} %all_to_all.26.own_ref), channel_id=1, source_target_pairs={{0,1},{1,0},{2,3},{3,2},{4,5},{5,4},{6,7},{7,6},{8,9},{9,8},{10,11... | collective-permute-start | bytes 2359304 | tf_op jit(solution)/shard_map/ppermute | solution.py:287
  61.8 1.1 %shard_map.116 = (bf16[3,256,512]{2,1,0:T(8,128)(2,1)S(1)}, f32[3,256,128]{2,1,0:T(8,128)S(1)}, f32[8,128]{1,0:T(8,128)S(1)}) custom-call(bf16[4,768,128]{2,1,0:T(8,128)(2,1)S(1)} %all_to_all.26.own_ref, bf16[3,64,512]{2,1,0:T(8,128)(2,1)S(1)} %get-tuple-element.13.rf_ref, bf16[3,512,512]{2,1,0:T(8,128)(2,1)S(1)} %get-tuple-element.12.after_ref.left_ref), custom_call_target="tpu_custom_call" | custom-call | tf_op jit(solution)/shard_map/pallas_call | solution.py:47
  62.9 1.2 %collective-permute-done.other_ref = bf16[4,768,128]{2,1,0:T(8,128)(2,1)S(1)} collective-permute-done((bf16[4,768,128]{2,1,0:T(8,128)(2,1)S(1)}, bf16[4,768,128]{2,1,0:T(8,128)(2,1)S(1)}, u32[]{:S(2)}, u32[]{:S(2)}) %collective-permute-start) | collective-permute-done | bytes 786464 | tf_op jit(solution)/shard_map/ppermute | solution.py:287
  64.0 1.3 %shard_map.117 = (bf16[3,256,512]{2,1,0:T(8,128)(2,1)S(1)}, f32[64,1536]{1,0:T(8,128)S(1)}, f32[8,128]{1,0:T(8,128)S(1)}, f32[8,128]{1,0:T(8,128)S(1)}) custom-call(bf16[4,768,128]{2,1,0:T(8,128)(2,1)S(1)} %collective-permute-done.other_ref, bf16[3,64,512]{2,1,0:T(8,128)(2,1)S(1)} %get-tuple-element.13.rf_ref, ...), custom_call_target="tpu_custom_call" | custom-call | tf_op jit(solution)/shard_map/pallas_call | solution.py:47
  65.3 0.0 copy-start.1
  65.3 7.8 %all_to_all.27 = f32[8,1,128]{2,1,0:T(1,128)S(1)} all-to-all(f32[8,1,128]{2,1,0:T(1,128)S(1)} %bitcast.23), channel_id=1, replica_groups=mesh['fsdp'=64,'x'=4,'core'=2] {'x','core'}, dimensions={0} | all-to-all | bytes 8192 | tf_op jit(solution)/shard_map/all_to_all | solution.py:252
  73.1 0.1 shard_map.118.after_ref
  73.2 0.0 copy-start.2
  73.2 0.7 reshape.45
  74.0 5.3 %all-to-all-start.4 = ((bf16[64,2,768]{2,1,0:T(2,128)(2,1)}), bf16[64,2,768]{2,1,0:T(2,128)(2,1)S(1)}, u32[]{:S(2)}, u32[]{:S(2)}) async-start(bf16[64,2,768]{2,1,0:T(2,128)(2,1)} %reshape.45), calls=%async_computation.4 | async-start | bytes 393216 | tf_op jit(solution)/shard_map/all_to_all | solution.py:252
  79.3 0.1 copy.22.slot_ref
  79.4 0.0 copy-done.1
  79.4 1.8 %shard_map.121 = f32[3,64,512]{2,1,0:T(8,128)} custom-call(s32[1]{0:T(128)} %bitcast.10.replica_ref, bf16[3,256,512]{2,1,0:T(8,128)(2,1)S(1)} %get-tuple-element.19.own_ref, bf16[3,256,512]{2,1,0:T(8,128)(2,1)S(1)} %get-tuple-element.20.other_ref, f32[3,64,512]{2,1,0:T(8,128)S(1)} %copy-done.1), custom_call_target="tpu_custom_call" | custom-call | tf_op jit(solution)/shard_map/pallas_call | solution.py:47
  81.2 0.0 copy-done.2
  81.2 0.0 copy-start.3
  81.2 2.6 %shard_map.120 = f32[3,64,512]{2,1,0:T(8,128)} custom-call(s32[1]{0:T(128)} %bitcast.10.replica_ref, s32[1]{0:T(128)} %bitcast.3.core_ref, bf16[3,256,512]{2,1,0:T(8,128)(2,1)S(1)} %get-tuple-element.19.own_ref, bf16[3,256,512]{2,1,0:T(8,128)(2,1)S(1)} %get-tuple-element.20.other_ref, f32[3,64,512]{2,1,0:T(8,128)S(1)} %copy-done.2, ...), custom_call_target="tpu_custom_call" | custom-call | tf_op jit(solution)/shard_map/pallas_call | solution.py:47
  83.8 9.2 %all-to-all-done.4 = bf16[64,2,768]{2,1,0:T(2,128)(2,1)S(1)} async-done(((bf16[64,2,768]{2,1,0:T(2,128)(2,1)}), bf16[64,2,768]{2,1,0:T(2,128)(2,1)S(1)}, u32[]{:S(2)}, u32[]{:S(2)}) %all-to-all-start.4) | async-done | bytes 196640 | tf_op jit(solution)/shard_map/all_to_all | solution.py:252
  93.0 0.0 copy-done.3
  93.0 1.4 %shard_map.119 = f32[64,8,64]{2,1,0:T(8,128)} custom-call(bf16[64,1536]{1,0:T(8,128)(2,1)S(1)} %bitcast.19, s32[64,1]{1,0:T(8,128)S(1)} %copy.22.slot_ref, f32[64,8,64]{2,1,0:T(8,128)S(1)} %copy-done.3), custom_call_target="tpu_custom_call" | custom-call | tf_op jit(solution)/shard_map/pallas_call | solution.py:319
  (3 shorter events, 0.1 us)
Async XLA Ops:
  0.6 11.7 %copy-start.5 = (f32[3,512]{1,0:T(4,128)S(1)}, f32[3,512]{1,0:T(4,128)}, u32[]{:S(2)}) copy-start(f32[3,512]{1,0:T(4,128)} %param.15) | copy-start | bytes 18436
  0.6 11.9 %copy-start.6 = (f32[3,64]{1,0:T(4,128)S(1)}, f32[3,64]{1,0:T(4,128)}, u32[]{:S(2)}) copy-start(f32[3,64]{1,0:T(4,128)} %param.16) | copy-start | bytes 2308
  0.7 12.0 %copy-start.4 = (bf16[3,64,512]{2,1,0:T(8,128)(2,1)S(1)}, bf16[3,64,512]{2,1,0:T(8,128)(2,1)}, u32[]{:S(2)}) copy-start(bf16[3,64,512]{2,1,0:T(8,128)(2,1)} %rc_ref.1) | copy-start | bytes 589828
  3.0 13.0 %copy-start.7 = (s32[64]{0:T(128)S(1)}, s32[64]{0:T(128)}, u32[]{:S(2)}) copy-start(s32[64]{0:T(128)} %param.17) | copy-start | bytes 772
  3.0 18.2 %all-to-all-start = ((bf16[8,256,128]{2,1,0:T(8,128)(2,1)}), bf16[8,256,128]{2,1,0:T(8,128)(2,1)S(1)}, u32[]{:S(2)}, u32[]{:S(2)}) async-start(bf16[8,256,128]{2,1,0:T(8,128)(2,1)} %bitcast.24), calls=%async_computation | async-start | bytes 1048576 | tf_op jit(solution)/shard_map/all_to_all | solution.py:252
  12.6 1.4 %copy-start = (bf16[3,512,512]{2,1,0:T(8,128)(2,1)S(1)}, bf16[3,512,512]{2,1,0:T(8,128)(2,1)}, u32[]{:S(2)}) copy-start(bf16[3,512,512]{2,1,0:T(8,128)(2,1)} %lc_ref.1) | copy-start | bytes 4718596
  59.9 4.2 %collective-permute-start = (bf16[4,768,128]{2,1,0:T(8,128)(2,1)S(1)}, bf16[4,768,128]{2,1,0:T(8,128)(2,1)S(1)}, u32[]{:S(2)}, u32[]{:S(2)}) collective-permute-start(bf16[4,768,128]{2,1,0:T(8,128)(2,1)S(1)} %all_to_all.26.own_ref), channel_id=1, source_target_pairs={{0,1},{1,0},{2,3},{3,2},{4,5},{5,4},{6,7},{7,6},{8,9},{9,8},{10,11... | collective-permute-start | bytes 2359304 | tf_op jit(solution)/shard_map/ppermute | solution.py:287
  65.3 14.1 %copy-start.1 = (f32[3,64,512]{2,1,0:T(8,128)S(1)}, f32[3,64,512]{2,1,0:T(8,128)}, u32[]{:S(2)}) copy-start(f32[3,64,512]{2,1,0:T(8,128)} %stat_ref.3) | copy-start | bytes 1179652
  73.2 8.0 %copy-start.2 = (f32[3,64,512]{2,1,0:T(8,128)S(1)}, f32[3,64,512]{2,1,0:T(8,128)}, u32[]{:S(2)}) copy-start(f32[3,64,512]{2,1,0:T(8,128)} %stat_ref.2) | copy-start | bytes 1179652
  74.0 19.0 %all-to-all-start.4 = ((bf16[64,2,768]{2,1,0:T(2,128)(2,1)}), bf16[64,2,768]{2,1,0:T(2,128)(2,1)S(1)}, u32[]{:S(2)}, u32[]{:S(2)}) async-start(bf16[64,2,768]{2,1,0:T(2,128)(2,1)} %reshape.45), calls=%async_computation.4 | async-start | bytes 393216 | tf_op jit(solution)/shard_map/all_to_all | solution.py:252
  81.2 11.8 %copy-start.3 = (f32[64,8,64]{2,1,0:T(8,128)S(1)}, f32[64,8,64]{2,1,0:T(8,128)}, u32[]{:S(2)}) copy-start(f32[64,8,64]{2,1,0:T(8,128)} %w_ref.1) | copy-start | bytes 393220

commit v5 on v4

--- a/solution.py
+++ b/solution.py
@@ -61,53 +61,44 @@
 CHUNKS = 4
 
 
-def split_kernel(x_ref, out_ref, x_buf, out_buf, in_sem, out_sem):
-    rows = x_buf.shape[1]
+def split_kernel(x_ref, out_ref, buf, sem):
+    rows = 512 // CHUNKS
     per = rows // 8
 
-    def arrival(i):
-        return pltpu.make_async_copy(x_ref.at[pl.ds(rows * i, rows)], x_buf.at[i], in_sem.at[i])
-
     def leaving(i):
-        target = out_ref.at[:, :, pl.ds(per * i, per)]
-        return pltpu.make_async_copy(out_buf.at[i], target, out_sem.at[i])
-
-    for i in range(CHUNKS):
-        arrival(i).start()
+        return pltpu.make_async_copy(buf.at[i], out_ref.at[:, :, pl.ds(per * i, per)], sem.at[i])
+
     order = iota((rows, rows), 0)
     half, r, block = order // (4 * per), (order // per) % 4, order % per
     perm = onehot(8 * block + 4 * half + r == iota((rows, rows), 1))
     for i in range(CHUNKS):
-        arrival(i).wait()
-        moved = dot(perm, x_buf[i]).astype(bf16)
+        moved = dot(perm, x_ref[rows * i : rows * i + rows]).astype(bf16)
         for x in range(4):
             for c in range(2):
                 for r in range(4):
                     at = (4 * c + r) * per
                     piece = moved[at : at + per, LANES * x : LANES * x + LANES]
-                    out_buf[i, 2 * x + c, r] = piece
+                    buf[i, 2 * x + c, r] = piece
         leaving(i).start()
     for i in range(CHUNKS):
         leaving(i).wait()
 
 
 def split(x):
-    rows = 512 // CHUNKS
     return pl.pallas_call(
         split_kernel,
         out_shape=sds((8, 4, 64, 128), bf16),
-        in_specs=[ANY],
+        in_specs=vmem(1),
         out_specs=ANY,
         scratch_shapes=[
-            pltpu.VMEM((CHUNKS, rows, 512), bf16),
-            pltpu.VMEM((CHUNKS, 8, 4, rows // 8, 128), bf16),
-            pltpu.SemaphoreType.DMA((CHUNKS,)),
+            pltpu.VMEM((CHUNKS, 8, 4, 64 // CHUNKS, 128), bf16),
             pltpu.SemaphoreType.DMA((CHUNKS,)),
         ],
+        compiler_params=pltpu.CompilerParams(vmem_limit_bytes=VMEM_GRANT),
     )(x)
 
 
-def route_kernel(parts_ref, slot_ref, after_ref, out_ref):
+def route_kernel(parts_ref, slot_ref, out_ref):
     total = parts_ref[0].astype(f32)
     for s in range(1, 8):
         total = total + parts_ref[s].astype(f32)
@@ -119,7 +110,7 @@
         out_ref[:, 512 * k : 512 * k + 512] = dot(pick, wide).astype(bf16)
 
 
-def left_kernel(core_ref, lc_ref, ls_ref, rc_ref, rs_ref, out_ref, rf_ref):
+def left_kernel(core_ref, lc_ref, ls_ref, rc_ref, rs_ref, after_ref, out_ref, rf_ref):
     back = onehot(natural_row(iota((512, 512), 0), 0) == iota((512, 512), 1))
     cols = onehot(natural_row(iota((512, 512), 1), core_ref[0]) == iota((512, 512), 0))
     for k in range(3):
@@ -129,7 +120,7 @@
         rf_ref[k] = (rc_ref[k].astype(f32) * rs_ref[:, k : k + 1]).astype(bf16)
 
 
-def spread_kernel(piece_ref, out_ref):
+def spread_kernel(piece_ref, after_ref, out_ref):
     for q in range(4):
         for kr in range(12):
             tile = piece_ref[16 * q : 16 * q + 16, LANES * kr : LANES * kr + LANES]
@@ -269,21 +260,21 @@
     slot_of = slot_table(owners, 3)
 
     pieces = split(grad_parts.reshape(512, 512))
+    parts = exchange(pieces.reshape(8, 256, 128), ("x", "core"))
+    routed = call(
+        route_kernel, vmem(2), sds((64, 1536), bf16), (parts, slot_of.reshape(1, 64))
+    )
     left, right_factor = call(
         left_kernel,
-        [SMEM, *vmem(4)],
+        [SMEM, *vmem(4), ANY],
         [sds((3, 512, 512), bf16), sds((3, 64, 512), bf16)],
-        (core, left_codes, left_scales.T, right_codes, right_scales.T),
-    )
-    parts = exchange(pieces.reshape(8, 256, 128), ("x", "core"))
-    routed = call(
-        route_kernel,
-        [*vmem(2), ANY],
-        sds((64, 1536), bf16),
-        (parts, slot_of.reshape(1, 64), left),
+        (core, left_codes, left_scales.T, right_codes, right_scales.T, routed),
     )
     arrived = exchange(routed.reshape(64, 2, 768), "fsdp").reshape(64, 1536)
-    own = exchange(call(spread_kernel, vmem(1), sds((4, 768, 128), bf16), (arrived,)), "x")
+    spread = call(
+        spread_kernel, [*vmem(1), ANY], sds((4, 768, 128), bf16), (arrived, right_factor)
+    )
+    own = exchange(spread, "x")
     other = lax.ppermute(own, "core", [(0, 1), (1, 0)])
     half_grad = sds((3, 256, 512), bf16)
     small = sds((8, 128), f32)

time: 94.9 us -> 95.7 us (level)
  blocking collectives: 46 us -> 20.7 us
  waiting for transfers between devices: 15.4 us -> 28.7 us
  starting transfers between devices: 16.5 us -> 28.7 us
  local copies, waits for them, and re-layouts: 2.6 us -> 4.32 us
  Pallas kernels: 13 us -> 11.7 us
    all_to_all x3 -> x2, blocking collectives: 46 us -> 20.7 us  [exchange(): return lax.all_to_all(x, axis, split_axis=0, concat_axis=0, tiled=True)]
    all_to_all x2 -> x3, waiting for transfers between devices: 14.2 us -> 27.6 us  [exchange(): return lax.all_to_all(x, axis, split_axis=0, concat_axis=0, tiled=True)]
    all_to_all x2 -> x3, starting transfers between devices: 14.6 us -> 26.8 us  [exchange(): return lax.all_to_all(x, axis, split_axis=0, concat_axis=0, tiled=True)]
    pallas_call x1, Pallas kernels: 2.37 us -> 1.04 us  [split(): pl.pallas_call(split_kernel, out_shape=sds((8, 4, 64, 128), bf16), in_spe...]
    unnamed x20 -> x22, local copies, waits for them, and re-layouts: 1.72 us -> 2.76 us
  transfers between devices with their start and end apart: 3 -> 4, of which waited for: 3 -> 4; matrix products, arithmetic and copies ran while one was open for 1% -> 1% of each run, Pallas kernels for 8% -> 8%
where the time goes in v5:
time: 95.7 us; the launch traced here: 95.2 us
  starting transfers between devices  28.7 us (30%)
  waiting for transfers between devices  28.7 us (30%)
  blocking collectives  20.7 us (22%)
  Pallas kernels  11.7 us (12%)
  local copies, waits for them, and re-layouts  4.32 us (5%)
    all_to_all x3, waiting for transfers between devices, exchange(): return lax.all_to_all(x, axis, split_axis=0, concat_axis=0, tiled=True)  27.6 us
    all_to_all x3, starting transfers between devices, exchange(): return lax.all_to_all(x, axis, split_axis=0, concat_axis=0, tiled=True)  26.8 us
    all_to_all x2, blocking collectives, exchange(): return lax.all_to_all(x, axis, split_axis=0, concat_axis=0, tiled=True)  20.7 us
    pallas_call x8, Pallas kernels, call(): pl.pallas_call(kernel, out_shape=shapes, in_specs=ins, out_specs=vmem(len...  9.22 us
    unnamed x22, local copies, waits for them, and re-layouts  2.76 us
  transfers between devices with their start and end apart: 4, of which 4 were waited for; matrix products, arithmetic and copies ran while one was open for 1% of the time, Pallas kernels for 8%

profile of v5, /device:TPU:2, one launch (start us, length us, event | category | flops | bytes accessed | tf_op | source)
XLA Modules:
  0.0 95.2 jit_solution(3493772925431259648)
XLA Ops:
  0.6 0.0 copy-start.8
  0.6 0.0 copy-start.1
  0.7 1.0 %copy-done.1 = bf16[1,64,8,512]{3,2,1,0:T(8,128)(2,1)S(1)} copy-done((bf16[1,64,8,512]{3,2,1,0:T(8,128)(2,1)S(1)}, bf16[1,64,8,512]{3,2,1,0:T(8,128)(2,1)}, u32[]{:S(2)}) %copy-start.1) | copy-done | bytes 524312
  1.7 0.0 copy-start.6
  1.7 1.0 %shard_map.112 = bf16[8,4,64,128]{3,2,1,0:T(8,128)(2,1)} custom-call(bf16[512,512]{1,0:T(8,128)(2,1)S(1)} %bitcast.21), custom_call_target="tpu_custom_call" | custom-call | tf_op jit(solution)/shard_map/pallas_call | solution.py:88
  2.7 0.0 copy-start.7
  2.8 0.0 copy-start.5
  2.8 9.4 %all-to-all-start = ((bf16[8,256,128]{2,1,0:T(8,128)(2,1)}), bf16[8,256,128]{2,1,0:T(8,128)(2,1)S(1)}, u32[]{:S(2)}, u32[]{:S(2)}) async-start(bf16[8,256,128]{2,1,0:T(8,128)(2,1)} %bitcast.1), calls=%async_computation | async-start | bytes 1048576 | tf_op jit(solution)/shard_map/all_to_all | solution.py:243
  12.2 0.0 copy-done.8
  12.2 0.2 convert_reduce_fusion
  12.4 8.7 %all-to-all-done.parts_ref = bf16[8,256,128]{2,1,0:T(8,128)(2,1)S(1)} async-done(((bf16[8,256,128]{2,1,0:T(8,128)(2,1)}), bf16[8,256,128]{2,1,0:T(8,128)(2,1)S(1)}, u32[]{:S(2)}, u32[]{:S(2)}) %all-to-all-start) | async-done | bytes 524320 | tf_op jit(solution)/shard_map/all_to_all | solution.py:243
  21.1 0.2 shard_map.113.after_ref
  21.3 0.7 reshape.41
  22.1 12.1 %all-to-all-start.1 = ((bf16[64,2,768]{2,1,0:T(2,128)(2,1)}), bf16[64,2,768]{2,1,0:T(2,128)(2,1)S(1)}, u32[]{:S(2)}, u32[]{:S(2)}) async-start(bf16[64,2,768]{2,1,0:T(2,128)(2,1)} %reshape.41), calls=%async_computation.1 | async-start | bytes 393216 | tf_op jit(solution)/shard_map/all_to_all | solution.py:243
  34.2 0.0 copy-done.6
  34.2 0.1 copy.19
  34.3 0.0 copy-done.7
  34.4 0.1 copy.20
  34.5 0.0 copy-done.5
  34.5 0.0 copy-start
  34.5 1.4 %copy-done = bf16[3,512,512]{2,1,0:T(8,128)(2,1)S(1)} copy-done((bf16[3,512,512]{2,1,0:T(8,128)(2,1)S(1)}, bf16[3,512,512]{2,1,0:T(8,128)(2,1)}, u32[]{:S(2)}) %copy-start) | copy-done | bytes 1572888
  35.9 2.0 %shard_map.114 = (bf16[3,512,512]{2,1,0:T(8,128)(2,1)S(1)}, bf16[3,64,512]{2,1,0:T(8,128)(2,1)S(1)}) custom-call(s32[1]{0:T(128)} %bitcast.3.core_ref, bf16[3,512,512]{2,1,0:T(8,128)(2,1)S(1)} %copy-done, f32[512,3]{1,0:T(8,128)S(1)} %bitcast.18, bf16[3,64,512]{2,1,0:T(8,128)(2,1)S(1)} %copy-done.5, f32[64,3]{1,0:T(8,128)S(1)} %bitcast.22, ...), custom_call_target="tpu_custom_call" | custom-call | tf_op jit(solution)/shard_map/pallas_call | solution.py:47
  37.9 9.7 %all-to-all-done.1 = bf16[64,2,768]{2,1,0:T(2,128)(2,1)S(1)} async-done(((bf16[64,2,768]{2,1,0:T(2,128)(2,1)}), bf16[64,2,768]{2,1,0:T(2,128)(2,1)S(1)}, u32[]{:S(2)}, u32[]{:S(2)}) %all-to-all-start.1) | async-done | bytes 196640 | tf_op jit(solution)/shard_map/all_to_all | solution.py:243
  47.6 0.1 shard_map.115
  47.7 12.9 %all_to_all.25.own_ref = bf16[4,768,128]{2,1,0:T(8,128)(2,1)S(1)} all-to-all(bf16[4,768,128]{2,1,0:T(8,128)(2,1)S(1)} %shard_map.115), channel_id=1, replica_groups=mesh['fsdp'=64,'x'=4,'core'=2] {'x'}, dimensions={0} | all-to-all | bytes 1572864 | tf_op jit(solution)/shard_map/all_to_all | solution.py:243
  60.6 1.9 %collective-permute-start = (bf16[4,768,128]{2,1,0:T(8,128)(2,1)S(1)}, bf16[4,768,128]{2,1,0:T(8,128)(2,1)S(1)}, u32[]{:S(2)}, u32[]{:S(2)}) collective-permute-start(bf16[4,768,128]{2,1,0:T(8,128)(2,1)S(1)} %all_to_all.25.own_ref), channel_id=1, source_target_pairs={{0,1},{1,0},{2,3},{3,2},{4,5},{5,4},{6,7},{7,6},{8,9},{9,8},{10,11... | collective-permute-start | bytes 2359304 | tf_op jit(solution)/shard_map/ppermute | solution.py:278
  62.5 1.1 %shard_map.116 = (bf16[3,256,512]{2,1,0:T(8,128)(2,1)S(1)}, f32[3,256,128]{2,1,0:T(8,128)S(1)}, f32[8,128]{1,0:T(8,128)S(1)}) custom-call(bf16[4,768,128]{2,1,0:T(8,128)(2,1)S(1)} %all_to_all.25.own_ref, bf16[3,64,512]{2,1,0:T(8,128)(2,1)S(1)} %get-tuple-element.12.after_ref.rf_ref, bf16[3,512,512]{2,1,0:T(8,128)(2,1)S(1)} %get-tuple-element.13.left_ref), custom_call_target="tpu_custom_call" | custom-call | tf_op jit(solution)/shard_map/pallas_call | solution.py:47
  63.6 1.2 %collective-permute-done.other_ref = bf16[4,768,128]{2,1,0:T(8,128)(2,1)S(1)} collective-permute-done((bf16[4,768,128]{2,1,0:T(8,128)(2,1)S(1)}, bf16[4,768,128]{2,1,0:T(8,128)(2,1)S(1)}, u32[]{:S(2)}, u32[]{:S(2)}) %collective-permute-start) | collective-permute-done | bytes 786464 | tf_op jit(solution)/shard_map/ppermute | solution.py:278
  64.8 1.3 %shard_map.117 = (bf16[3,256,512]{2,1,0:T(8,128)(2,1)S(1)}, f32[64,1536]{1,0:T(8,128)S(1)}, f32[8,128]{1,0:T(8,128)S(1)}, f32[8,128]{1,0:T(8,128)S(1)}) custom-call(bf16[4,768,128]{2,1,0:T(8,128)(2,1)S(1)} %collective-permute-done.other_ref, bf16[3,64,512]{2,1,0:T(8,128)(2,1)S(1)} %get-tuple-element.12.after_ref.rf_ref, ...), custom_call_target="tpu_custom_call" | custom-call | tf_op jit(solution)/shard_map/pallas_call | solution.py:47
  66.0 0.0 copy-start.2
  66.0 7.8 %all_to_all.26 = f32[8,1,128]{2,1,0:T(1,128)S(1)} all-to-all(f32[8,1,128]{2,1,0:T(1,128)S(1)} %bitcast.24), channel_id=1, replica_groups=mesh['fsdp'=64,'x'=4,'core'=2] {'x','core'}, dimensions={0} | all-to-all | bytes 8192 | tf_op jit(solution)/shard_map/all_to_all | solution.py:243
  73.8 0.1 shard_map.118.after_ref
  74.0 0.0 copy-start.3
  74.0 0.7 reshape.45
  74.7 5.3 %all-to-all-start.4 = ((bf16[64,2,768]{2,1,0:T(2,128)(2,1)}), bf16[64,2,768]{2,1,0:T(2,128)(2,1)S(1)}, u32[]{:S(2)}, u32[]{:S(2)}) async-start(bf16[64,2,768]{2,1,0:T(2,128)(2,1)} %reshape.45), calls=%async_computation.4 | async-start | bytes 393216 | tf_op jit(solution)/shard_map/all_to_all | solution.py:243
  80.0 0.1 copy.22.slot_ref
  80.1 0.0 copy-done.2
  80.1 1.8 %shard_map.121 = f32[3,64,512]{2,1,0:T(8,128)} custom-call(s32[1]{0:T(128)} %bitcast.10.replica_ref, bf16[3,256,512]{2,1,0:T(8,128)(2,1)S(1)} %get-tuple-element.19.own_ref, bf16[3,256,512]{2,1,0:T(8,128)(2,1)S(1)} %get-tuple-element.20.other_ref, f32[3,64,512]{2,1,0:T(8,128)S(1)} %copy-done.2), custom_call_target="tpu_custom_call" | custom-call | tf_op jit(solution)/shard_map/pallas_call | solution.py:47
  81.9 0.0 copy-done.3
  82.0 0.0 copy-start.4
  82.0 2.6 %shard_map.120 = f32[3,64,512]{2,1,0:T(8,128)} custom-call(s32[1]{0:T(128)} %bitcast.10.replica_ref, s32[1]{0:T(128)} %bitcast.3.core_ref, bf16[3,256,512]{2,1,0:T(8,128)(2,1)S(1)} %get-tuple-element.19.own_ref, bf16[3,256,512]{2,1,0:T(8,128)(2,1)S(1)} %get-tuple-element.20.other_ref, f32[3,64,512]{2,1,0:T(8,128)S(1)} %copy-done.3, ...), custom_call_target="tpu_custom_call" | custom-call | tf_op jit(solution)/shard_map/pallas_call | solution.py:47
  84.5 9.2 %all-to-all-done.4 = bf16[64,2,768]{2,1,0:T(2,128)(2,1)S(1)} async-done(((bf16[64,2,768]{2,1,0:T(2,128)(2,1)}), bf16[64,2,768]{2,1,0:T(2,128)(2,1)S(1)}, u32[]{:S(2)}, u32[]{:S(2)}) %all-to-all-start.4) | async-done | bytes 196640 | tf_op jit(solution)/shard_map/all_to_all | solution.py:243
  93.7 0.0 copy-done.4
  93.8 1.4 %shard_map.119 = f32[64,8,64]{2,1,0:T(8,128)} custom-call(bf16[64,1536]{1,0:T(8,128)(2,1)S(1)} %bitcast.20, s32[64,1]{1,0:T(8,128)S(1)} %copy.22.slot_ref, f32[64,8,64]{2,1,0:T(8,128)S(1)} %copy-done.4), custom_call_target="tpu_custom_call" | custom-call | tf_op jit(solution)/shard_map/pallas_call | solution.py:310
  (3 shorter events, 0.1 us)
Async XLA Ops:
  0.6 11.6 %copy-start.8 = (s32[64]{0:T(128)S(1)}, s32[64]{0:T(128)}, u32[]{:S(2)}) copy-start(s32[64]{0:T(128)} %param.17) | copy-start | bytes 772
  0.6 1.0 %copy-start.1 = (bf16[1,64,8,512]{3,2,1,0:T(8,128)(2,1)S(1)}, bf16[1,64,8,512]{3,2,1,0:T(8,128)(2,1)}, u32[]{:S(2)}) copy-start(bf16[1,64,8,512]{3,2,1,0:T(8,128)(2,1)} %param.9) | copy-start | bytes 1572868
  1.7 32.5 %copy-start.6 = (f32[3,512]{1,0:T(4,128)S(1)}, f32[3,512]{1,0:T(4,128)}, u32[]{:S(2)}) copy-start(f32[3,512]{1,0:T(4,128)} %param.15) | copy-start | bytes 18436
  2.7 31.6 %copy-start.7 = (f32[3,64]{1,0:T(4,128)S(1)}, f32[3,64]{1,0:T(4,128)}, u32[]{:S(2)}) copy-start(f32[3,64]{1,0:T(4,128)} %param.16) | copy-start | bytes 2308
  2.8 31.7 %copy-start.5 = (bf16[3,64,512]{2,1,0:T(8,128)(2,1)S(1)}, bf16[3,64,512]{2,1,0:T(8,128)(2,1)}, u32[]{:S(2)}) copy-start(bf16[3,64,512]{2,1,0:T(8,128)(2,1)} %rc_ref.1) | copy-start | bytes 589828
  2.8 18.3 %all-to-all-start = ((bf16[8,256,128]{2,1,0:T(8,128)(2,1)}), bf16[8,256,128]{2,1,0:T(8,128)(2,1)S(1)}, u32[]{:S(2)}, u32[]{:S(2)}) async-start(bf16[8,256,128]{2,1,0:T(8,128)(2,1)} %bitcast.1), calls=%async_computation | async-start | bytes 1048576 | tf_op jit(solution)/shard_map/all_to_all | solution.py:243
  22.1 25.5 %all-to-all-start.1 = ((bf16[64,2,768]{2,1,0:T(2,128)(2,1)}), bf16[64,2,768]{2,1,0:T(2,128)(2,1)S(1)}, u32[]{:S(2)}, u32[]{:S(2)}) async-start(bf16[64,2,768]{2,1,0:T(2,128)(2,1)} %reshape.41), calls=%async_computation.1 | async-start | bytes 393216 | tf_op jit(solution)/shard_map/all_to_all | solution.py:243
  34.5 1.4 %copy-start = (bf16[3,512,512]{2,1,0:T(8,128)(2,1)S(1)}, bf16[3,512,512]{2,1,0:T(8,128)(2,1)}, u32[]{:S(2)}) copy-start(bf16[3,512,512]{2,1,0:T(8,128)(2,1)} %lc_ref.1) | copy-start | bytes 4718596
  60.6 4.2 %collective-permute-start = (bf16[4,768,128]{2,1,0:T(8,128)(2,1)S(1)}, bf16[4,768,128]{2,1,0:T(8,128)(2,1)S(1)}, u32[]{:S(2)}, u32[]{:S(2)}) collective-permute-start(bf16[4,768,128]{2,1,0:T(8,128)(2,1)S(1)} %all_to_all.25.own_ref), channel_id=1, source_target_pairs={{0,1},{1,0},{2,3},{3,2},{4,5},{5,4},{6,7},{7,6},{8,9},{9,8},{10,11... | collective-permute-start | bytes 2359304 | tf_op jit(solution)/shard_map/ppermute | solution.py:278
  66.0 14.1 %copy-start.2 = (f32[3,64,512]{2,1,0:T(8,128)S(1)}, f32[3,64,512]{2,1,0:T(8,128)}, u32[]{:S(2)}) copy-start(f32[3,64,512]{2,1,0:T(8,128)} %stat_ref.3) | copy-start | bytes 1179652
  74.0 8.0 %copy-start.3 = (f32[3,64,512]{2,1,0:T(8,128)S(1)}, f32[3,64,512]{2,1,0:T(8,128)}, u32[]{:S(2)}) copy-start(f32[3,64,512]{2,1,0:T(8,128)} %stat_ref.2) | copy-start | bytes 1179652
  74.7 19.0 %all-to-all-start.4 = ((bf16[64,2,768]{2,1,0:T(2,128)(2,1)}), bf16[64,2,768]{2,1,0:T(2,128)(2,1)S(1)}, u32[]{:S(2)}, u32[]{:S(2)}) async-start(bf16[64,2,768]{2,1,0:T(2,128)(2,1)} %reshape.45), calls=%async_computation.4 | async-start | bytes 393216 | tf_op jit(solution)/shard_map/all_to_all | solution.py:243
  82.0 11.8 %copy-start.4 = (f32[64,8,64]{2,1,0:T(8,128)S(1)}, f32[64,8,64]{2,1,0:T(8,128)}, u32[]{:S(2)}) copy-start(f32[64,8,64]{2,1,0:T(8,128)} %w_ref.1) | copy-start | bytes 393220

commit v6 on v4

--- a/solution.py
+++ b/solution.py
@@ -61,49 +61,40 @@
 CHUNKS = 4
 
 
-def split_kernel(x_ref, out_ref, x_buf, out_buf, in_sem, out_sem):
-    rows = x_buf.shape[1]
+def split_kernel(x_ref, out_ref, buf, sem):
+    rows = 512 // CHUNKS
     per = rows // 8
 
-    def arrival(i):
-        return pltpu.make_async_copy(x_ref.at[pl.ds(rows * i, rows)], x_buf.at[i], in_sem.at[i])
-
     def leaving(i):
-        target = out_ref.at[:, :, pl.ds(per * i, per)]
-        return pltpu.make_async_copy(out_buf.at[i], target, out_sem.at[i])
-
-    for i in range(CHUNKS):
-        arrival(i).start()
+        return pltpu.make_async_copy(buf.at[i], out_ref.at[:, :, pl.ds(per * i, per)], sem.at[i])
+
     order = iota((rows, rows), 0)
     half, r, block = order // (4 * per), (order // per) % 4, order % per
     perm = onehot(8 * block + 4 * half + r == iota((rows, rows), 1))
     for i in range(CHUNKS):
-        arrival(i).wait()
-        moved = dot(perm, x_buf[i]).astype(bf16)
+        moved = dot(perm, x_ref[rows * i : rows * i + rows]).astype(bf16)
         for x in range(4):
             for c in range(2):
                 for r in range(4):
                     at = (4 * c + r) * per
                     piece = moved[at : at + per, LANES * x : LANES * x + LANES]
-                    out_buf[i, 2 * x + c, r] = piece
+                    buf[i, 2 * x + c, r] = piece
         leaving(i).start()
     for i in range(CHUNKS):
         leaving(i).wait()
 
 
 def split(x):
-    rows = 512 // CHUNKS
     return pl.pallas_call(
         split_kernel,
         out_shape=sds((8, 4, 64, 128), bf16),
-        in_specs=[ANY],
+        in_specs=vmem(1),
         out_specs=ANY,
         scratch_shapes=[
-            pltpu.VMEM((CHUNKS, rows, 512), bf16),
-            pltpu.VMEM((CHUNKS, 8, 4, rows // 8, 128), bf16),
-            pltpu.SemaphoreType.DMA((CHUNKS,)),
+            pltpu.VMEM((CHUNKS, 8, 4, 64 // CHUNKS, 128), bf16),
             pltpu.SemaphoreType.DMA((CHUNKS,)),
         ],
+        compiler_params=pltpu.CompilerParams(vmem_limit_bytes=VMEM_GRANT),
     )(x)
 
 
@@ -129,7 +120,9 @@
         rf_ref[k] = (rc_ref[k].astype(f32) * rs_ref[:, k : k + 1]).astype(bf16)
 
 
-def spread_kernel(piece_ref, out_ref):
+def spread_kernel(piece_ref, f0_ref, f1_ref, f2_ref, f3_ref, out_ref, near_ref):
+    for x, ref in enumerate((f0_ref, f1_ref, f2_ref, f3_ref)):
+        near_ref[x] = ref[...]
     for q in range(4):
         for kr in range(12):
             tile = piece_ref[16 * q : 16 * q + 16, LANES * kr : LANES * kr + LANES]
@@ -138,58 +131,54 @@
                 out_ref[x, at : at + 16] = tile
 
 
-def half_products(at, src_ref, rf_ref, left_ref, g_ref):
+def gather_half(k, src_ref, g_ref):
+    for x in range(4):
+        for q in range(4):
+            for r in range(4):
+                row = 64 * r + 16 * q
+                g_ref[k, row : row + 16, LANES * x : LANES * x + LANES] = src_ref[
+                    x, pl.ds(192 * q + 16 * (4 * k + r), 16)
+                ]
+
+
+def times_factor(g, factor_ref, k):
+    factor = jnp.concatenate([factor_ref[x, k] for x in range(4)], axis=0)
+    return dot(g, factor, 1, 1).astype(bf16)
+
+
+def own_kernel(own_ref, near_ref, g_ref, m_ref, gs_ref):
     lane = iota((8, LANES), 1)
     grad_squares = jnp.zeros((8, LANES), f32)
-    products = []
-    for k in range(3):
-        for x in range(4):
-            for q in range(4):
-                for r in range(4):
-                    row = 64 * r + 16 * q
-                    g_ref[k, row : row + 16, LANES * x : LANES * x + LANES] = src_ref[
-                        x, pl.ds(192 * q + 16 * (4 * k + r), 16)
-                    ]
+    for k in range(3):
+        gather_half(k, own_ref, g_ref)
         g = g_ref[k]
-        rf = rf_ref[k]
-        wide = jnp.concatenate([rf, jnp.zeros((128, 512), bf16), rf], axis=0)
-        mixed = dot(g, wide, 1, 1).astype(bf16)
-        pre = dot(left_ref[k, :256, at : at + 256], mixed[:, :128])
-        products.append(pre + dot(left_ref[k, 256:, at : at + 256], mixed[:, 128:]))
+        m_ref[k] = times_factor(g, near_ref, k)
         gf = g.astype(f32)
         grad_squares = jnp.where(lane == k, jnp.sum(gf * gf), grad_squares)
-    return products, grad_squares
-
-
-def own_kernel(own_ref, rf_ref, left_ref, g_ref, p_ref, gs_ref):
-    products, grad_squares = half_products(0, own_ref, rf_ref, left_ref, g_ref)
-    for k in range(3):
-        p_ref[k] = products[k]
     gs_ref[...] = grad_squares
 
 
 def other_kernel(
-    other_ref, rf_ref, left_ref, own_p_ref, own_gs_ref, g_ref, p_ref, sq_ref, gs_ref
+    other_ref, near_ref, far_ref, left_ref, own_g_ref, own_m_ref, own_gs_ref, g_ref, out_ref
 ):
-    products, grad_squares = half_products(256, other_ref, rf_ref, left_ref, g_ref)
-    lane = iota((8, LANES), 1)
-    squares = jnp.zeros((8, LANES), f32)
-    for k in range(3):
-        pre = own_p_ref[k] + products[k]
+    low = iota((256, LANES), 1) < 64
+    for k in range(3):
+        gather_half(k, other_ref, g_ref)
+        g = g_ref[k]
+        gf = g.astype(f32)
+        squares = own_gs_ref[0:1, k : k + 1] + jnp.sum(gf * gf)
+        mixed = jnp.concatenate([own_m_ref[k], times_factor(g, near_ref, k)], axis=0)
+        pre = dot(left_ref[k], mixed)
+        total = jnp.sum(pre * pre)
+        mine = jnp.where(low, pre[:256, :128], pltpu.roll(pre[256:, :128], 64, 1))
+        whole = jnp.concatenate([own_g_ref[k], g], axis=0)
+        pre = dot(left_ref[k], times_factor(whole, far_ref, k))
+        total = total + jnp.sum(pre * pre)
+        ratio = step_size * jnp.sqrt(squares) * lax.rsqrt(jnp.full((1, 1), total) + epsilon)
+        mine = (mine * ratio).astype(bf16)
         for t in range(4):
             at = 512 * k + LANES * t
-            p_ref[:, at : at + LANES] = pre[64 * t : 64 * t + 64]
-        squares = jnp.where(lane == k, jnp.sum(pre * pre), squares)
-    sq_ref[...] = squares
-    gs_ref[...] = own_gs_ref[...] + grad_squares
-
-
-def scale_kernel(sq_ref, gs_ref, p_ref, out_ref):
-    total = jnp.sum(sq_ref[...], axis=0, keepdims=True)
-    ratio = step_size * jnp.sqrt(gs_ref[0:1, :]) * lax.rsqrt(total + epsilon)
-    for k in range(3):
-        span = slice(512 * k, 512 * k + 512)
-        out_ref[:, span] = (p_ref[:, span] * ratio[:, k : k + 1]).astype(bf16)
+            out_ref[:, at : at + LANES] = mine[64 * t : 64 * t + 64]
 
 
 def right_kernel(replica_ref, own_ref, other_ref, stat_ref, out_ref):
@@ -282,32 +271,39 @@
         sds((64, 1536), bf16),
         (parts, slot_of.reshape(1, 64), left),
     )
+    swap = [(0, 1), (1, 0)]
     arrived = exchange(routed.reshape(64, 2, 768), "fsdp").reshape(64, 1536)
-    own = exchange(call(spread_kernel, vmem(1), sds((4, 768, 128), bf16), (arrived,)), "x")
-    other = lax.ppermute(own, "core", [(0, 1), (1, 0)])
+    shared = [right_factor]
+    for step in (2, 1, 3):
+        ring = [(x, (x + step) % 4) for x in range(4)]
+        shared.append(lax.ppermute(right_factor, "x", ring))
+    spread, near = call(
+        spread_kernel,
+        vmem(5),
+        [sds((4, 768, 128), bf16), sds((4, 3, 64, 512), bf16)],
+        (arrived, *shared),
+    )
+    own, near = lax.optimization_barrier((exchange(spread, "x"), near))
+    far = lax.ppermute(near, "core", swap)
+    other = lax.ppermute(own, "core", swap)
     half_grad = sds((3, 256, 512), bf16)
-    small = sds((8, 128), f32)
-    own_grad, own_pre, own_squares = call(
+    own_grad, own_mixed, own_squares = call(
         own_kernel,
-        vmem(3),
-        [half_grad, sds((3, 256, 128), f32), small],
-        (own, right_factor, left),
-    )
-    other_grad, pre, squares, grad_squares = call(
+        vmem(2),
+        [half_grad, sds((3, 256, 256), bf16), sds((8, 128), f32)],
+        (own, near),
+    )
+    other_grad, scaled = call(
         other_kernel,
-        vmem(5),
-        [half_grad, sds((64, 1536), f32), small, small],
-        (other, right_factor, left, own_pre, own_squares),
-    )
-    all_squares = exchange(squares.reshape(8, 1, 128), ("x", "core")).reshape(8, 128)
+        vmem(7),
+        [half_grad, sds((64, 1536), bf16)],
+        (other, near, far, left, own_grad, own_mixed, own_squares),
+    )
     right_new = call(
         right_kernel,
         [SMEM, *vmem(3)],
         sds((3, 64, 512), f32),
         (replica, own_grad, other_grad, right_stat),
-    )
-    scaled = call(
-        scale_kernel, vmem(3), sds((64, 1536), bf16), (all_squares, grad_squares, pre)
     )
     returned = exchange(scaled.reshape(64, 2, 768), "fsdp").reshape(64, 1536)
     left_new = call(

time: 94.9 us -> 101 us (1.064)
  the two profiles are of different devices: /device:TPU:2 before, /device:TPU:1 now
where the time goes in v6:
time: 101 us; the launch traced here: 100 us
  starting transfers between devices  50.1 us (50%)
  waiting for transfers between devices  19.2 us (19%)
  blocking collectives  12.4 us (12%)
  Pallas kernels  12.2 us (12%)
  local copies, waits for them, and re-layouts  5.29 us (5%)
    all_to_all x3, starting transfers between devices, exchange(): return lax.all_to_all(x, axis, split_axis=0, concat_axis=0, tiled=True)  34.1 us
    all_to_all x3, waiting for transfers between devices, exchange(): return lax.all_to_all(x, axis, split_axis=0, concat_axis=0, tiled=True)  15.2 us
    all_to_all x1, blocking collectives, exchange(): return lax.all_to_all(x, axis, split_axis=0, concat_axis=0, tiled=True)  12.4 us
    pallas_call x7, Pallas kernels, call(): pl.pallas_call(kernel, out_shape=shapes, in_specs=ins, out_specs=vmem(len...  9.74 us
    ppermute x3, starting transfers between devices, local(): shared.append(lax.ppermute(right_factor, 'x', ring))  8.9 us
    ppermute x1, starting transfers between devices, local(): far = lax.ppermute(near, 'core', swap)  5.16 us
    unnamed x22, local copies, waits for them, and re-layouts  3.74 us
    ppermute x3, waiting for transfers between devices, local(): shared.append(lax.ppermute(right_factor, 'x', ring))  2.17 us
  transfers between devices with their start and end apart: 8, of which 5 were waited for; matrix products, arithmetic and copies ran while one was open for 1% of the time, Pallas kernels for 7%

profile of v6, /device:TPU:1, one launch (start us, length us, event | category | flops | bytes accessed | tf_op | source)
XLA Modules:
  0.0 100.1 jit_solution(10561394365106574517)
XLA Ops:
  0.6 0.0 copy-start.1
  0.6 1.0 %copy-done.1 = bf16[1,64,8,512]{3,2,1,0:T(8,128)(2,1)S(1)} copy-done((bf16[1,64,8,512]{3,2,1,0:T(8,128)(2,1)S(1)}, bf16[1,64,8,512]{3,2,1,0:T(8,128)(2,1)}, u32[]{:S(2)}) %copy-start.1) | copy-done | bytes 524312
  1.7 0.0 copy-start.6
  1.7 0.0 copy-start.7
  1.7 0.0 copy-start.5
  1.7 1.0 %shard_map.112 = bf16[8,4,64,128]{3,2,1,0:T(8,128)(2,1)} custom-call(bf16[512,512]{1,0:T(8,128)(2,1)S(1)} %bitcast.17), custom_call_target="tpu_custom_call" | custom-call | tf_op jit(solution)/shard_map/pallas_call | solution.py:88
  2.7 0.0 copy-start.8
  2.7 10.2 %all-to-all-start = ((bf16[8,256,128]{2,1,0:T(8,128)(2,1)}), bf16[8,256,128]{2,1,0:T(8,128)(2,1)S(1)}, u32[]{:S(2)}, u32[]{:S(2)}) async-start(bf16[8,256,128]{2,1,0:T(8,128)(2,1)} %bitcast.1), calls=%async_computation | async-start | bytes 1048576 | tf_op jit(solution)/shard_map/all_to_all | solution.py:241
  13.0 0.0 copy-done.6
  13.0 0.1 copy.15
  13.1 0.0 copy-done.7
  13.1 0.1 copy.16
  13.2 0.0 copy-done.5
  13.2 0.0 copy-start
  13.2 1.4 %copy-done = bf16[3,512,512]{2,1,0:T(8,128)(2,1)S(1)} copy-done((bf16[3,512,512]{2,1,0:T(8,128)(2,1)S(1)}, bf16[3,512,512]{2,1,0:T(8,128)(2,1)}, u32[]{:S(2)}) %copy-start) | copy-done | bytes 1572888
  14.6 2.0 %shard_map.113 = (bf16[3,512,512]{2,1,0:T(8,128)(2,1)S(1)}, bf16[3,64,512]{2,1,0:T(8,128)(2,1)S(1)}) custom-call(s32[1]{0:T(128)} %bitcast.3.core_ref, bf16[3,512,512]{2,1,0:T(8,128)(2,1)S(1)} %copy-done, f32[512,3]{1,0:T(8,128)S(1)} %bitcast.14, bf16[3,64,512]{2,1,0:T(8,128)(2,1)S(1)} %copy-done.5, f32[64,3]{1,0:T(8,128)S(1)} %bitcast.18), custom_call_target="tpu_custom_call" | custom-call | tf_op jit(solution)/shard_map/pallas_call | solution.py:47
  16.6 0.0 copy-done.8
  16.6 0.2 convert_reduce_fusion
  16.8 5.5 %all-to-all-done.parts_ref = bf16[8,256,128]{2,1,0:T(8,128)(2,1)S(1)} async-done(((bf16[8,256,128]{2,1,0:T(8,128)(2,1)}), bf16[8,256,128]{2,1,0:T(8,128)(2,1)S(1)}, u32[]{:S(2)}, u32[]{:S(2)}) %all-to-all-start) | async-done | bytes 524320 | tf_op jit(solution)/shard_map/all_to_all | solution.py:241
  22.3 0.2 shard_map.114
  22.6 0.7 reshape.35
  23.3 11.8 %all-to-all-start.1 = ((bf16[64,2,768]{2,1,0:T(2,128)(2,1)}), bf16[64,2,768]{2,1,0:T(2,128)(2,1)S(1)}, u32[]{:S(2)}, u32[]{:S(2)}) async-start(bf16[64,2,768]{2,1,0:T(2,128)(2,1)} %reshape.35), calls=%async_computation.1 | async-start | bytes 393216 | tf_op jit(solution)/shard_map/all_to_all | solution.py:241
  35.2 2.4 %collective-permute-start = (bf16[3,64,512]{2,1,0:T(8,128)(2,1)S(1)}, bf16[3,64,512]{2,1,0:T(8,128)(2,1)S(1)}, u32[]{:S(2)}, u32[]{:S(2)}) collective-permute-start(bf16[3,64,512]{2,1,0:T(8,128)(2,1)S(1)} %get-tuple-element.15.f0_ref), channel_id=1, source_target_pairs={{0,4},{2,6},{4,0},{6,2},{1,5},{3,7},{5,1},{7,3},{8,12},{10,14},{12... | collective-permute-start | bytes 589832 | tf_op jit(solution)/shard_map/ppermute | solution.py:279
  37.6 2.9 %collective-permute-start.1 = (bf16[3,64,512]{2,1,0:T(8,128)(2,1)S(1)}, bf16[3,64,512]{2,1,0:T(8,128)(2,1)S(1)}, u32[]{:S(2)}, u32[]{:S(2)}) collective-permute-start(bf16[3,64,512]{2,1,0:T(8,128)(2,1)S(1)} %get-tuple-element.15.f0_ref), channel_id=1, source_target_pairs={{0,2},{2,4},{4,6},{6,0},{1,3},{3,5},{5,7},{7,1},{8,10},{10,12},{12... | collective-permute-start | bytes 589832 | tf_op jit(solution)/shard_map/ppermute | solution.py:279
  40.5 3.6 %collective-permute-start.2 = (bf16[3,64,512]{2,1,0:T(8,128)(2,1)S(1)}, bf16[3,64,512]{2,1,0:T(8,128)(2,1)S(1)}, u32[]{:S(2)}, u32[]{:S(2)}) collective-permute-start(bf16[3,64,512]{2,1,0:T(8,128)(2,1)S(1)} %get-tuple-element.15.f0_ref), channel_id=1, source_target_pairs={{0,6},{2,0},{4,2},{6,4},{1,7},{3,1},{5,3},{7,5},{8,14},{10,8},{12,... | collective-permute-start | bytes 589832 | tf_op jit(solution)/shard_map/ppermute | solution.py:279
  44.1 2.9 %all-to-all-done.1 = bf16[64,2,768]{2,1,0:T(2,128)(2,1)S(1)} async-done(((bf16[64,2,768]{2,1,0:T(2,128)(2,1)}), bf16[64,2,768]{2,1,0:T(2,128)(2,1)S(1)}, u32[]{:S(2)}, u32[]{:S(2)}) %all-to-all-start.1) | async-done | bytes 196640 | tf_op jit(solution)/shard_map/all_to_all | solution.py:241
  47.1 0.0 collective-permute-done.f1_ref
  47.1 2.2 %collective-permute-done.1.f2_ref = bf16[3,64,512]{2,1,0:T(8,128)(2,1)S(1)} collective-permute-done((bf16[3,64,512]{2,1,0:T(8,128)(2,1)S(1)}, bf16[3,64,512]{2,1,0:T(8,128)(2,1)S(1)}, u32[]{:S(2)}, u32[]{:S(2)}) %collective-permute-start.1) | collective-permute-done | bytes 196640 | tf_op jit(solution)/shard_map/ppermute | solution.py:279
  49.2 0.0 collective-permute-done.2.f3_ref
  49.3 0.2 shard_map.115
  49.4 12.4 %all_to_all.20.own_ref = bf16[4,768,128]{2,1,0:T(8,128)(2,1)S(1)} all-to-all(bf16[4,768,128]{2,1,0:T(8,128)(2,1)S(1)} %get-tuple-element.16), channel_id=1, replica_groups=mesh['fsdp'=64,'x'=4,'core'=2] {'x'}, dimensions={0} | all-to-all | bytes 1572864 | tf_op jit(solution)/shard_map/all_to_all | solution.py:241
  61.8 5.2 %collective-permute-start.4 = (bf16[4,3,64,512]{3,2,1,0:T(8,128)(2,1)S(1)}, bf16[4,3,64,512]{3,2,1,0:T(8,128)(2,1)S(1)}, u32[]{:S(2)}, u32[]{:S(2)}) collective-permute-start(bf16[4,3,64,512]{3,2,1,0:T(8,128)(2,1)S(1)} %get-tuple-element.19.near_ref), channel_id=1, source_target_pairs={{0,1},{1,0},{2,3},{3,2},{4,5},{5,4},{6,7},{7,6},{8,9},{9,8},{10,11... | collective-permute-start | bytes 2359304 | tf_op jit(solution)/shard_map/ppermute | solution.py:287
  67.0 1.9 %collective-permute-start.3 = (bf16[4,768,128]{2,1,0:T(8,128)(2,1)S(1)}, bf16[4,768,128]{2,1,0:T(8,128)(2,1)S(1)}, u32[]{:S(2)}, u32[]{:S(2)}) collective-permute-start(bf16[4,768,128]{2,1,0:T(8,128)(2,1)S(1)} %all_to_all.20.own_ref), channel_id=1, source_target_pairs={{0,1},{1,0},{2,3},{3,2},{4,5},{5,4},{6,7},{7,6},{8,9},{9,8},{10,11... | collective-permute-start | bytes 2359304 | tf_op jit(solution)/shard_map/ppermute | solution.py:288
  68.9 0.5 shard_map.116
  69.4 0.0 collective-permute-done.4.far_ref
  69.4 1.8 %collective-permute-done.3.other_ref = bf16[4,768,128]{2,1,0:T(8,128)(2,1)S(1)} collective-permute-done((bf16[4,768,128]{2,1,0:T(8,128)(2,1)S(1)}, bf16[4,768,128]{2,1,0:T(8,128)(2,1)S(1)}, u32[]{:S(2)}, u32[]{:S(2)}) %collective-permute-start.3) | collective-permute-done | bytes 786464 | tf_op jit(solution)/shard_map/ppermute | solution.py:288
  71.1 2.5 %shard_map.117 = (bf16[3,256,512]{2,1,0:T(8,128)(2,1)S(1)}, bf16[64,1536]{1,0:T(8,128)(2,1)S(1)}) custom-call(bf16[4,768,128]{2,1,0:T(8,128)(2,1)S(1)} %collective-permute-done.3.other_ref, bf16[4,3,64,512]{3,2,1,0:T(8,128)(2,1)S(1)} %get-tuple-element.19.near_ref, bf16[4,3,64,512]{3,2,1,0:T(8,128)(2,1)S(1)} %collective-permute-done.4.far_ref, ...), custom_call_target="tpu_custom_call" | custom-call | tf_op jit(solution)/shard_map/pallas_call | solution.py:47
  73.6 0.0 copy-start.3
  73.6 0.7 reshape.37
  74.4 12.0 %all-to-all-start.3 = ((bf16[64,2,768]{2,1,0:T(2,128)(2,1)}), bf16[64,2,768]{2,1,0:T(2,128)(2,1)S(1)}, u32[]{:S(2)}, u32[]{:S(2)}) async-start(bf16[64,2,768]{2,1,0:T(2,128)(2,1)} %reshape.37), calls=%async_computation.3 | async-start | bytes 393216 | tf_op jit(solution)/shard_map/all_to_all | solution.py:241
  86.4 0.1 copy.17.slot_ref
  86.5 0.0 copy-start.2
  86.5 1.0 copy-done.2
  87.5 1.8 %shard_map.120 = f32[3,64,512]{2,1,0:T(8,128)} custom-call(s32[1]{0:T(128)} %bitcast.7.replica_ref, bf16[3,256,512]{2,1,0:T(8,128)(2,1)S(1)} %get-tuple-element.20.own_g_ref.own_ref, bf16[3,256,512]{2,1,0:T(8,128)(2,1)S(1)} %get-tuple-element.24.other_ref, f32[3,64,512]{2,1,0:T(8,128)S(1)} %copy-done.2), custom_call_target="tpu_custom_call" | custom-call | tf_op jit(solution)/shard_map/pallas_call | solution.py:47
  89.3 0.0 copy-done.3
  89.3 0.0 copy-start.4
  89.3 2.6 %shard_map.119 = f32[3,64,512]{2,1,0:T(8,128)} custom-call(s32[1]{0:T(128)} %bitcast.7.replica_ref, s32[1]{0:T(128)} %bitcast.3.core_ref, bf16[3,256,512]{2,1,0:T(8,128)(2,1)S(1)} %get-tuple-element.20.own_g_ref.own_ref, bf16[3,256,512]{2,1,0:T(8,128)(2,1)S(1)} %get-tuple-element.24.other_ref, f32[3,64,512]{2,1,0:T(8,128)S(1)} %copy-done.3, ...), custom_call_target="tpu_custom_call" | custom-call | tf_op jit(solution)/shard_map/pallas_call | solution.py:47
  91.9 6.8 %all-to-all-done.3 = bf16[64,2,768]{2,1,0:T(2,128)(2,1)S(1)} async-done(((bf16[64,2,768]{2,1,0:T(2,128)(2,1)}), bf16[64,2,768]{2,1,0:T(2,128)(2,1)S(1)}, u32[]{:S(2)}, u32[]{:S(2)}) %all-to-all-start.3) | async-done | bytes 196640 | tf_op jit(solution)/shard_map/all_to_all | solution.py:241
  98.7 0.0 copy-done.4
  98.7 1.4 %shard_map.118 = f32[64,8,64]{2,1,0:T(8,128)} custom-call(bf16[64,1536]{1,0:T(8,128)(2,1)S(1)} %bitcast.15, s32[64,1]{1,0:T(8,128)S(1)} %copy.17.slot_ref, f32[64,8,64]{2,1,0:T(8,128)S(1)} %copy-done.4), custom_call_target="tpu_custom_call" | custom-call | tf_op jit(solution)/shard_map/pallas_call | solution.py:315
  (3 shorter events, 0.1 us)
Async XLA Ops:
  0.6 1.0 %copy-start.1 = (bf16[1,64,8,512]{3,2,1,0:T(8,128)(2,1)S(1)}, bf16[1,64,8,512]{3,2,1,0:T(8,128)(2,1)}, u32[]{:S(2)}) copy-start(bf16[1,64,8,512]{3,2,1,0:T(8,128)(2,1)} %param.9) | copy-start | bytes 1572868
  1.7 11.3 %copy-start.6 = (f32[3,512]{1,0:T(4,128)S(1)}, f32[3,512]{1,0:T(4,128)}, u32[]{:S(2)}) copy-start(f32[3,512]{1,0:T(4,128)} %param.15) | copy-start | bytes 18436
  1.7 11.4 %copy-start.7 = (f32[3,64]{1,0:T(4,128)S(1)}, f32[3,64]{1,0:T(4,128)}, u32[]{:S(2)}) copy-start(f32[3,64]{1,0:T(4,128)} %param.16) | copy-start | bytes 2308
  1.7 11.6 %copy-start.5 = (bf16[3,64,512]{2,1,0:T(8,128)(2,1)S(1)}, bf16[3,64,512]{2,1,0:T(8,128)(2,1)}, u32[]{:S(2)}) copy-start(bf16[3,64,512]{2,1,0:T(8,128)(2,1)} %rc_ref.1) | copy-start | bytes 589828
  2.7 13.9 %copy-start.8 = (s32[64]{0:T(128)S(1)}, s32[64]{0:T(128)}, u32[]{:S(2)}) copy-start(s32[64]{0:T(128)} %param.17) | copy-start | bytes 772
  2.7 19.6 %all-to-all-start = ((bf16[8,256,128]{2,1,0:T(8,128)(2,1)}), bf16[8,256,128]{2,1,0:T(8,128)(2,1)S(1)}, u32[]{:S(2)}, u32[]{:S(2)}) async-start(bf16[8,256,128]{2,1,0:T(8,128)(2,1)} %bitcast.1), calls=%async_computation | async-start | bytes 1048576 | tf_op jit(solution)/shard_map/all_to_all | solution.py:241
  13.2 1.4 %copy-start = (bf16[3,512,512]{2,1,0:T(8,128)(2,1)S(1)}, bf16[3,512,512]{2,1,0:T(8,128)(2,1)}, u32[]{:S(2)}) copy-start(bf16[3,512,512]{2,1,0:T(8,128)(2,1)} %lc_ref.1) | copy-start | bytes 4718596
  23.3 23.7 %all-to-all-start.1 = ((bf16[64,2,768]{2,1,0:T(2,128)(2,1)}), bf16[64,2,768]{2,1,0:T(2,128)(2,1)S(1)}, u32[]{:S(2)}, u32[]{:S(2)}) async-start(bf16[64,2,768]{2,1,0:T(2,128)(2,1)} %reshape.35), calls=%async_computation.1 | async-start | bytes 393216 | tf_op jit(solution)/shard_map/all_to_all | solution.py:241
  35.2 11.9 %collective-permute-start = (bf16[3,64,512]{2,1,0:T(8,128)(2,1)S(1)}, bf16[3,64,512]{2,1,0:T(8,128)(2,1)S(1)}, u32[]{:S(2)}, u32[]{:S(2)}) collective-permute-start(bf16[3,64,512]{2,1,0:T(8,128)(2,1)S(1)} %get-tuple-element.15.f0_ref), channel_id=1, source_target_pairs={{0,4},{2,6},{4,0},{6,2},{1,5},{3,7},{5,1},{7,3},{8,12},{10,14},{12... | collective-permute-start | bytes 589832 | tf_op jit(solution)/shard_map/ppermute | solution.py:279
  37.6 11.7 %collective-permute-start.1 = (bf16[3,64,512]{2,1,0:T(8,128)(2,1)S(1)}, bf16[3,64,512]{2,1,0:T(8,128)(2,1)S(1)}, u32[]{:S(2)}, u32[]{:S(2)}) collective-permute-start(bf16[3,64,512]{2,1,0:T(8,128)(2,1)S(1)} %get-tuple-element.15.f0_ref), channel_id=1, source_target_pairs={{0,2},{2,4},{4,6},{6,0},{1,3},{3,5},{5,7},{7,1},{8,10},{10,12},{12... | collective-permute-start | bytes 589832 | tf_op jit(solution)/shard_map/ppermute | solution.py:279
  40.5 8.8 %collective-permute-start.2 = (bf16[3,64,512]{2,1,0:T(8,128)(2,1)S(1)}, bf16[3,64,512]{2,1,0:T(8,128)(2,1)S(1)}, u32[]{:S(2)}, u32[]{:S(2)}) collective-permute-start(bf16[3,64,512]{2,1,0:T(8,128)(2,1)S(1)} %get-tuple-element.15.f0_ref), channel_id=1, source_target_pairs={{0,6},{2,0},{4,2},{6,4},{1,7},{3,1},{5,3},{7,5},{8,14},{10,8},{12,... | collective-permute-start | bytes 589832 | tf_op jit(solution)/shard_map/ppermute | solution.py:279
  61.8 7.6 %collective-permute-start.4 = (bf16[4,3,64,512]{3,2,1,0:T(8,128)(2,1)S(1)}, bf16[4,3,64,512]{3,2,1,0:T(8,128)(2,1)S(1)}, u32[]{:S(2)}, u32[]{:S(2)}) collective-permute-start(bf16[4,3,64,512]{3,2,1,0:T(8,128)(2,1)S(1)} %get-tuple-element.19.near_ref), channel_id=1, source_target_pairs={{0,1},{1,0},{2,3},{3,2},{4,5},{5,4},{6,7},{7,6},{8,9},{9,8},{10,11... | collective-permute-start | bytes 2359304 | tf_op jit(solution)/shard_map/ppermute | solution.py:287
  67.0 4.2 %collective-permute-start.3 = (bf16[4,768,128]{2,1,0:T(8,128)(2,1)S(1)}, bf16[4,768,128]{2,1,0:T(8,128)(2,1)S(1)}, u32[]{:S(2)}, u32[]{:S(2)}) collective-permute-start(bf16[4,768,128]{2,1,0:T(8,128)(2,1)S(1)} %all_to_all.20.own_ref), channel_id=1, source_target_pairs={{0,1},{1,0},{2,3},{3,2},{4,5},{5,4},{6,7},{7,6},{8,9},{9,8},{10,11... | collective-permute-start | bytes 2359304 | tf_op jit(solution)/shard_map/ppermute | solution.py:288
  73.6 15.7 %copy-start.3 = (f32[3,64,512]{2,1,0:T(8,128)S(1)}, f32[3,64,512]{2,1,0:T(8,128)}, u32[]{:S(2)}) copy-start(f32[3,64,512]{2,1,0:T(8,128)} %stat_ref.2) | copy-start | bytes 1179652
  74.4 24.3 %all-to-all-start.3 = ((bf16[64,2,768]{2,1,0:T(2,128)(2,1)}), bf16[64,2,768]{2,1,0:T(2,128)(2,1)S(1)}, u32[]{:S(2)}, u32[]{:S(2)}) async-start(bf16[64,2,768]{2,1,0:T(2,128)(2,1)} %reshape.37), calls=%async_computation.3 | async-start | bytes 393216 | tf_op jit(solution)/shard_map/all_to_all | solution.py:241
  86.5 1.0 copy-start.2
  89.3 9.4 %copy-start.4 = (f32[64,8,64]{2,1,0:T(8,128)S(1)}, f32[64,8,64]{2,1,0:T(8,128)}, u32[]{:S(2)}) copy-start(f32[64,8,64]{2,1,0:T(8,128)} %w_ref.1) | copy-start | bytes 393220

commit v7 on v4

--- a/solution.py
+++ b/solution.py
@@ -61,49 +61,40 @@
 CHUNKS = 4
 
 
-def split_kernel(x_ref, out_ref, x_buf, out_buf, in_sem, out_sem):
-    rows = x_buf.shape[1]
+def split_kernel(x_ref, out_ref, buf, sem):
+    rows = 512 // CHUNKS
     per = rows // 8
 
-    def arrival(i):
-        return pltpu.make_async_copy(x_ref.at[pl.ds(rows * i, rows)], x_buf.at[i], in_sem.at[i])
-
     def leaving(i):
-        target = out_ref.at[:, :, pl.ds(per * i, per)]
-        return pltpu.make_async_copy(out_buf.at[i], target, out_sem.at[i])
-
-    for i in range(CHUNKS):
-        arrival(i).start()
+        return pltpu.make_async_copy(buf.at[i], out_ref.at[:, :, pl.ds(per * i, per)], sem.at[i])
+
     order = iota((rows, rows), 0)
     half, r, block = order // (4 * per), (order // per) % 4, order % per
     perm = onehot(8 * block + 4 * half + r == iota((rows, rows), 1))
     for i in range(CHUNKS):
-        arrival(i).wait()
-        moved = dot(perm, x_buf[i]).astype(bf16)
+        moved = dot(perm, x_ref[rows * i : rows * i + rows]).astype(bf16)
         for x in range(4):
             for c in range(2):
                 for r in range(4):
                     at = (4 * c + r) * per
                     piece = moved[at : at + per, LANES * x : LANES * x + LANES]
-                    out_buf[i, 2 * x + c, r] = piece
+                    buf[i, 2 * x + c, r] = piece
         leaving(i).start()
     for i in range(CHUNKS):
         leaving(i).wait()
 
 
 def split(x):
-    rows = 512 // CHUNKS
     return pl.pallas_call(
         split_kernel,
         out_shape=sds((8, 4, 64, 128), bf16),
-        in_specs=[ANY],
+        in_specs=vmem(1),
         out_specs=ANY,
         scratch_shapes=[
-            pltpu.VMEM((CHUNKS, rows, 512), bf16),
-            pltpu.VMEM((CHUNKS, 8, 4, rows // 8, 128), bf16),
-            pltpu.SemaphoreType.DMA((CHUNKS,)),
+            pltpu.VMEM((CHUNKS, 8, 4, 64 // CHUNKS, 128), bf16),
             pltpu.SemaphoreType.DMA((CHUNKS,)),
         ],
+        compiler_params=pltpu.CompilerParams(vmem_limit_bytes=VMEM_GRANT),
     )(x)
 
 

time: 94.9 us -> 94.6 us (level)
  Pallas kernels: 13 us -> 11.7 us
  local copies, waits for them, and re-layouts: 2.6 us -> 3.63 us
    pallas_call x1, Pallas kernels: 2.37 us -> 1.05 us  [split(): pl.pallas_call(split_kernel, out_shape=sds((8, 4, 64, 128), bf16), in_spe...]
    unnamed x20 -> x22, local copies, waits for them, and re-layouts: 1.72 us -> 2.75 us
where the time goes in v7:
time: 94.6 us; the launch traced here: 94.1 us
  blocking collectives  46 us (49%)
  starting transfers between devices  16.5 us (17%)
  waiting for transfers between devices  15.4 us (16%)
  Pallas kernels  11.7 us (12%)
  local copies, waits for them, and re-layouts  3.63 us (4%)
    all_to_all x3, blocking collectives, exchange(): return lax.all_to_all(x, axis, split_axis=0, concat_axis=0, tiled=True)  46 us
    all_to_all x2, starting transfers between devices, exchange(): return lax.all_to_all(x, axis, split_axis=0, concat_axis=0, tiled=True)  14.6 us
    all_to_all x2, waiting for transfers between devices, exchange(): return lax.all_to_all(x, axis, split_axis=0, concat_axis=0, tiled=True)  14.2 us
    pallas_call x8, Pallas kernels, call(): pl.pallas_call(kernel, out_shape=shapes, in_specs=ins, out_specs=vmem(len...  9.22 us
    unnamed x22, local copies, waits for them, and re-layouts  2.75 us
    ppermute x1, starting transfers between devices, local(): other = lax.ppermute(own, 'core', [(0, 1), (1, 0)])  1.91 us
  transfers between devices with their start and end apart: 3, of which 3 were waited for; matrix products, arithmetic and copies ran while one was open for 1% of the time, Pallas kernels for 8%

profile of v7, /device:TPU:2, one launch (start us, length us, event | category | flops | bytes accessed | tf_op | source)
XLA Modules:
  0.0 94.1 jit_solution(8120365595849793211)
XLA Ops:
  0.6 0.0 copy-start.1
  0.6 1.0 %copy-done.1 = bf16[1,64,8,512]{3,2,1,0:T(8,128)(2,1)S(1)} copy-done((bf16[1,64,8,512]{3,2,1,0:T(8,128)(2,1)S(1)}, bf16[1,64,8,512]{3,2,1,0:T(8,128)(2,1)}, u32[]{:S(2)}) %copy-start.1) | copy-done | bytes 524312
  1.7 0.0 copy-start.6
  1.7 0.0 copy-start.7
  1.7 0.0 copy-start.5
  1.7 1.0 %shard_map.112 = bf16[8,4,64,128]{3,2,1,0:T(8,128)(2,1)} custom-call(bf16[512,512]{1,0:T(8,128)(2,1)S(1)} %bitcast.21), custom_call_target="tpu_custom_call" | custom-call | tf_op jit(solution)/shard_map/pallas_call | solution.py:88
  2.7 0.0 copy-start.8
  2.7 9.3 %all-to-all-start = ((bf16[8,256,128]{2,1,0:T(8,128)(2,1)}), bf16[8,256,128]{2,1,0:T(8,128)(2,1)S(1)}, u32[]{:S(2)}, u32[]{:S(2)}) async-start(bf16[8,256,128]{2,1,0:T(8,128)(2,1)} %bitcast.1), calls=%async_computation | async-start | bytes 1048576 | tf_op jit(solution)/shard_map/all_to_all | solution.py:243
  12.0 0.0 copy-done.6
  12.0 0.1 copy.19
  12.2 0.0 copy-done.7
  12.2 0.1 copy.20
  12.3 0.0 copy-done.5
  12.3 0.0 copy-start
  12.3 1.4 %copy-done = bf16[3,512,512]{2,1,0:T(8,128)(2,1)S(1)} copy-done((bf16[3,512,512]{2,1,0:T(8,128)(2,1)S(1)}, bf16[3,512,512]{2,1,0:T(8,128)(2,1)}, u32[]{:S(2)}) %copy-start) | copy-done | bytes 1572888
  13.7 2.0 %shard_map.113 = (bf16[3,512,512]{2,1,0:T(8,128)(2,1)S(1)}, bf16[3,64,512]{2,1,0:T(8,128)(2,1)S(1)}) custom-call(s32[1]{0:T(128)} %bitcast.3.core_ref, bf16[3,512,512]{2,1,0:T(8,128)(2,1)S(1)} %copy-done, f32[512,3]{1,0:T(8,128)S(1)} %bitcast.18, bf16[3,64,512]{2,1,0:T(8,128)(2,1)S(1)} %copy-done.5, f32[64,3]{1,0:T(8,128)S(1)} %bitcast.22), custom_call_target="tpu_custom_call" | custom-call | tf_op jit(solution)/shard_map/pallas_call | solution.py:47
  15.7 0.0 copy-done.8
  15.7 0.2 convert_reduce_fusion
  15.9 5.0 %all-to-all-done.parts_ref = bf16[8,256,128]{2,1,0:T(8,128)(2,1)S(1)} async-done(((bf16[8,256,128]{2,1,0:T(8,128)(2,1)}), bf16[8,256,128]{2,1,0:T(8,128)(2,1)S(1)}, u32[]{:S(2)}, u32[]{:S(2)}) %all-to-all-start) | async-done | bytes 524320 | tf_op jit(solution)/shard_map/all_to_all | solution.py:243
  20.9 0.2 shard_map.114
  21.2 0.1 reshape.41
  21.2 25.3 %all_to_all.25 = bf16[64,2,768]{2,1,0:T(2,128)(2,1)S(1)} all-to-all(bf16[64,2,768]{2,1,0:T(2,128)(2,1)S(1)} %reshape.41), channel_id=1, replica_groups=mesh['fsdp'=64,'x'=4,'core'=2] {'fsdp'}, dimensions={0} | all-to-all | bytes 393216 | tf_op jit(solution)/shard_map/all_to_all | solution.py:243
  46.5 0.1 shard_map.115
  46.6 12.9 %all_to_all.26.own_ref = bf16[4,768,128]{2,1,0:T(8,128)(2,1)S(1)} all-to-all(bf16[4,768,128]{2,1,0:T(8,128)(2,1)S(1)} %shard_map.115), channel_id=1, replica_groups=mesh['fsdp'=64,'x'=4,'core'=2] {'x'}, dimensions={0} | all-to-all | bytes 1572864 | tf_op jit(solution)/shard_map/all_to_all | solution.py:243
  59.5 1.9 %collective-permute-start = (bf16[4,768,128]{2,1,0:T(8,128)(2,1)S(1)}, bf16[4,768,128]{2,1,0:T(8,128)(2,1)S(1)}, u32[]{:S(2)}, u32[]{:S(2)}) collective-permute-start(bf16[4,768,128]{2,1,0:T(8,128)(2,1)S(1)} %all_to_all.26.own_ref), channel_id=1, source_target_pairs={{0,1},{1,0},{2,3},{3,2},{4,5},{5,4},{6,7},{7,6},{8,9},{9,8},{10,11... | collective-permute-start | bytes 2359304 | tf_op jit(solution)/shard_map/ppermute | solution.py:278
  61.5 1.1 %shard_map.116 = (bf16[3,256,512]{2,1,0:T(8,128)(2,1)S(1)}, f32[3,256,128]{2,1,0:T(8,128)S(1)}, f32[8,128]{1,0:T(8,128)S(1)}) custom-call(bf16[4,768,128]{2,1,0:T(8,128)(2,1)S(1)} %all_to_all.26.own_ref, bf16[3,64,512]{2,1,0:T(8,128)(2,1)S(1)} %get-tuple-element.13.rf_ref, bf16[3,512,512]{2,1,0:T(8,128)(2,1)S(1)} %get-tuple-element.12.after_ref.left_ref), custom_call_target="tpu_custom_call" | custom-call | tf_op jit(solution)/shard_map/pallas_call | solution.py:47
  62.6 1.2 %collective-permute-done.other_ref = bf16[4,768,128]{2,1,0:T(8,128)(2,1)S(1)} collective-permute-done((bf16[4,768,128]{2,1,0:T(8,128)(2,1)S(1)}, bf16[4,768,128]{2,1,0:T(8,128)(2,1)S(1)}, u32[]{:S(2)}, u32[]{:S(2)}) %collective-permute-start) | collective-permute-done | bytes 786464 | tf_op jit(solution)/shard_map/ppermute | solution.py:278
  63.7 1.3 %shard_map.117 = (bf16[3,256,512]{2,1,0:T(8,128)(2,1)S(1)}, f32[64,1536]{1,0:T(8,128)S(1)}, f32[8,128]{1,0:T(8,128)S(1)}, f32[8,128]{1,0:T(8,128)S(1)}) custom-call(bf16[4,768,128]{2,1,0:T(8,128)(2,1)S(1)} %collective-permute-done.other_ref, bf16[3,64,512]{2,1,0:T(8,128)(2,1)S(1)} %get-tuple-element.13.rf_ref, ...), custom_call_target="tpu_custom_call" | custom-call | tf_op jit(solution)/shard_map/pallas_call | solution.py:47
  65.0 0.0 copy-start.2
  65.0 7.8 %all_to_all.27 = f32[8,1,128]{2,1,0:T(1,128)S(1)} all-to-all(f32[8,1,128]{2,1,0:T(1,128)S(1)} %bitcast.24), channel_id=1, replica_groups=mesh['fsdp'=64,'x'=4,'core'=2] {'x','core'}, dimensions={0} | all-to-all | bytes 8192 | tf_op jit(solution)/shard_map/all_to_all | solution.py:243
  72.8 0.1 shard_map.118.after_ref
  72.9 0.0 copy-start.3
  72.9 0.7 reshape.45
  73.7 5.3 %all-to-all-start.4 = ((bf16[64,2,768]{2,1,0:T(2,128)(2,1)}), bf16[64,2,768]{2,1,0:T(2,128)(2,1)S(1)}, u32[]{:S(2)}, u32[]{:S(2)}) async-start(bf16[64,2,768]{2,1,0:T(2,128)(2,1)} %reshape.45), calls=%async_computation.4 | async-start | bytes 393216 | tf_op jit(solution)/shard_map/all_to_all | solution.py:243
  79.0 0.1 copy.22.slot_ref
  79.1 0.0 copy-done.2
  79.1 1.8 %shard_map.121 = f32[3,64,512]{2,1,0:T(8,128)} custom-call(s32[1]{0:T(128)} %bitcast.10.replica_ref, bf16[3,256,512]{2,1,0:T(8,128)(2,1)S(1)} %get-tuple-element.19.own_ref, bf16[3,256,512]{2,1,0:T(8,128)(2,1)S(1)} %get-tuple-element.20.other_ref, f32[3,64,512]{2,1,0:T(8,128)S(1)} %copy-done.2), custom_call_target="tpu_custom_call" | custom-call | tf_op jit(solution)/shard_map/pallas_call | solution.py:47
  80.9 0.0 copy-done.3
  80.9 0.0 copy-start.4
  80.9 2.6 %shard_map.120 = f32[3,64,512]{2,1,0:T(8,128)} custom-call(s32[1]{0:T(128)} %bitcast.10.replica_ref, s32[1]{0:T(128)} %bitcast.3.core_ref, bf16[3,256,512]{2,1,0:T(8,128)(2,1)S(1)} %get-tuple-element.19.own_ref, bf16[3,256,512]{2,1,0:T(8,128)(2,1)S(1)} %get-tuple-element.20.other_ref, f32[3,64,512]{2,1,0:T(8,128)S(1)} %copy-done.3, ...), custom_call_target="tpu_custom_call" | custom-call | tf_op jit(solution)/shard_map/pallas_call | solution.py:47
  83.5 9.2 %all-to-all-done.4 = bf16[64,2,768]{2,1,0:T(2,128)(2,1)S(1)} async-done(((bf16[64,2,768]{2,1,0:T(2,128)(2,1)}), bf16[64,2,768]{2,1,0:T(2,128)(2,1)S(1)}, u32[]{:S(2)}, u32[]{:S(2)}) %all-to-all-start.4) | async-done | bytes 196640 | tf_op jit(solution)/shard_map/all_to_all | solution.py:243
  92.7 0.0 copy-done.4
  92.7 1.4 %shard_map.119 = f32[64,8,64]{2,1,0:T(8,128)} custom-call(bf16[64,1536]{1,0:T(8,128)(2,1)S(1)} %bitcast.19, s32[64,1]{1,0:T(8,128)S(1)} %copy.22.slot_ref, f32[64,8,64]{2,1,0:T(8,128)S(1)} %copy-done.4), custom_call_target="tpu_custom_call" | custom-call | tf_op jit(solution)/shard_map/pallas_call | solution.py:310
  (3 shorter events, 0.1 us)
Async XLA Ops:
  0.6 1.0 %copy-start.1 = (bf16[1,64,8,512]{3,2,1,0:T(8,128)(2,1)S(1)}, bf16[1,64,8,512]{3,2,1,0:T(8,128)(2,1)}, u32[]{:S(2)}) copy-start(bf16[1,64,8,512]{3,2,1,0:T(8,128)(2,1)} %param.9) | copy-start | bytes 1572868
  1.7 10.4 %copy-start.6 = (f32[3,512]{1,0:T(4,128)S(1)}, f32[3,512]{1,0:T(4,128)}, u32[]{:S(2)}) copy-start(f32[3,512]{1,0:T(4,128)} %param.15) | copy-start | bytes 18436
  1.7 10.5 %copy-start.7 = (f32[3,64]{1,0:T(4,128)S(1)}, f32[3,64]{1,0:T(4,128)}, u32[]{:S(2)}) copy-start(f32[3,64]{1,0:T(4,128)} %param.16) | copy-start | bytes 2308
  1.7 10.6 %copy-start.5 = (bf16[3,64,512]{2,1,0:T(8,128)(2,1)S(1)}, bf16[3,64,512]{2,1,0:T(8,128)(2,1)}, u32[]{:S(2)}) copy-start(bf16[3,64,512]{2,1,0:T(8,128)(2,1)} %rc_ref.1) | copy-start | bytes 589828
  2.7 13.0 %copy-start.8 = (s32[64]{0:T(128)S(1)}, s32[64]{0:T(128)}, u32[]{:S(2)}) copy-start(s32[64]{0:T(128)} %param.17) | copy-start | bytes 772
  2.7 18.2 %all-to-all-start = ((bf16[8,256,128]{2,1,0:T(8,128)(2,1)}), bf16[8,256,128]{2,1,0:T(8,128)(2,1)S(1)}, u32[]{:S(2)}, u32[]{:S(2)}) async-start(bf16[8,256,128]{2,1,0:T(8,128)(2,1)} %bitcast.1), calls=%async_computation | async-start | bytes 1048576 | tf_op jit(solution)/shard_map/all_to_all | solution.py:243
  12.3 1.4 %copy-start = (bf16[3,512,512]{2,1,0:T(8,128)(2,1)S(1)}, bf16[3,512,512]{2,1,0:T(8,128)(2,1)}, u32[]{:S(2)}) copy-start(bf16[3,512,512]{2,1,0:T(8,128)(2,1)} %lc_ref.1) | copy-start | bytes 4718596
  59.5 4.2 %collective-permute-start = (bf16[4,768,128]{2,1,0:T(8,128)(2,1)S(1)}, bf16[4,768,128]{2,1,0:T(8,128)(2,1)S(1)}, u32[]{:S(2)}, u32[]{:S(2)}) collective-permute-start(bf16[4,768,128]{2,1,0:T(8,128)(2,1)S(1)} %all_to_all.26.own_ref), channel_id=1, source_target_pairs={{0,1},{1,0},{2,3},{3,2},{4,5},{5,4},{6,7},{7,6},{8,9},{9,8},{10,11... | collective-permute-start | bytes 2359304 | tf_op jit(solution)/shard_map/ppermute | solution.py:278
  65.0 14.1 %copy-start.2 = (f32[3,64,512]{2,1,0:T(8,128)S(1)}, f32[3,64,512]{2,1,0:T(8,128)}, u32[]{:S(2)}) copy-start(f32[3,64,512]{2,1,0:T(8,128)} %stat_ref.3) | copy-start | bytes 1179652
  72.9 8.0 %copy-start.3 = (f32[3,64,512]{2,1,0:T(8,128)S(1)}, f32[3,64,512]{2,1,0:T(8,128)}, u32[]{:S(2)}) copy-start(f32[3,64,512]{2,1,0:T(8,128)} %stat_ref.2) | copy-start | bytes 1179652
  73.7 19.0 %all-to-all-start.4 = ((bf16[64,2,768]{2,1,0:T(2,128)(2,1)}), bf16[64,2,768]{2,1,0:T(2,128)(2,1)S(1)}, u32[]{:S(2)}, u32[]{:S(2)}) async-start(bf16[64,2,768]{2,1,0:T(2,128)(2,1)} %reshape.45), calls=%async_computation.4 | async-start | bytes 393216 | tf_op jit(solution)/shard_map/all_to_all | solution.py:243
  80.9 11.8 %copy-start.4 = (f32[64,8,64]{2,1,0:T(8,128)S(1)}, f32[64,8,64]{2,1,0:T(8,128)}, u32[]{:S(2)}) copy-start(f32[64,8,64]{2,1,0:T(8,128)} %w_ref.1) | copy-start | bytes 393220

commit v8 on v7

--- a/solution.py
+++ b/solution.py
@@ -120,13 +120,12 @@
         rf_ref[k] = (rc_ref[k].astype(f32) * rs_ref[:, k : k + 1]).astype(bf16)
 
 
-def spread_kernel(piece_ref, out_ref):
+def tile_kernel(piece_ref, out_ref):
     for q in range(4):
         for kr in range(12):
+            at = 192 * q + 16 * kr
             tile = piece_ref[16 * q : 16 * q + 16, LANES * kr : LANES * kr + LANES]
-            for x in range(4):
-                at = 192 * q + 16 * kr
-                out_ref[x, at : at + 16] = tile
+            out_ref[at : at + 16] = tile
 
 
 def half_products(at, src_ref, rf_ref, left_ref, g_ref):
@@ -274,7 +273,8 @@
         (parts, slot_of.reshape(1, 64), left),
     )
     arrived = exchange(routed.reshape(64, 2, 768), "fsdp").reshape(64, 1536)
-    own = exchange(call(spread_kernel, vmem(1), sds((4, 768, 128), bf16), (arrived,)), "x")
+    piece = call(tile_kernel, vmem(1), sds((768, 128), bf16), (arrived,))
+    own = lax.all_gather(piece, "x", axis=0, tiled=True).reshape(4, 768, 128)
     other = lax.ppermute(own, "core", [(0, 1), (1, 0)])
     half_grad = sds((3, 256, 512), bf16)
     small = sds((8, 128), f32)

time: 94.6 us -> 95.3 us (level)
  the two profiles are of different devices: /device:TPU:2 before, /device:TPU:8 now
where the time goes in v8:
time: 95.3 us; the launch traced here: 94.9 us
  blocking collectives  50.4 us (53%)
  waiting for transfers between devices  16.3 us (17%)
  starting transfers between devices  11.9 us (12%)
  Pallas kernels  11.6 us (12%)
  local copies, waits for them, and re-layouts  3.63 us (4%)
    all_to_all x2, blocking collectives, exchange(): return lax.all_to_all(x, axis, split_axis=0, concat_axis=0, tiled=True)  37.1 us
    all_to_all x2, waiting for transfers between devices, exchange(): return lax.all_to_all(x, axis, split_axis=0, concat_axis=0, tiled=True)  15.2 us
    all_gather x1, blocking collectives, local(): own = lax.all_gather(piece, 'x', axis=0, tiled=True).reshape(4, 768, 128)  13.3 us
    all_to_all x2, starting transfers between devices, exchange(): return lax.all_to_all(x, axis, split_axis=0, concat_axis=0, tiled=True)  10 us
    pallas_call x8, Pallas kernels, call(): pl.pallas_call(kernel, out_shape=shapes, in_specs=ins, out_specs=vmem(len...  9.15 us
    unnamed x22, local copies, waits for them, and re-layouts  2.76 us
    ppermute x1, starting transfers between devices, local(): other = lax.ppermute(own, 'core', [(0, 1), (1, 0)])  1.91 us
  transfers between devices with their start and end apart: 3, of which 3 were waited for; matrix products, arithmetic and copies ran while one was open for 1% of the time, Pallas kernels for 8%

profile of v8, /device:TPU:8, one launch (start us, length us, event | category | flops | bytes accessed | tf_op | source)
XLA Modules:
  0.0 94.9 jit_solution(17278468050426378222)
XLA Ops:
  0.6 0.0 copy-start.1
  0.6 1.0 %copy-done.1 = bf16[1,64,8,512]{3,2,1,0:T(8,128)(2,1)S(1)} copy-done((bf16[1,64,8,512]{3,2,1,0:T(8,128)(2,1)S(1)}, bf16[1,64,8,512]{3,2,1,0:T(8,128)(2,1)}, u32[]{:S(2)}) %copy-start.1) | copy-done | bytes 524312
  1.7 0.0 copy-start.6
  1.7 0.0 copy-start.7
  1.7 0.0 copy-start.5
  1.7 1.0 %shard_map.112 = bf16[8,4,64,128]{3,2,1,0:T(8,128)(2,1)} custom-call(bf16[512,512]{1,0:T(8,128)(2,1)S(1)} %bitcast.24), custom_call_target="tpu_custom_call" | custom-call | tf_op jit(solution)/shard_map/pallas_call | solution.py:88
  2.7 0.0 copy-start.8
  2.7 4.3 %all-to-all-start = ((bf16[8,256,128]{2,1,0:T(8,128)(2,1)}), bf16[8,256,128]{2,1,0:T(8,128)(2,1)S(1)}, u32[]{:S(2)}, u32[]{:S(2)}) async-start(bf16[8,256,128]{2,1,0:T(8,128)(2,1)} %bitcast.1), calls=%async_computation | async-start | bytes 1048576 | tf_op jit(solution)/shard_map/all_to_all | solution.py:242
  7.1 0.0 copy-done.6
  7.1 0.1 copy.19
  7.2 0.0 copy-done.7
  7.2 0.1 copy.20
  7.3 0.0 copy-done.5
  7.3 0.0 copy-start
  7.3 1.4 %copy-done = bf16[3,512,512]{2,1,0:T(8,128)(2,1)S(1)} copy-done((bf16[3,512,512]{2,1,0:T(8,128)(2,1)S(1)}, bf16[3,512,512]{2,1,0:T(8,128)(2,1)}, u32[]{:S(2)}) %copy-start) | copy-done | bytes 1572888
  8.7 2.0 %shard_map.113 = (bf16[3,512,512]{2,1,0:T(8,128)(2,1)S(1)}, bf16[3,64,512]{2,1,0:T(8,128)(2,1)S(1)}) custom-call(s32[1]{0:T(128)} %bitcast.3.core_ref, bf16[3,512,512]{2,1,0:T(8,128)(2,1)S(1)} %copy-done, f32[512,3]{1,0:T(8,128)S(1)} %bitcast.21, bf16[3,64,512]{2,1,0:T(8,128)(2,1)S(1)} %copy-done.5, f32[64,3]{1,0:T(8,128)S(1)} %bitcast.25), custom_call_target="tpu_custom_call" | custom-call | tf_op jit(solution)/shard_map/pallas_call | solution.py:47
  10.7 0.0 copy-done.8
  10.7 0.2 convert_reduce_fusion
  10.9 6.5 %all-to-all-done.parts_ref = bf16[8,256,128]{2,1,0:T(8,128)(2,1)S(1)} async-done(((bf16[8,256,128]{2,1,0:T(8,128)(2,1)}), bf16[8,256,128]{2,1,0:T(8,128)(2,1)S(1)}, u32[]{:S(2)}, u32[]{:S(2)}) %all-to-all-start) | async-done | bytes 524320 | tf_op jit(solution)/shard_map/all_to_all | solution.py:242
  17.4 0.2 shard_map.114
  17.6 0.1 reshape.44
  17.7 28.7 %all_to_all.20 = bf16[64,2,768]{2,1,0:T(2,128)(2,1)S(1)} all-to-all(bf16[64,2,768]{2,1,0:T(2,128)(2,1)S(1)} %reshape.44), channel_id=1, replica_groups=mesh['fsdp'=64,'x'=4,'core'=2] {'fsdp'}, dimensions={0} | all-to-all | bytes 393216 | tf_op jit(solution)/shard_map/all_to_all | solution.py:242
  46.4 13.3 %all_gather.3 = bf16[3072,128]{1,0:T(8,128)(2,1)S(1)} all-gather(bf16[768,128]{1,0:T(8,128)(2,1)S(1)} %shard_map.115), channel_id=1, replica_groups=mesh['fsdp'=64,'x'=4,'core'=2] {'x'}, dimensions={0}, use_global_device_ids=true | all-gather | bytes 983040 | tf_op jit(solution)/shard_map/all_gather | solution.py:277
  59.7 1.9 %collective-permute-start = (bf16[4,768,128]{2,1,0:T(8,128)(2,1)S(1)}, bf16[4,768,128]{2,1,0:T(8,128)(2,1)S(1)}, u32[]{:S(2)}, u32[]{:S(2)}) collective-permute-start(bf16[4,768,128]{2,1,0:T(8,128)(2,1)S(1)} %bitcast.19), channel_id=1, source_target_pairs={{0,1},{1,0},{2,3},{3,2},{4,5},{5,4},{6,7},{7,6},{8,9},{9,8},{10,11... | collective-permute-start | bytes 2359304 | tf_op jit(solution)/shard_map/ppermute | solution.py:278
  61.6 1.1 %shard_map.116 = (bf16[3,256,512]{2,1,0:T(8,128)(2,1)S(1)}, f32[3,256,128]{2,1,0:T(8,128)S(1)}, f32[8,128]{1,0:T(8,128)S(1)}) custom-call(bf16[4,768,128]{2,1,0:T(8,128)(2,1)S(1)} %bitcast.20, bf16[3,64,512]{2,1,0:T(8,128)(2,1)S(1)} %get-tuple-element.13.rf_ref, bf16[3,512,512]{2,1,0:T(8,128)(2,1)S(1)} %get-tuple-element.12.after_ref.left_ref), custom_call_target="tpu_custom_call" | custom-call | tf_op jit(solution)/shard_map/pallas_call | solution.py:47
  62.7 1.2 %collective-permute-done.other_ref = bf16[4,768,128]{2,1,0:T(8,128)(2,1)S(1)} collective-permute-done((bf16[4,768,128]{2,1,0:T(8,128)(2,1)S(1)}, bf16[4,768,128]{2,1,0:T(8,128)(2,1)S(1)}, u32[]{:S(2)}, u32[]{:S(2)}) %collective-permute-start) | collective-permute-done | bytes 786464 | tf_op jit(solution)/shard_map/ppermute | solution.py:278
  63.9 1.3 %shard_map.117 = (bf16[3,256,512]{2,1,0:T(8,128)(2,1)S(1)}, f32[64,1536]{1,0:T(8,128)S(1)}, f32[8,128]{1,0:T(8,128)S(1)}, f32[8,128]{1,0:T(8,128)S(1)}) custom-call(bf16[4,768,128]{2,1,0:T(8,128)(2,1)S(1)} %collective-permute-done.other_ref, bf16[3,64,512]{2,1,0:T(8,128)(2,1)S(1)} %get-tuple-element.13.rf_ref, ...), custom_call_target="tpu_custom_call" | custom-call | tf_op jit(solution)/shard_map/pallas_call | solution.py:47
  65.2 0.0 copy-start.2
  65.2 8.4 %all_to_all.21 = f32[8,1,128]{2,1,0:T(1,128)S(1)} all-to-all(f32[8,1,128]{2,1,0:T(1,128)S(1)} %bitcast.27), channel_id=1, replica_groups=mesh['fsdp'=64,'x'=4,'core'=2] {'x','core'}, dimensions={0} | all-to-all | bytes 8192 | tf_op jit(solution)/shard_map/all_to_all | solution.py:242
  73.6 0.1 shard_map.118.after_ref
  73.7 0.0 copy-start.3
  73.8 0.7 reshape.49
  74.5 5.7 %all-to-all-start.3 = ((bf16[64,2,768]{2,1,0:T(2,128)(2,1)}), bf16[64,2,768]{2,1,0:T(2,128)(2,1)S(1)}, u32[]{:S(2)}, u32[]{:S(2)}) async-start(bf16[64,2,768]{2,1,0:T(2,128)(2,1)} %reshape.49), calls=%async_computation.3 | async-start | bytes 393216 | tf_op jit(solution)/shard_map/all_to_all | solution.py:242
  80.2 0.1 copy.22.slot_ref
  80.3 0.0 copy-done.2
  80.3 1.8 %shard_map.121 = f32[3,64,512]{2,1,0:T(8,128)} custom-call(s32[1]{0:T(128)} %bitcast.11.replica_ref, bf16[3,256,512]{2,1,0:T(8,128)(2,1)S(1)} %get-tuple-element.19.own_ref, bf16[3,256,512]{2,1,0:T(8,128)(2,1)S(1)} %get-tuple-element.20.other_ref, f32[3,64,512]{2,1,0:T(8,128)S(1)} %copy-done.2), custom_call_target="tpu_custom_call" | custom-call | tf_op jit(solution)/shard_map/pallas_call | solution.py:47
  82.2 0.0 copy-done.3
  82.2 0.0 copy-start.4
  82.2 2.6 %shard_map.120 = f32[3,64,512]{2,1,0:T(8,128)} custom-call(s32[1]{0:T(128)} %bitcast.11.replica_ref, s32[1]{0:T(128)} %bitcast.3.core_ref, bf16[3,256,512]{2,1,0:T(8,128)(2,1)S(1)} %get-tuple-element.19.own_ref, bf16[3,256,512]{2,1,0:T(8,128)(2,1)S(1)} %get-tuple-element.20.other_ref, f32[3,64,512]{2,1,0:T(8,128)S(1)} %copy-done.3, ...), custom_call_target="tpu_custom_call" | custom-call | tf_op jit(solution)/shard_map/pallas_call | solution.py:47
  84.7 8.7 %all-to-all-done.3 = bf16[64,2,768]{2,1,0:T(2,128)(2,1)S(1)} async-done(((bf16[64,2,768]{2,1,0:T(2,128)(2,1)}), bf16[64,2,768]{2,1,0:T(2,128)(2,1)S(1)}, u32[]{:S(2)}, u32[]{:S(2)}) %all-to-all-start.3) | async-done | bytes 196640 | tf_op jit(solution)/shard_map/all_to_all | solution.py:242
  93.5 0.0 copy-done.4
  93.5 1.4 %shard_map.119 = f32[64,8,64]{2,1,0:T(8,128)} custom-call(bf16[64,1536]{1,0:T(8,128)(2,1)S(1)} %bitcast.23, s32[64,1]{1,0:T(8,128)S(1)} %copy.22.slot_ref, f32[64,8,64]{2,1,0:T(8,128)S(1)} %copy-done.4), custom_call_target="tpu_custom_call" | custom-call | tf_op jit(solution)/shard_map/pallas_call | solution.py:310
  (4 shorter events, 0.1 us)
Async XLA Ops:
  0.6 1.0 %copy-start.1 = (bf16[1,64,8,512]{3,2,1,0:T(8,128)(2,1)S(1)}, bf16[1,64,8,512]{3,2,1,0:T(8,128)(2,1)}, u32[]{:S(2)}) copy-start(bf16[1,64,8,512]{3,2,1,0:T(8,128)(2,1)} %param.9) | copy-start | bytes 1572868
  1.7 5.4 %copy-start.6 = (f32[3,512]{1,0:T(4,128)S(1)}, f32[3,512]{1,0:T(4,128)}, u32[]{:S(2)}) copy-start(f32[3,512]{1,0:T(4,128)} %param.15) | copy-start | bytes 18436
  1.7 5.5 %copy-start.7 = (f32[3,64]{1,0:T(4,128)S(1)}, f32[3,64]{1,0:T(4,128)}, u32[]{:S(2)}) copy-start(f32[3,64]{1,0:T(4,128)} %param.16) | copy-start | bytes 2308
  1.7 5.6 %copy-start.5 = (bf16[3,64,512]{2,1,0:T(8,128)(2,1)S(1)}, bf16[3,64,512]{2,1,0:T(8,128)(2,1)}, u32[]{:S(2)}) copy-start(bf16[3,64,512]{2,1,0:T(8,128)(2,1)} %rc_ref.1) | copy-start | bytes 589828
  2.7 8.0 %copy-start.8 = (s32[64]{0:T(128)S(1)}, s32[64]{0:T(128)}, u32[]{:S(2)}) copy-start(s32[64]{0:T(128)} %param.17) | copy-start | bytes 772
  2.7 14.6 %all-to-all-start = ((bf16[8,256,128]{2,1,0:T(8,128)(2,1)}), bf16[8,256,128]{2,1,0:T(8,128)(2,1)S(1)}, u32[]{:S(2)}, u32[]{:S(2)}) async-start(bf16[8,256,128]{2,1,0:T(8,128)(2,1)} %bitcast.1), calls=%async_computation | async-start | bytes 1048576 | tf_op jit(solution)/shard_map/all_to_all | solution.py:242
  7.3 1.4 %copy-start = (bf16[3,512,512]{2,1,0:T(8,128)(2,1)S(1)}, bf16[3,512,512]{2,1,0:T(8,128)(2,1)}, u32[]{:S(2)}) copy-start(bf16[3,512,512]{2,1,0:T(8,128)(2,1)} %lc_ref.1) | copy-start | bytes 4718596
  59.7 4.2 %collective-permute-start = (bf16[4,768,128]{2,1,0:T(8,128)(2,1)S(1)}, bf16[4,768,128]{2,1,0:T(8,128)(2,1)S(1)}, u32[]{:S(2)}, u32[]{:S(2)}) collective-permute-start(bf16[4,768,128]{2,1,0:T(8,128)(2,1)S(1)} %bitcast.19), channel_id=1, source_target_pairs={{0,1},{1,0},{2,3},{3,2},{4,5},{5,4},{6,7},{7,6},{8,9},{9,8},{10,11... | collective-permute-start | bytes 2359304 | tf_op jit(solution)/shard_map/ppermute | solution.py:278
  65.2 15.2 %copy-start.2 = (f32[3,64,512]{2,1,0:T(8,128)S(1)}, f32[3,64,512]{2,1,0:T(8,128)}, u32[]{:S(2)}) copy-start(f32[3,64,512]{2,1,0:T(8,128)} %stat_ref.3) | copy-start | bytes 1179652
  73.7 8.4 %copy-start.3 = (f32[3,64,512]{2,1,0:T(8,128)S(1)}, f32[3,64,512]{2,1,0:T(8,128)}, u32[]{:S(2)}) copy-start(f32[3,64,512]{2,1,0:T(8,128)} %stat_ref.2) | copy-start | bytes 1179652
  74.5 18.9 %all-to-all-start.3 = ((bf16[64,2,768]{2,1,0:T(2,128)(2,1)}), bf16[64,2,768]{2,1,0:T(2,128)(2,1)S(1)}, u32[]{:S(2)}, u32[]{:S(2)}) async-start(bf16[64,2,768]{2,1,0:T(2,128)(2,1)} %reshape.49), calls=%async_computation.3 | async-start | bytes 393216 | tf_op jit(solution)/shard_map/all_to_all | solution.py:242
  82.2 11.3 %copy-start.4 = (f32[64,8,64]{2,1,0:T(8,128)S(1)}, f32[64,8,64]{2,1,0:T(8,128)}, u32[]{:S(2)}) copy-start(f32[64,8,64]{2,1,0:T(8,128)} %w_ref.1) | copy-start | bytes 393220
